TPU v7x, 32 devices: a whole 2x2x4 slice. The times are simulated.
32 devices in a mesh: gx: 2 (over y), gy: 4 (over z), gz: 4 (over x, core).
Axes of the slice: x: 2, y: 2, z: 4, core: 2. Of those that a mesh axis runs over, the one named last changes fastest.
Arguments:
- velocity: float32 [3, 32, 256, 512], P(None, 'gy', 'gx', 'gz'), may hold values from -6 to 6
- stress: float32 [6, 32, 256, 512], P(None, 'gy', 'gx', 'gz'), may hold values from -6 to 6
- buoyancy: float32 [32, 256, 512], P('gy', 'gx', 'gz'), may hold values from 0.5 to 2
- stiff_xx: float32 [32, 256, 512], P('gy', 'gx', 'gz'), may hold values from 2 to 4
- stiff_xz: float32 [32, 256, 512], P('gy', 'gx', 'gz'), may hold values from 0.5 to 1
- stiff_zz: float32 [32, 256, 512], P('gy', 'gx', 'gz'), may hold values from 1.5 to 3
- shear_vert: float32 [32, 256, 512], P('gy', 'gx', 'gz'), may hold values from 0.5 to 1
- shear_horiz: float32 [32, 256, 512], P('gy', 'gx', 'gz'), may hold values from 0.6 to 1.2
- prestress: float32 [2, 32, 512], P(None, 'gy', 'gz'), may hold values from -24 to 24
- fault_mask: int32 [32, 512], P('gy', 'gz'), may hold values 0 or 1
- region_ids: int32 [32, 512], P('gy', 'gz'), may hold values from 0 to 7
- inverse_rate: float32 [32, 512], P('gy', 'gz'), may hold values from 100 to 10000
- slip_prev: float32 [32, 512], P('gy', 'gz'), may hold values from 0.01 to 2
- region_a: float32 [8], replicated, may hold values from 0.01 to 0.04
- region_normal: float32 [8], replicated, may hold values from 20 to 60
Outputs:
- new_velocity: float32 [3, 32, 256, 512], P(None, 'gy', 'gx', 'gz')
- new_stress: float32 [6, 32, 256, 512], P(None, 'gy', 'gx', 'gz')
- slip_rate: float32 [32, 512], P('gy', 'gz')
All inputs are finite; a program needn't handle non-finite values. No bound on the sum of `fault_mask` on one device may be relied on, other than what follows from the above.
Results may differ from a plain program's by a relative error of at most 0.0003.
Values sent between devices are 32-bit elements; how exact they have to be, the bound alone decides.
No kernel may reach another device: no remote copies, remote signals or barrier semaphores. Data moves between devices by JAX's collectives and lax.ppermute only.
A program may use at most 128 MiB of HBM per device.

v0:
```python
import jax
import jax.numpy as jnp
from jax import lax
from jax.sharding import PartitionSpec as P

STEPS = 3
NEWTON = 3


step_dt = 0.2


def from_behind(shard, axis, by):
    devices = lax.axis_size(axis)
    pairs = [(i, i + by) for i in range(devices) if 0 <= i + by < devices]
    return lax.ppermute(shard, axis, pairs)


def swapped(shard, axis, apart):
    return lax.ppermute(shard, axis, [(i, i ^ 1 << apart) for i in range(lax.axis_size(axis))])


def inverse_sinh(values):
    size_abs = jnp.abs(values)
    return jnp.sign(values) * jnp.log(size_abs + jnp.sqrt(size_abs * size_abs + 1.0))


def local_lower(values):
    beneath = jnp.concatenate([jnp.zeros_like(values[:, :1]), values[:, :-1]], axis=1)
    return values - beneath


def local_upper(values):
    overhead = jnp.concatenate([values[:, 1:], jnp.zeros_like(values[:, :1])], axis=1)
    return overhead - values


def lower_strike(values, beneath):
    return values - jnp.concatenate([beneath, values[:-1]], axis=0)


def upper_strike(values, overhead):
    return jnp.concatenate([values[1:], overhead], axis=0) - values


def lower_dip(values, beneath):
    return values - jnp.concatenate([beneath, values[:, :, :-1]], axis=2)


def upper_dip(values, overhead):
    return jnp.concatenate([values[:, :, 1:], overhead], axis=2) - values


def friction(
    minus_side,
    plus_side,
    minus_buoy,
    plus_buoy,
    prestress,
    fault_mask,
    region_ids,
    inverse_rate,
    slip_prev,
    region_a,
    region_normal,
):
    impedance = 1.0 / (step_dt * (minus_buoy + plus_buoy))
    jump_vec = plus_side - minus_side
    normal_part = impedance * jump_vec[0]
    locked_y = prestress[0] + impedance * jump_vec[1]
    locked_z = prestress[1] + impedance * jump_vec[2]
    magnitude = jnp.sqrt(locked_y * locked_y + locked_z * locked_z + 1.0)
    labels = jnp.arange(region_a.shape[0], dtype=jnp.int32)
    picked = (region_ids[None] == labels[:, None, None]).astype(jnp.float32)
    strength = jnp.sum(picked * region_a[:, None, None], axis=0) * jnp.sum(
        picked * region_normal[:, None, None], axis=0
    )
    velocity_slip = slip_prev
    for turn in range(NEWTON):
        scaled = inverse_rate * velocity_slip
        residual = magnitude - impedance * velocity_slip - strength * inverse_sinh(scaled)
        tangent = -impedance - strength * inverse_rate / jnp.sqrt(1.0 + scaled * scaled)
        velocity_slip = velocity_slip - residual / tangent
    velocity_slip = velocity_slip * fault_mask.astype(jnp.float32)
    retained = 1.0 - impedance * velocity_slip / magnitude
    traction = jnp.stack(
        [normal_part, retained * locked_y - prestress[0], retained * locked_z - prestress[1]]
    )
    return (traction, velocity_slip)


def solve_pair(
    is_minus,
    own_plane,
    other_plane,
    own_buoy,
    other_buoy,
    prestress,
    fault_mask,
    region_ids,
    inverse_rate,
    slip_prev,
    region_a,
    region_normal,
):
    minus_side = jnp.where(is_minus, own_plane, other_plane)
    plus_side = jnp.where(is_minus, other_plane, own_plane)
    minus_buoy = jnp.where(is_minus, own_buoy, other_buoy)
    plus_buoy = jnp.where(is_minus, other_buoy, own_buoy)
    return friction(
        minus_side,
        plus_side,
        minus_buoy,
        plus_buoy,
        prestress,
        fault_mask,
        region_ids,
        inverse_rate,
        slip_prev,
        region_a,
        region_normal,
    )


def one_step(
    velocity,
    stress,
    buoyancy,
    stiff_xx,
    stiff_xz,
    stiff_zz,
    shear_vert,
    shear_horiz,
    prestress,
    fault_mask,
    region_ids,
    inverse_rate,
    slip_prev,
    region_a,
    region_normal,
):
    depth = velocity.shape[2]
    side = lax.axis_index("gx")
    is_minus = side == 0
    stress_xx, stress_yy, stress_zz, stress_yz, stress_xz, stress_xy = stress
    strike_rims = from_behind(jnp.stack([stress_xy[-1:], stress_yy[-1:], stress_yz[-1:]]), "gy", 1)
    dip_rims = from_behind(
        jnp.stack([stress_xz[:, :, -1:], stress_yz[:, :, -1:], stress_zz[:, :, -1:]]), "gz", 1
    )
    trial_x = velocity[0] + step_dt * buoyancy * (
        local_lower(stress_xx)
        + lower_strike(stress_xy, strike_rims[0])
        + lower_dip(stress_xz, dip_rims[0])
    )
    trial_y = velocity[1] + step_dt * buoyancy * (
        local_lower(stress_xy)
        + lower_strike(stress_yy, strike_rims[1])
        + lower_dip(stress_yz, dip_rims[1])
    )
    trial_z = velocity[2] + step_dt * buoyancy * (
        local_lower(stress_xz)
        + lower_strike(stress_yz, strike_rims[2])
        + lower_dip(stress_zz, dip_rims[2])
    )
    trial = jnp.stack([trial_x, trial_y, trial_z])
    own_plane = jnp.where(is_minus, trial[:, :, depth - 1, :], trial[:, :, 0, :])
    own_buoy = jnp.where(is_minus, buoyancy[:, depth - 1, :], buoyancy[:, 0, :])
    marker = (jnp.arange(depth, dtype=jnp.int32) == jnp.where(is_minus, depth - 1, 0)).astype(
        jnp.float32
    )
    other_plane, other_buoy = swapped((own_plane, own_buoy), "gx", 0)
    traction, slip_rate = solve_pair(
        is_minus,
        own_plane,
        other_plane,
        own_buoy,
        other_buoy,
        prestress,
        fault_mask,
        region_ids,
        inverse_rate,
        slip_prev,
        region_a,
        region_normal,
    )
    sign = jnp.where(is_minus, 1.0, -1.0)
    correction = sign * (step_dt * own_buoy * traction)
    spread = marker[None, None, :, None]
    moved = trial + spread * correction[:, :, None, :]
    strike_next = from_behind(moved[:, 0:1], "gy", -1)
    dip_next = from_behind(moved[:, :, :, 0:1], "gz", -1)
    moved_x, moved_y, moved_z = moved
    strain_xx = local_upper(moved_x)
    strain_yy = upper_strike(moved_y, strike_next[1])
    strain_zz = upper_dip(moved_z, dip_next[2])
    lame = stiff_xx - 2.0 * shear_horiz
    new_xx = stress_xx + step_dt * (stiff_xx * strain_xx + lame * strain_yy + stiff_xz * strain_zz)
    new_yy = stress_yy + step_dt * (lame * strain_xx + stiff_xx * strain_yy + stiff_xz * strain_zz)
    new_zz = stress_zz + step_dt * (stiff_xz * (strain_xx + strain_yy) + stiff_zz * strain_zz)
    new_yz = stress_yz + step_dt * shear_vert * (
        upper_dip(moved_y, dip_next[1]) + upper_strike(moved_z, strike_next[2])
    )
    new_xz = stress_xz + step_dt * shear_vert * (
        upper_dip(moved_x, dip_next[0]) + local_upper(moved_z)
    )
    new_xy = stress_xy + step_dt * shear_horiz * (
        upper_strike(moved_x, strike_next[0]) + local_upper(moved_y)
    )
    return (moved, jnp.stack([new_xx, new_yy, new_zz, new_yz, new_xz, new_xy]), slip_rate)


def local(
    velocity,
    stress,
    buoyancy,
    stiff_xx,
    stiff_xz,
    stiff_zz,
    shear_vert,
    shear_horiz,
    prestress,
    fault_mask,
    region_ids,
    inverse_rate,
    slip_prev,
    region_a,
    region_normal,
):
    slip_rate = slip_prev
    for count in range(STEPS):
        velocity, stress, slip_rate = one_step(
            velocity,
            stress,
            buoyancy,
            stiff_xx,
            stiff_xz,
            stiff_zz,
            shear_vert,
            shear_horiz,
            prestress,
            fault_mask,
            region_ids,
            inverse_rate,
            slip_rate,
            region_a,
            region_normal,
        )
    return (velocity, stress, slip_rate)


def solution(mesh):
    in_specs = (
        P(None, "gy", "gx", "gz"),
        P(None, "gy", "gx", "gz"),
        P("gy", "gx", "gz"),
        P("gy", "gx", "gz"),
        P("gy", "gx", "gz"),
        P("gy", "gx", "gz"),
        P("gy", "gx", "gz"),
        P("gy", "gx", "gz"),
        P(None, "gy", "gz"),
        P("gy", "gz"),
        P("gy", "gz"),
        P("gy", "gz"),
        P("gy", "gz"),
        P(),
        P(),
    )
    out_specs = (P(None, "gy", "gx", "gz"), P(None, "gy", "gx", "gz"), P("gy", "gz"))
    return jax.shard_map(local, mesh=mesh, in_specs=in_specs, out_specs=out_specs, check_vma=False)
```

profile of v0, /device:TPU:0, one launch (start us, length us, event | category | flops | bytes accessed | tf_op | source)
XLA Modules:
  0.0 172.1 jit_solution(15557459763601997681)
XLA Ops:
  0.6 3.4 %fusion.128 = (f32[1,8,128,128]{3,2,1,0:T(8,128)}, f32[8,128,128]{2,1,0:T(8,128)}, f32[1,8,128,128]{3,2,1,0:T(8,128)}, f32[1,8,128,128]{3,2,1,0:T(8,128)S(1)}, f...) fusion(f32[6,8,128,128]{3,2,1,0:T(8,128)} %param.16), kind=kLoop, calls=%fused_computation.290 | loop fusion | bytes 6815744 | tf_op jit(solution)/shard_map/unstack | solution.py:145
  4.7 2.4 %collective-permute-start.1 = (f32[3,8,128,1]{2,1,3,0:T(8,128)S(1)}, f32[3,8,128,1]{2,1,3,0:T(8,128)S(1)}, u32[]{:S(2)}, u32[]{:S(2)}) collective-permute-start(f32[3,8,128,1]{2,1,3,0:T(8,128)S(1)} %pad_maximum_fusion.7), channel_id=1, source_target_pairs={{0,1},{1,2},{2,3},{4,5},{5,6},{6,7},{8,9},{9,10},{10,11},{12,13},{... | collective-permute-start | bytes 36872 | tf_op jit(solution)/shard_map/ppermute | solution.py:16
  8.1 5.0 %collective-permute-start = (f32[3,1,128,128]{3,2,1,0:T(8,128)S(1)}, f32[3,1,128,128]{3,2,1,0:T(8,128)}, u32[]{:S(2)}, u32[]{:S(2)}) collective-permute-start(f32[3,1,128,128]{3,2,1,0:T(8,128)S(1)} %pad_maximum_fusion.4), channel_id=1, source_target_pairs={{0,4},{4,8},{8,12},{1,5},{5,9},{9,13},{2,6},{6,10},{10,14},{3,7},{... | collective-permute-start | bytes 589832 | tf_op jit(solution)/shard_map/ppermute | solution.py:16
  13.9 1.6 collective-permute-start.2
  15.5 2.5 %fusion.129 = (f32[1,7,128,128]{3,2,1,0:T(8,128)}, f32[1,7,128,128]{3,2,1,0:T(8,128)}, f32[1,7,128,128]{3,2,1,0:T(8,128)}) fusion(f32[6,8,128,128]{3,2,1,0:T(8,128)} %param.16), kind=kLoop, calls=%fused_computation.291 | loop fusion | bytes 2752512 | tf_op jit(solution)/shard_map/slice | solution.py:39
  17.9 2.7 %fusion.133 = (f32[1,8,128,128]{3,2,1,0:T(8,128)}, f32[1,8,128,128]{3,2,1,0:T(8,128)}, f32[1,8,128,128]{3,2,1,0:T(8,128)}) fusion(f32[3,8,128,128]{3,2,1,0:T(8,128)} %param.15), kind=kLoop, calls=%fused_computation.295 | loop fusion | bytes 3145728 | tf_op jit(solution)/shard_map/slice | solution.py:150
  21.1 1.5 copy.781
  24.4 1.2 copy.744
  25.7 1.4 copy.847
  27.1 2.2 %copy.848 = f32[1,8,128,128]{2,3,1,0:T(8,128)} copy(f32[1,8,128,128]{3,2,1,0:T(8,128)} %get-tuple-element.58) | data formatting | bytes 1048576
  29.4 2.0 %copy.854 = f32[1,8,128,128]{2,3,1,0:T(8,128)} copy(f32[1,8,128,128]{3,2,1,0:T(8,128)} %get-tuple-element.54) | data formatting | bytes 1048576
  31.4 2.0 %copy.846 = f32[1,8,128,128]{2,3,1,0:T(8,128)} copy(f32[1,8,128,128]{3,2,1,0:T(8,128)} %get-tuple-element.91) | data formatting | bytes 1048576
  33.5 2.1 %copy.853 = f32[1,8,128,128]{2,3,1,0:T(8,128)} copy(f32[1,8,128,128]{3,2,1,0:T(8,128)} %get-tuple-element.92) | data formatting | bytes 1048576
  35.5 2.0 %copy.855 = f32[1,7,128,128]{2,3,1,0:T(8,128)} copy(f32[1,7,128,128]{3,2,1,0:T(8,128)} %get-tuple-element.61) | data formatting | bytes 917504
  37.5 2.0 %copy.849 = f32[1,7,128,128]{2,3,1,0:T(8,128)} copy(f32[1,7,128,128]{3,2,1,0:T(8,128)} %get-tuple-element.59) | data formatting | bytes 917504
  39.5 2.0 %copy.764 = f32[8,128,128]{1,2,0:T(8,128)} copy(f32[8,128,128]{2,1,0:T(8,128)} %get-tuple-element.53) | data formatting | bytes 1048576 | tf_op jit(solution)/shard_map/unstack | solution.py:145
  41.6 2.0 %copy.856 = f32[1,8,128,128]{2,3,1,0:T(8,128)} copy(f32[1,8,128,128]{3,2,1,0:T(8,128)} %get-tuple-element.93) | data formatting | bytes 1048576
  43.6 2.0 %copy.857 = f32[1,7,128,128]{2,3,1,0:T(8,128)} copy(f32[1,7,128,128]{3,2,1,0:T(8,128)} %get-tuple-element.60) | data formatting | bytes 917504
  46.9 2.0 %fusion.17 = f32[1,8,128,128]{2,3,1,0:T(8,128)S(1)} fusion(f32[7,128,128]{1,2,0:T(8,128)} %bitcast.508, f32[1,128,128]{1,2,0:T(8,128)S(1)} %copy.761, f32[8,128,128]{1,2,0:T(8,128)} %copy.764, f32[8,128,127]{1,2,0:T(8,128)} %bitcast.498, f32[8,128,1]{1,2,0:T(1,128)S(1)} %bitcast.533, f32[1,8,128,128]{2,3,1,0:T(8,128)} %copy.856, ...), kind=kLoop, calls=%fused_computation.41 | loop fusion | flops 1310720 | bytes 4714496 | tf_op jit(solution)/shard_map/stack | solution.py:165
  49.3 1.6 fusion.7
  51.9 0.9 fusion.1
  53.4 1.0 copy.767
  54.5 2.1 %copy.776 = f32[8,128,128]{1,2,0:T(8,128)} copy(f32[8,128,128]{2,1,0:T(8,128)} %param.22) | data formatting | bytes 1048576 | tf_op args[7]
  56.6 2.1 %copy.774 = f32[8,128,128]{1,2,0:T(8,128)} copy(f32[8,128,128]{2,1,0:T(8,128)} %param.19) | data formatting | bytes 1048576 | tf_op args[4]
  58.7 2.0 %copy.792 = f32[8,128,128]{1,2,0:T(8,128)} copy(f32[8,128,128]{2,1,0:T(8,128)} %param.20) | data formatting | bytes 1048576 | tf_op args[5]
  60.9 1.5 multiply_add_fusion.1
  62.6 1.3 collective-permute-start.5
  64.8 1.3 collective-permute-start.4
  66.1 7.7 %collective-permute-done.4 = f32[3,1,128,128]{2,3,1,0:T(8,128)S(1)} collective-permute-done((f32[3,1,128,128]{2,3,1,0:T(8,128)S(1)}, f32[3,1,128,128]{2,3,1,0:T(8,128)S(1)}, u32[]{:S(2)}, u32[]{:S(2)}) %collective-permute-start.4) | collective-permute-done | bytes 196640 | tf_op jit(solution)/shard_map/ppermute | solution.py:16
  75.9 1.7 multiply_add_fusion.3
  79.4 2.3 %collective-permute-start.7 = (f32[3,8,128,1]{2,1,3,0:T(8,128)S(1)}, f32[3,8,128,1]{2,1,3,0:T(8,128)S(1)}, u32[]{:S(2)}, u32[]{:S(2)}) collective-permute-start(f32[3,8,128,1]{2,1,3,0:T(8,128)S(1)} %pad_maximum_fusion.8), channel_id=1, source_target_pairs={{0,1},{1,2},{2,3},{4,5},{5,6},{6,7},{8,9},{9,10},{10,11},{12,13},{... | collective-permute-start | bytes 36872 | tf_op jit(solution)/shard_map/ppermute | solution.py:16
  81.9 3.1 %collective-permute-start.6 = (f32[3,1,128,128]{2,3,1,0:T(8,128)S(1)}, f32[3,1,128,128]{2,3,1,0:T(8,128)S(1)}, u32[]{:S(2)}, u32[]{:S(2)}) collective-permute-start(f32[3,1,128,128]{2,3,1,0:T(8,128)S(1)} %pad_maximum_fusion.5), channel_id=1, source_target_pairs={{0,4},{4,8},{8,12},{1,5},{5,9},{9,13},{2,6},{6,10},{10,14},{3,7},{... | collective-permute-start | bytes 589832 | tf_op jit(solution)/shard_map/ppermute | solution.py:16
  85.2 3.8 %collective-permute-done.6 = f32[3,1,128,128]{2,3,1,0:T(8,128)S(1)} collective-permute-done((f32[3,1,128,128]{2,3,1,0:T(8,128)S(1)}, f32[3,1,128,128]{2,3,1,0:T(8,128)S(1)}, u32[]{:S(2)}, u32[]{:S(2)}) %collective-permute-start.6) | collective-permute-done | bytes 196640 | tf_op jit(solution)/shard_map/ppermute | solution.py:16
  91.4 0.9 fusion
  92.3 1.6 collective-permute-start.8
  93.9 1.3 copy.806
  95.2 2.2 %copy.821 = f32[8,128,128]{1,0,2:T(8,128)} copy(f32[8,128,128]{2,1,0:T(8,128)} %param.20) | data formatting | bytes 1048576 | tf_op args[5]
  97.6 1.5 multiply_add_fusion
  99.3 1.3 collective-permute-start.10
  102.7 1.4 collective-permute-start.9
  104.2 8.2 %collective-permute-done.9 = f32[3,1,128,128]{2,3,1,0:T(8,128)S(1)} collective-permute-done((f32[3,1,128,128]{2,3,1,0:T(8,128)S(1)}, f32[3,1,128,128]{2,3,1,0:T(8,128)S(1)}, u32[]{:S(2)}, u32[]{:S(2)}) %collective-permute-start.9) | collective-permute-done | bytes 196640 | tf_op jit(solution)/shard_map/ppermute | solution.py:16
  112.5 3.4 %fusion.52 = (f32[8,128,128]{1,0,2:T(8,128)S(1)}, f32[8,128,128]{1,0,2:T(8,128)S(1)}, f32[8,128,128]{1,0,2:T(8,128)S(1)}) fusion(f32[8,128,1]{1,0,2:T(8,128)S(1)} %bitcast.526, f32[8,128,127]{1,0,2:T(8,128)S(1)} %slice.721, f32[8,128,128]{1,2,0:T(8,128)S(1)} %copy-done.7, f32[8,127,128]{1,0,2:T(8,128)S(1)} %slice.723, ...), kind=kLoop, calls=%fused_computation.96 | loop fusion | flops 2228224 | bytes 8904704 | tf_op jit(solution)/shard_map/add | solution.py:203
  116.1 1.4 copy_add_fusion.4
  117.6 1.2 multiply_add_fusion.2
  118.8 2.4 %collective-permute-start.12 = (f32[3,8,128,1]{2,1,3,0:T(8,128)S(1)}, f32[3,8,128,1]{2,1,3,0:T(8,128)S(1)}, u32[]{:S(2)}, u32[]{:S(2)}) collective-permute-start(f32[3,8,128,1]{2,1,3,0:T(8,128)S(1)} %pad_maximum_fusion.9), channel_id=1, source_target_pairs={{0,1},{1,2},{2,3},{4,5},{5,6},{6,7},{8,9},{9,10},{10,11},{12,13},{... | collective-permute-start | bytes 36872 | tf_op jit(solution)/shard_map/ppermute | solution.py:16
  121.5 4.3 %collective-permute-start.11 = (f32[3,1,128,128]{2,3,1,0:T(8,128)S(1)}, f32[3,1,128,128]{2,3,1,0:T(8,128)S(1)}, u32[]{:S(2)}, u32[]{:S(2)}) collective-permute-start(f32[3,1,128,128]{2,3,1,0:T(8,128)S(1)} %pad_maximum_fusion.6), channel_id=1, source_target_pairs={{0,4},{4,8},{8,12},{1,5},{5,9},{9,13},{2,6},{6,10},{10,14},{3,7},{... | collective-permute-start | bytes 589832 | tf_op jit(solution)/shard_map/ppermute | solution.py:16
  125.8 4.5 %collective-permute-done.11 = f32[3,1,128,128]{2,3,1,0:T(8,128)S(1)} collective-permute-done((f32[3,1,128,128]{2,3,1,0:T(8,128)S(1)}, f32[3,1,128,128]{2,3,1,0:T(8,128)S(1)}, u32[]{:S(2)}, u32[]{:S(2)}) %collective-permute-start.11) | collective-permute-done | bytes 196640 | tf_op jit(solution)/shard_map/ppermute | solution.py:16
  131.1 1.4 fusion.49
  134.3 3.2 %collective-permute-done.13 = f32[3,8,128]{2,1,0:T(8,128)S(1)} collective-permute-done((f32[3,8,128]{2,1,0:T(8,128)S(1)}, f32[3,8,128]{2,1,0:T(8,128)S(1)}, u32[]{:S(2)}, u32[]{:S(2)}) %collective-permute-start.13) | collective-permute-done | bytes 12320 | tf_op jit(solution)/shard_map/ppermute | solution.py:20
  138.7 1.0 copy_add_fusion
  139.7 1.2 slice_bitcast_fusion
  140.9 1.3 collective-permute-start.15
  143.2 1.0 slice.757
  144.3 1.0 slice.744
  146.1 1.6 copy.839
  147.8 1.3 collective-permute-start.14
  149.1 8.4 %collective-permute-done.14 = f32[3,1,128,128]{2,3,1,0:T(8,128)S(1)} collective-permute-done((f32[3,1,128,128]{2,3,1,0:T(8,128)S(1)}, f32[3,1,128,128]{2,3,1,0:T(8,128)S(1)}, u32[]{:S(2)}, u32[]{:S(2)}) %collective-permute-start.14) | collective-permute-done | bytes 196640 | tf_op jit(solution)/shard_map/ppermute | solution.py:16
  157.5 3.1 %bitcast_dynamic-update-slice_fusion.2 = (f32[6,8,128,128]{2,1,3,0:T(8,128)}, f32[8,128,128]{1,0,2:T(8,128)S(1)}) fusion(f32[8,128,128]{1,0,2:T(8,128)} %copy-done.23, f32[8,128,128]{1,0,2:T(8,128)} %copy-done, f32[8,128,128]{1,0,2:T(8,128)} %copy-done.2, f32[3,8,128,128]{2,1,3,0:T(8,128)S(1)} %copy_add_fusion, f32[8,127,128]{1,0,2:T(8,128)} %slice.744, ...), kind=kLoop, calls=%fused_computation.135 | loop fusion | flops 1835007 | bytes 6287360
  160.7 1.2 slice_bitcast_fusion.3
  163.1 1.1 bitcast_dynamic-update-slice_fusion
  164.3 1.1 fusion.67
  165.8 1.0 fusion.72
  167.2 1.4 fusion.77
  168.5 3.5 %copy.840 = f32[6,8,128,128]{3,2,1,0:T(8,128)} copy(f32[6,8,128,128]{2,1,3,0:T(8,128)} %fusion.77) | data formatting | bytes 6291456
  (277 shorter events, 25.7 us)
Async XLA Ops:
  4.7 13.2 %copy-start.52 = (f32[1,8,128,128]{2,1,3,0:T(8,128)}, f32[1,8,128,128]{2,1,3,0:T(8,128)S(1)}, u32[]{:S(2)}) copy-start(f32[1,8,128,128]{2,1,3,0:T(8,128)S(1)} %copy.852) | copy-start | bytes 1572868
  4.7 40.9 %collective-permute-start.1 = (f32[3,8,128,1]{2,1,3,0:T(8,128)S(1)}, f32[3,8,128,1]{2,1,3,0:T(8,128)S(1)}, u32[]{:S(2)}, u32[]{:S(2)}) collective-permute-start(f32[3,8,128,1]{2,1,3,0:T(8,128)S(1)} %pad_maximum_fusion.7), channel_id=1, source_target_pairs={{0,1},{1,2},{2,3},{4,5},{5,6},{6,7},{8,9},{9,10},{10,11},{12,13},{... | collective-permute-start | bytes 36872 | tf_op jit(solution)/shard_map/ppermute | solution.py:16
  8.1 37.5 %collective-permute-start = (f32[3,1,128,128]{3,2,1,0:T(8,128)S(1)}, f32[3,1,128,128]{3,2,1,0:T(8,128)}, u32[]{:S(2)}, u32[]{:S(2)}) collective-permute-start(f32[3,1,128,128]{3,2,1,0:T(8,128)S(1)} %pad_maximum_fusion.4), channel_id=1, source_target_pairs={{0,4},{4,8},{8,12},{1,5},{5,9},{9,13},{2,6},{6,10},{10,14},{3,7},{... | collective-permute-start | bytes 589832 | tf_op jit(solution)/shard_map/ppermute | solution.py:16
  13.9 46.8 %collective-permute-start.2 = (f32[8,128]{1,0:T(8,128)S(1)}, f32[8,128]{1,0:T(8,128)S(1)}, u32[]{:S(2)}, u32[]{:S(2)}) collective-permute-start(f32[8,128]{1,0:T(8,128)S(1)} %get-tuple-element.38), channel_id=1, source_target_pairs={{0,16},{16,0},{1,17},{17,1},{2,18},{18,2},{3,19},{19,3},{4,20},{20... | collective-permute-start | bytes 12296 | tf_op jit(solution)/shard_map/ppermute | solution.py:20
  17.9 2.7 %copy-start.62 = (f32[8,128,128]{2,1,0:T(8,128)S(1)}, f32[8,128,128]{2,1,0:T(8,128)}, u32[]{:S(2)}) copy-start(f32[8,128,128]{2,1,0:T(8,128)} %param.22) | copy-start | bytes 1572868
  17.9 2.9 %copy-start.60 = (f32[8,128,128]{2,1,0:T(8,128)S(1)}, f32[8,128,128]{2,1,0:T(8,128)}, u32[]{:S(2)}) copy-start(f32[8,128,128]{2,1,0:T(8,128)} %param.18) | copy-start | bytes 1572868
  21.1 96.4 %copy-start = (f32[8,128,128]{1,0,2:T(8,128)}, f32[8,128,128]{1,0,2:T(8,128)S(1)}, u32[]{:S(2)}) copy-start(f32[8,128,128]{1,0,2:T(8,128)S(1)} %copy.769) | copy-start | bytes 1572868
  22.6 3.1 %copy-start.10 = (f32[8,128,128]{1,0,2:T(8,128)}, f32[8,128,128]{1,0,2:T(8,128)S(1)}, u32[]{:S(2)}) copy-start(f32[8,128,128]{1,0,2:T(8,128)S(1)} %copy.781) | copy-start | bytes 1572868
  22.6 1.7 %copy-start.72 = (s32[8,128]{1,0:T(8,128)S(1)}, s32[8,128]{1,0:T(8,128)}, u32[]{:S(2)}) copy-start(s32[8,128]{1,0:T(8,128)} %param.25) | copy-start | bytes 12292
  25.7 23.3 %copy-start.13 = (f32[8,128,128]{1,2,0:T(8,128)}, f32[8,128,128]{1,2,0:T(8,128)S(1)}, u32[]{:S(2)}) copy-start(f32[8,128,128]{1,2,0:T(8,128)S(1)} %copy.744) | copy-start | bytes 1572868
  27.1 21.8 %copy-start.19 = (f32[1,8,128,128]{2,3,1,0:T(8,128)}, f32[1,8,128,128]{2,3,1,0:T(8,128)S(1)}, u32[]{:S(2)}) copy-start(f32[1,8,128,128]{2,3,1,0:T(8,128)S(1)} %copy.847) | copy-start | bytes 1572868
  46.8 2.1 %copy-start.21 = (f32[1,8,128,128]{2,3,1,0:T(8,128)S(1)}, f32[1,8,128,128]{2,3,1,0:T(8,128)}, u32[]{:S(2)}) copy-start(f32[1,8,128,128]{2,3,1,0:T(8,128)} %copy.848) | copy-start | bytes 1572868
  46.9 2.1 %copy-start.36 = (f32[1,8,128,128]{2,3,1,0:T(8,128)S(1)}, f32[1,8,128,128]{2,3,1,0:T(8,128)}, u32[]{:S(2)}) copy-start(f32[1,8,128,128]{2,3,1,0:T(8,128)} %copy.854) | copy-start | bytes 1572868
  46.9 2.1 %copy-start.58 = (f32[1,8,128,128]{2,3,1,0:T(8,128)S(1)}, f32[1,8,128,128]{2,3,1,0:T(8,128)}, u32[]{:S(2)}) copy-start(f32[1,8,128,128]{2,3,1,0:T(8,128)} %copy.846) | copy-start | bytes 1572868
  46.9 2.1 %copy-start.59 = (f32[1,8,128,128]{2,3,1,0:T(8,128)S(1)}, f32[1,8,128,128]{2,3,1,0:T(8,128)}, u32[]{:S(2)}) copy-start(f32[1,8,128,128]{2,3,1,0:T(8,128)} %copy.853) | copy-start | bytes 1572868
  46.9 2.2 %copy-start.66 = (f32[1,7,128,128]{2,3,1,0:T(8,128)S(1)}, f32[1,7,128,128]{2,3,1,0:T(8,128)}, u32[]{:S(2)}) copy-start(f32[1,7,128,128]{2,3,1,0:T(8,128)} %copy.855) | copy-start | bytes 1376260
  46.9 2.4 %copy-start.67 = (f32[1,7,128,128]{2,3,1,0:T(8,128)S(1)}, f32[1,7,128,128]{2,3,1,0:T(8,128)}, u32[]{:S(2)}) copy-start(f32[1,7,128,128]{2,3,1,0:T(8,128)} %copy.849) | copy-start | bytes 1376260
  48.9 1.9 %copy-start.50 = (f32[1,8,128,128]{2,3,1,0:T(8,128)}, f32[1,8,128,128]{2,3,1,0:T(8,128)S(1)}, u32[]{:S(2)}) copy-start(f32[1,8,128,128]{2,3,1,0:T(8,128)S(1)} %fusion.17) | copy-start | bytes 1572868
  52.9 7.9 %collective-permute-start.3 = (f32[3,8,128]{2,1,0:T(8,128)S(1)}, f32[3,8,128]{2,1,0:T(8,128)S(1)}, u32[]{:S(2)}, u32[]{:S(2)}) collective-permute-start(f32[3,8,128]{2,1,0:T(8,128)S(1)} %fusion.1), channel_id=1, source_target_pairs={{0,16},{16,0},{1,17},{17,1},{2,18},{18,2},{3,19},{19,3},{4,20},{20... | collective-permute-start | bytes 36872 | tf_op jit(solution)/shard_map/ppermute | solution.py:20
  54.4 6.3 %copy-start.68 = (f32[2,8,128]{2,1,0:T(8,128)S(1)}, f32[2,8,128]{2,1,0:T(8,128)}, u32[]{:S(2)}) copy-start(f32[2,8,128]{2,1,0:T(8,128)} %param.23) | copy-start | bytes 24580
  54.4 6.3 %copy-start.69 = (s32[8,128]{1,0:T(8,128)S(1)}, s32[8,128]{1,0:T(8,128)}, u32[]{:S(2)}) copy-start(s32[8,128]{1,0:T(8,128)} %param.24) | copy-start | bytes 12292
  54.4 6.3 %copy-start.70 = (f32[8,128]{1,0:T(8,128)S(1)}, f32[8,128]{1,0:T(8,128)}, u32[]{:S(2)}) copy-start(f32[8,128]{1,0:T(8,128)} %param.26) | copy-start | bytes 12292
  54.4 6.3 %copy-start.71 = (f32[8,128]{1,0:T(8,128)S(1)}, f32[8,128]{1,0:T(8,128)}, u32[]{:S(2)}) copy-start(f32[8,128]{1,0:T(8,128)} %param.27) | copy-start | bytes 12292
  54.4 6.5 %copy-start.41 = (f32[1,8,128,128]{2,3,1,0:T(8,128)S(1)}, f32[1,8,128,128]{2,3,1,0:T(8,128)}, u32[]{:S(2)}) copy-start(f32[1,8,128,128]{2,3,1,0:T(8,128)} %copy-done.40) | copy-start | bytes 1572868
  54.4 6.5 %copy-start.43 = (f32[1,8,128,128]{2,3,1,0:T(8,128)S(1)}, f32[1,8,128,128]{2,3,1,0:T(8,128)}, u32[]{:S(2)}) copy-start(f32[1,8,128,128]{2,3,1,0:T(8,128)} %copy-done.42) | copy-start | bytes 1572868
  62.6 3.5 %collective-permute-start.5 = (f32[3,8,128,1]{2,3,1,0:T(1,128)S(1)}, f32[3,8,128,1]{2,3,1,0:T(1,128)S(1)}, u32[]{:S(2)}, u32[]{:S(2)}) collective-permute-start(f32[3,8,128,1]{2,3,1,0:T(1,128)S(1)} %slice.662), channel_id=1, source_target_pairs={{1,0},{2,1},{3,2},{5,4},{6,5},{7,6},{9,8},{10,9},{11,10},{13,12},{... | collective-permute-start | bytes 36872 | tf_op jit(solution)/shard_map/ppermute | solution.py:16
  64.5 9.4 %copy-start.54 = (f32[8,128,128]{1,0,2:T(8,128)S(1)}, f32[8,128,128]{1,0,2:T(8,128)}, u32[]{:S(2)}) copy-start(f32[8,128,128]{1,0,2:T(8,128)} %broadcast_multiply_fusion.3) | copy-start | bytes 1572868
  64.8 9.1 %collective-permute-start.4 = (f32[3,1,128,128]{2,3,1,0:T(8,128)S(1)}, f32[3,1,128,128]{2,3,1,0:T(8,128)S(1)}, u32[]{:S(2)}, u32[]{:S(2)}) collective-permute-start(f32[3,1,128,128]{2,3,1,0:T(8,128)S(1)} %slice.659), channel_id=1, source_target_pairs={{4,0},{8,4},{12,8},{5,1},{9,5},{13,9},{6,2},{10,6},{14,10},{7,3},{... | collective-permute-start | bytes 589832 | tf_op jit(solution)/shard_map/ppermute | solution.py:16
  73.9 1.8 %copy-start.39 = (f32[8,128,128]{1,2,0:T(8,128)S(1)}, f32[8,128,128]{1,2,0:T(8,128)}, u32[]{:S(2)}) copy-start(f32[8,128,128]{1,2,0:T(8,128)} %copy.774) | copy-start | bytes 1572868
  73.9 2.0 %copy-start.56 = (f32[8,128,128]{1,2,0:T(8,128)S(1)}, f32[8,128,128]{1,2,0:T(8,128)}, u32[]{:S(2)}) copy-start(f32[8,128,128]{1,2,0:T(8,128)} %copy.776) | copy-start | bytes 1572868
  74.5 15.0 %copy-start.6 = (f32[8,128,128]{1,2,0:T(8,128)}, f32[8,128,128]{1,2,0:T(8,128)S(1)}, u32[]{:S(2)}) copy-start(f32[8,128,128]{1,2,0:T(8,128)S(1)} %get-tuple-element.67) | copy-start | bytes 1572868
  77.6 11.9 %copy-start.4 = (f32[8,128,128]{1,2,0:T(8,128)}, f32[8,128,128]{1,2,0:T(8,128)S(1)}, u32[]{:S(2)}) copy-start(f32[8,128,128]{1,2,0:T(8,128)S(1)} %get-tuple-element.84) | copy-start | bytes 1572868
  77.6 11.9 %copy-start.17 = (f32[8,128,128]{1,2,0:T(8,128)}, f32[8,128,128]{1,2,0:T(8,128)S(1)}, u32[]{:S(2)}) copy-start(f32[8,128,128]{1,2,0:T(8,128)S(1)} %get-tuple-element.35) | copy-start | bytes 1572868
  78.1 10.9 %copy-start.29 = (f32[8,128,128]{1,2,0:T(8,128)}, f32[8,128,128]{1,2,0:T(8,128)S(1)}, u32[]{:S(2)}) copy-start(f32[8,128,128]{1,2,0:T(8,128)S(1)} %get-tuple-element.49) | copy-start | bytes 1572868
  79.3 10.1 %copy-start.25 = (f32[8,128,128]{1,0,2:T(8,128)}, f32[8,128,128]{1,0,2:T(8,128)S(1)}, u32[]{:S(2)}) copy-start(f32[8,128,128]{1,0,2:T(8,128)S(1)} %copy_add_fusion.5) | copy-start | bytes 1572868
  79.4 5.8 %collective-permute-start.7 = (f32[3,8,128,1]{2,1,3,0:T(8,128)S(1)}, f32[3,8,128,1]{2,1,3,0:T(8,128)S(1)}, u32[]{:S(2)}, u32[]{:S(2)}) collective-permute-start(f32[3,8,128,1]{2,1,3,0:T(8,128)S(1)} %pad_maximum_fusion.8), channel_id=1, source_target_pairs={{0,1},{1,2},{2,3},{4,5},{5,6},{6,7},{8,9},{9,10},{10,11},{12,13},{... | collective-permute-start | bytes 36872 | tf_op jit(solution)/shard_map/ppermute | solution.py:16
  81.8 7.2 %copy-start.14 = (f32[8,128,128]{1,2,0:T(8,128)S(1)}, f32[8,128,128]{1,2,0:T(8,128)}, u32[]{:S(2)}) copy-start(f32[8,128,128]{1,2,0:T(8,128)} %copy-done.13) | copy-start | bytes 1572868
  81.9 7.1 %collective-permute-start.6 = (f32[3,1,128,128]{2,3,1,0:T(8,128)S(1)}, f32[3,1,128,128]{2,3,1,0:T(8,128)S(1)}, u32[]{:S(2)}, u32[]{:S(2)}) collective-permute-start(f32[3,1,128,128]{2,3,1,0:T(8,128)S(1)} %pad_maximum_fusion.5), channel_id=1, source_target_pairs={{0,4},{4,8},{8,12},{1,5},{5,9},{9,13},{2,6},{6,10},{10,14},{3,7},{... | collective-permute-start | bytes 589832 | tf_op jit(solution)/shard_map/ppermute | solution.py:16
  92.3 5.3 %copy-start.45 = (f32[1,8,128,128]{2,3,1,0:T(8,128)S(1)}, f32[1,8,128,128]{2,3,1,0:T(8,128)}, u32[]{:S(2)}) copy-start(f32[1,8,128,128]{2,3,1,0:T(8,128)} %copy-done.44) | copy-start | bytes 1572868
  92.3 5.3 %copy-start.47 = (f32[1,8,128,128]{2,3,1,0:T(8,128)S(1)}, f32[1,8,128,128]{2,3,1,0:T(8,128)}, u32[]{:S(2)}) copy-start(f32[1,8,128,128]{2,3,1,0:T(8,128)} %copy-done.46) | copy-start | bytes 1572868
  92.3 5.1 %collective-permute-start.8 = (f32[3,8,128]{2,1,0:T(8,128)S(1)}, f32[3,8,128]{2,1,0:T(8,128)S(1)}, u32[]{:S(2)}, u32[]{:S(2)}) collective-permute-start(f32[3,8,128]{2,1,0:T(8,128)S(1)} %fusion), channel_id=1, source_target_pairs={{0,16},{16,0},{1,17},{17,1},{2,18},{18,2},{3,19},{19,3},{4,20},{20... | collective-permute-start | bytes 36872 | tf_op jit(solution)/shard_map/ppermute | solution.py:20
  95.2 22.4 %copy-start.2 = (f32[8,128,128]{1,0,2:T(8,128)}, f32[8,128,128]{1,0,2:T(8,128)S(1)}, u32[]{:S(2)}) copy-start(f32[8,128,128]{1,0,2:T(8,128)S(1)} %copy.806) | copy-start | bytes 1572868
  99.3 4.9 %collective-permute-start.10 = (f32[3,8,128,1]{2,3,1,0:T(1,128)S(1)}, f32[3,8,128,1]{2,3,1,0:T(1,128)S(1)}, u32[]{:S(2)}, u32[]{:S(2)}) collective-permute-start(f32[3,8,128,1]{2,3,1,0:T(1,128)S(1)} %slice.706), channel_id=1, source_target_pairs={{1,0},{2,1},{3,2},{5,4},{6,5},{7,6},{9,8},{10,9},{11,10},{13,12},{... | collective-permute-start | bytes 36872 | tf_op jit(solution)/shard_map/ppermute | solution.py:16
  102.7 9.8 %copy-start.5 = (f32[8,128,128]{1,2,0:T(8,128)S(1)}, f32[8,128,128]{1,2,0:T(8,128)}, u32[]{:S(2)}) copy-start(f32[8,128,128]{1,2,0:T(8,128)} %copy-done.4) | copy-start | bytes 1572868
  102.7 9.8 %copy-start.7 = (f32[8,128,128]{1,2,0:T(8,128)S(1)}, f32[8,128,128]{1,2,0:T(8,128)}, u32[]{:S(2)}) copy-start(f32[8,128,128]{1,2,0:T(8,128)} %copy-done.6) | copy-start | bytes 1572868
  102.7 9.8 %copy-start.11 = (f32[8,128,128]{1,0,2:T(8,128)S(1)}, f32[8,128,128]{1,0,2:T(8,128)}, u32[]{:S(2)}) copy-start(f32[8,128,128]{1,0,2:T(8,128)} %copy-done.10) | copy-start | bytes 1572868
  102.7 9.8 %copy-start.32 = (f32[8,128,128]{1,2,0:T(8,128)S(1)}, f32[8,128,128]{1,2,0:T(8,128)}, u32[]{:S(2)}) copy-start(f32[8,128,128]{1,2,0:T(8,128)} %get-tuple-element.143) | copy-start | bytes 1572868
  102.7 9.6 %collective-permute-start.9 = (f32[3,1,128,128]{2,3,1,0:T(8,128)S(1)}, f32[3,1,128,128]{2,3,1,0:T(8,128)S(1)}, u32[]{:S(2)}, u32[]{:S(2)}) collective-permute-start(f32[3,1,128,128]{2,3,1,0:T(8,128)S(1)} %slice.703), channel_id=1, source_target_pairs={{4,0},{8,4},{12,8},{5,1},{9,5},{13,9},{6,2},{10,6},{14,10},{7,3},{... | collective-permute-start | bytes 589832 | tf_op jit(solution)/shard_map/ppermute | solution.py:16
  112.5 3.5 %copy-start.18 = (f32[8,128,128]{1,2,0:T(8,128)S(1)}, f32[8,128,128]{1,2,0:T(8,128)}, u32[]{:S(2)}) copy-start(f32[8,128,128]{1,2,0:T(8,128)} %copy-done.17) | copy-start | bytes 1572868
  116.0 15.1 %copy-start.8 = (f32[8,128,128]{1,0,2:T(8,128)}, f32[8,128,128]{1,0,2:T(8,128)S(1)}, u32[]{:S(2)}) copy-start(f32[8,128,128]{1,0,2:T(8,128)S(1)} %get-tuple-element.96) | copy-start | bytes 1572868
  117.5 13.6 %copy-start.23 = (f32[8,128,128]{1,0,2:T(8,128)}, f32[8,128,128]{1,0,2:T(8,128)S(1)}, u32[]{:S(2)}) copy-start(f32[8,128,128]{1,0,2:T(8,128)S(1)} %get-tuple-element.28) | copy-start | bytes 1572868
  118.7 11.5 %copy-start.15 = (f32[8,128,128]{1,0,2:T(8,128)}, f32[8,128,128]{1,0,2:T(8,128)S(1)}, u32[]{:S(2)}) copy-start(f32[8,128,128]{1,0,2:T(8,128)S(1)} %get-tuple-element.51) | copy-start | bytes 1572868
  118.7 12.4 %copy-start.27 = (f32[8,128,128]{1,0,2:T(8,128)}, f32[8,128,128]{1,0,2:T(8,128)S(1)}, u32[]{:S(2)}) copy-start(f32[8,128,128]{1,0,2:T(8,128)S(1)} %get-tuple-element.50) | copy-start | bytes 1572868
  118.8 7.0 %collective-permute-start.12 = (f32[3,8,128,1]{2,1,3,0:T(8,128)S(1)}, f32[3,8,128,1]{2,1,3,0:T(8,128)S(1)}, u32[]{:S(2)}, u32[]{:S(2)}) collective-permute-start(f32[3,8,128,1]{2,1,3,0:T(8,128)S(1)} %pad_maximum_fusion.9), channel_id=1, source_target_pairs={{0,1},{1,2},{2,3},{4,5},{5,6},{6,7},{8,9},{9,10},{10,11},{12,13},{... | collective-permute-start | bytes 36872 | tf_op jit(solution)/shard_map/ppermute | solution.py:16
  121.3 9.0 %copy-start.34 = (f32[8,128,128]{1,2,0:T(8,128)S(1)}, f32[8,128,128]{1,2,0:T(8,128)}, u32[]{:S(2)}) copy-start(f32[8,128,128]{1,2,0:T(8,128)} %get-tuple-element.101) | copy-start | bytes 1572868
  121.5 8.8 %collective-permute-start.11 = (f32[3,1,128,128]{2,3,1,0:T(8,128)S(1)}, f32[3,1,128,128]{2,3,1,0:T(8,128)S(1)}, u32[]{:S(2)}, u32[]{:S(2)}) collective-permute-start(f32[3,1,128,128]{2,3,1,0:T(8,128)S(1)} %pad_maximum_fusion.6), channel_id=1, source_target_pairs={{0,4},{4,8},{8,12},{1,5},{5,9},{9,13},{2,6},{6,10},{10,14},{3,7},{... | collective-permute-start | bytes 589832 | tf_op jit(solution)/shard_map/ppermute | solution.py:16
  133.7 3.8 %collective-permute-start.13 = (f32[3,8,128]{2,1,0:T(8,128)S(1)}, f32[3,8,128]{2,1,0:T(8,128)S(1)}, u32[]{:S(2)}, u32[]{:S(2)}) collective-permute-start(f32[3,8,128]{2,1,0:T(8,128)S(1)} %fusion.2), channel_id=1, source_target_pairs={{0,16},{16,0},{1,17},{17,1},{2,18},{18,2},{3,19},{19,3},{4,20},{20... | collective-permute-start | bytes 36872 | tf_op jit(solution)/shard_map/ppermute | solution.py:20
  140.9 8.1 %collective-permute-start.15 = (f32[3,8,128,1]{2,1,3,0:T(8,128)S(1)}, f32[3,8,128,1]{2,1,3,0:T(8,128)S(1)}, u32[]{:S(2)}, u32[]{:S(2)}) collective-permute-start(f32[3,8,128,1]{2,1,3,0:T(8,128)S(1)} %slice.749), channel_id=1, source_target_pairs={{1,0},{2,1},{3,2},{5,4},{6,5},{7,6},{9,8},{10,9},{11,10},{13,12},{... | collective-permute-start | bytes 36872 | tf_op jit(solution)/shard_map/ppermute | solution.py:16
  147.8 9.7 %collective-permute-start.14 = (f32[3,1,128,128]{2,3,1,0:T(8,128)S(1)}, f32[3,1,128,128]{2,3,1,0:T(8,128)S(1)}, u32[]{:S(2)}, u32[]{:S(2)}) collective-permute-start(f32[3,1,128,128]{2,3,1,0:T(8,128)S(1)} %bitcast.519), channel_id=1, source_target_pairs={{4,0},{8,4},{12,8},{5,1},{9,5},{13,9},{6,2},{10,6},{14,10},{7,3},{... | collective-permute-start | bytes 589832 | tf_op jit(solution)/shard_map/ppermute | solution.py:16
  157.5 3.2 %copy-start.1 = (f32[8,128,128]{1,0,2:T(8,128)S(1)}, f32[8,128,128]{1,0,2:T(8,128)}, u32[]{:S(2)}) copy-start(f32[8,128,128]{1,0,2:T(8,128)} %copy-done) | copy-start | bytes 1572868
  157.5 3.2 %copy-start.3 = (f32[8,128,128]{1,0,2:T(8,128)S(1)}, f32[8,128,128]{1,0,2:T(8,128)}, u32[]{:S(2)}) copy-start(f32[8,128,128]{1,0,2:T(8,128)} %copy-done.2) | copy-start | bytes 1572868
  157.5 3.1 %copy-start.16 = (f32[8,128,128]{1,0,2:T(8,128)S(1)}, f32[8,128,128]{1,0,2:T(8,128)}, u32[]{:S(2)}) copy-start(f32[8,128,128]{1,0,2:T(8,128)} %copy-done.15) | copy-start | bytes 1572868
  157.5 3.1 %copy-start.24 = (f32[8,127,128]{1,0,2:T(8,128)S(1)}, f32[8,127,128]{1,0,2:T(8,128)}, u32[]{:S(2)}) copy-start(f32[8,127,128]{1,0,2:T(8,128)} %slice.744) | copy-start | bytes 1560580
  157.5 3.1 %copy-start.31 = (f32[8,128,127]{1,0,2:T(8,128)S(1)}, f32[8,128,127]{1,0,2:T(8,128)}, u32[]{:S(2)}) copy-start(f32[8,128,127]{1,0,2:T(8,128)} %slice.748) | copy-start | bytes 1560580
  (27 other events, 34.7 us)
where the time goes:
time: 174 us; the launch traced here: 172 us
  local copies, waits for them, and re-layouts  67.2 us (39%)
  waiting for transfers between devices  35.8 us (21%)
  other arithmetic  35.1 us (20%)
  starting transfers between devices  31.7 us (18%)
  between operations  2.29 us (1%)
    unnamed x175, local copies, waits for them, and re-layouts  43.8 us
    ppermute x12, waiting for transfers between devices, from_behind(): return lax.ppermute(shard, axis, pairs)  32.6 us
    ppermute x12, starting transfers between devices, from_behind(): return lax.ppermute(shard, axis, pairs)  27.3 us
    another operation x9, other arithmetic, one_step(): trial = jnp.stack([trial_x, trial_y, trial_z])  7.42 us
    unnamed x4, other arithmetic  6.28 us
    another operation x2, local copies, waits for them, and re-layouts, one_step(): stress_xx, stress_yy, stress_zz, stress_yz, stress_xz, stress_xy = stress  5.44 us
    ppermute x4, starting transfers between devices, swapped(): lax.ppermute(shard, axis, [(i, i ^ 1 << apart) for i in range(lax.axis_si...  4.31 us
    add x3, other arithmetic, one_step(): moved = trial + spread * correction[:, :, None, :]  4.05 us
  transfers between devices with their start and end apart: 16, of which 6 were waited for; matrix products, arithmetic and copies ran while one was open for 33% of the time, Pallas kernels for 0%

commit v1 on v0

v1 whole, which is shorter than its diff:
```python
import functools

import jax
import jax.numpy as jnp
from jax import lax
from jax.experimental import pallas as pl
from jax.experimental.pallas import tpu as pltpu
from jax.sharding import PartitionSpec as P

STEPS = 3
NEWTON = 3
DT = 0.2

PAD = 8
HALO = 3
STRIP = 8

XX, YY, ZZ, YZ, XZ, XY = range(6)
ALONG_Y = (XY, YY, YZ)
B, C11, C13, C33, C44, C66 = range(6)
FIELDS = [("v", c) for c in range(3)] + [("s", c) for c in range(6)] + [("m", c) for c in range(6)]
PRE_Y, PRE_Z, MASK, STRENGTH, RATE, SLIP, OWN_B, OTHER_B = range(8)

VMEM = pltpu.MemorySpace.VMEM
HBM = pltpu.MemorySpace.HBM
SMEM = pltpu.MemorySpace.SMEM


def in_vmem():
    return pl.BlockSpec(memory_space=VMEM)


def in_hbm():
    return pl.BlockSpec(memory_space=HBM)


def in_smem():
    return pl.BlockSpec(memory_space=SMEM)


def roll(values, by):
    by = by % values.shape[-1]
    return values if by == 0 else pltpu.roll(values, by, values.ndim - 1)


def at(ref, field, tile, y, row):
    return ref[field, tile, y, pl.ds(PAD + row, 8), :]


def z_below(pair, lanes):
    one, two = roll(pair[0], 1), roll(pair[1], 1)
    first = lanes == 0
    return jnp.where(first, two, one), jnp.where(first, one, two)


def z_above(pair, lanes):
    one, two = roll(pair[0], -1), roll(pair[1], -1)
    last = lanes == pair[0].shape[-1] - 1
    return jnp.where(last, two, one), jnp.where(last, one, two)


def trial_tile(v, s, m, y, row, below, lanes):
    both = (0, 1)
    behind = {c: z_below([at(s, c, t, y, row) for t in both], lanes) for c in (XZ, YZ, ZZ)}
    out = []
    for t in both:
        own = {c: at(s, c, t, y, row) for c in range(6)}
        lower_x = {c: own[c] - at(s, c, t, y, row - 1) for c in (XX, XY, XZ)}
        if below is None:
            lower_y = {c: own[c] for c in ALONG_Y}
        else:
            lower_y = {c: own[c] - below(c, t) for c in ALONG_Y}
        scale = DT * m[B, t, y, pl.ds(row, 8), :]
        total = (
            lower_x[XX] + lower_y[XY] + (own[XZ] - behind[XZ][t]),
            lower_x[XY] + lower_y[YY] + (own[YZ] - behind[YZ][t]),
            lower_x[XZ] + lower_y[YZ] + (own[ZZ] - behind[ZZ][t]),
        )
        out.append([at(v, c, t, y, row) + scale * total[c] for c in range(3)])
    return out


def stress_tile(v, s, m, y, row, lanes):
    both = (0, 1)
    own = [[at(v, c, t, y, row) for t in both] for c in range(3)]
    ahead = [z_above(own[c], lanes) for c in range(3)]
    for t in both:
        vx, vy, vz = own[0][t], own[1][t], own[2][t]
        over_x = [at(v, c, t, y, row + 1) for c in range(3)]
        over_y = [at(v, c, t, y + 1, row) for c in range(3)]
        exx, eyy, ezz = over_x[0] - vx, over_y[1] - vy, ahead[2][t] - vz
        c11, c13, c33, c44, c66 = (m[k, t, y, pl.ds(row, 8), :] for k in (C11, C13, C33, C44, C66))
        c12 = c11 - 2.0 * c66
        third = c13 * ezz
        change = {
            XX: c11 * exx + c12 * eyy + third,
            YY: c12 * exx + c11 * eyy + third,
            ZZ: c13 * (exx + eyy) + c33 * ezz,
            YZ: c44 * ((ahead[1][t] - vy) + (over_y[2] - vz)),
            XZ: c44 * ((ahead[0][t] - vx) + (over_x[2] - vz)),
            XY: c66 * ((over_y[0] - vx) + (over_x[1] - vy)),
        }
        for c, gain in change.items():
            s[c, t, y, pl.ds(PAD + row, 8), :] = at(s, c, t, y, row) + DT * gain


def lane_index(like):
    return lax.broadcasted_iota(jnp.int32, like, len(like) - 1)


def strip_pack(pieces, eighths):
    packed = jnp.zeros_like(pieces[0])
    for k, piece in enumerate(pieces):
        packed = jnp.where(eighths == k, roll(piece, STRIP * k + HALO), packed)
    return packed


def strip_take(packed, k):
    return roll(packed, -(STRIP * k + HALO))


def field_ref(kind, v, s, m):
    return {"v": v, "s": s, "m": m}[kind]


def slot_of(index, width):
    per_plane = (width - 5) // HALO
    return index // per_plane, index % per_plane


def z_slots(ny, width):
    slots = {}
    for f in range(len(FIELDS)):
        for y in range(ny):
            slots[f, y] = slot_of(f * ny + y, width)
    return slots, 1 + max(p for p, _ in slots.values())


def load_kernel(
    flags,
    region_a,
    region_normal,
    ids,
    mask,
    inverse_rate,
    slip,
    prestress,
    thirds,
    velocity,
    stress,
    *rest,
):
    raw_m = rest[:6]
    v, s, m, fault, z_a, z_b = rest[6:12]
    sems = rest[12]
    ny, nx, width = velocity.shape[1:]
    copies = []
    for c in range(3):
        copies.append((velocity.at[c], v.at[c, 0, pl.ds(0, ny), pl.ds(PAD, nx), :]))
    for c in range(6):
        copies.append((stress.at[c], s.at[c, 0, :, pl.ds(PAD, nx), :]))
    for c in range(6):
        copies.append((raw_m[c], m.at[c, 0]))
    copies = [pltpu.make_async_copy(a, b, sems.at[k]) for k, (a, b) in enumerate(copies)]
    for copy in copies:
        copy.start()
    zeros = jnp.zeros((PAD, width), jnp.float32)
    for t in range(2):
        for y in range(ny):
            for c in (XX, XY, XZ):
                s[c, t, y, 0:PAD, :] = zeros
            for c in range(3):
                v[c, t, y, PAD + nx : PAD + nx + PAD, :] = zeros
    kinds = ids[...]
    a_part = jnp.zeros((ny, width), jnp.float32)
    n_part = jnp.zeros((ny, width), jnp.float32)
    for k in range(region_a.shape[0]):
        a_part = jnp.where(kinds == k, region_a[k], a_part)
        n_part = jnp.where(kinds == k, region_normal[k], n_part)
    fault[PRE_Y, 0, 0:ny, :] = prestress[0]
    fault[PRE_Z, 0, 0:ny, :] = prestress[1]
    fault[MASK, 0, 0:ny, :] = mask[...].astype(jnp.float32)
    fault[STRENGTH, 0, 0:ny, :] = a_part * n_part
    fault[RATE, 0, 0:ny, :] = inverse_rate[...]
    fault[SLIP, 0, 0:ny, :] = slip[...]
    for copy in copies:
        copy.wait()

    slots, planes = z_slots(ny, width)
    odd = flags[2] == 1

    def emit(pieces, row):
        group = thirds[...]
        up = [jnp.zeros((8, width), jnp.float32) for _ in range(planes)]
        down = [jnp.zeros((8, width), jnp.float32) for _ in range(planes)]
        for plane, pos, piece in pieces:
            moved = roll(piece, HALO * pos + HALO)
            up[plane] = jnp.where(group == pos, moved, up[plane])
            down[plane] = jnp.where(group == pos + 1, moved, down[plane])
        for plane in range(planes):
            z_a[plane, pl.ds(row, 8), :] = jnp.where(odd, down[plane], up[plane])
            z_b[plane, pl.ds(row, 8), :] = jnp.where(odd, up[plane], down[plane])

    def pack(i, carry):
        row = pl.multiple_of(i * 8, 8)
        pieces = []
        for f, (kind, c) in enumerate(FIELDS):
            shift = 0 if kind == "m" else PAD
            for y in range(ny):
                ref = field_ref(kind, v, s, m)
                pieces.append((*slots[f, y], ref[c, 0, y, pl.ds(row + shift, 8), :]))
        emit(pieces, row)
        return carry

    lax.fori_loop(0, nx // 8, pack, 0)
    emit([(0, k, fault[k, 0, 0:8, :]) for k in range(6)], nx)


def write_messages(v, s, eighths, odd, row, y_a, y_b, extra):
    last = s.shape[2] - 1
    up = [at(s, c, 0, last, row) for c in ALONG_Y]
    down = [at(v, c, 0, 0, row) for c in range(3)]
    up_strip = [at(s, c, 1, last, row) for c in ALONG_Y]
    down_strip = [at(v, c, 1, 0, row) for c in range(3)]
    if extra is not None:
        both = extra[B, 0, 0, pl.ds(row, 8), :]
        up.append(both)
        down.append(both)
        both = extra[B, 1, 0, pl.ds(row, 8), :]
        up_strip.append(both)
        down_strip.append(both)
    up.append(strip_pack(up_strip, eighths))
    down.append(strip_pack(down_strip, eighths))
    for k in range(len(up)):
        y_a[k, pl.ds(row, 8), :] = jnp.where(odd, down[k], up[k])
        y_b[k, pl.ds(row, 8), :] = jnp.where(odd, up[k], down[k])


def partial_trials(v, s, m, nx, lanes):
    for row in range(0, nx, 8):
        new = trial_tile(v, s, m, 0, row, None, lanes)
        for t in range(2):
            for c in range(3):
                v[c, t, 0, pl.ds(PAD + row, 8), :] = new[t][c]


def widen_kernel(flags, thirds, eighths, r_a, r_b, v_in, s_in, m_in, f_in, v, s, m, fault, y_a, y_b):
    ny, nx, width = m.shape[2:]
    slots, planes = z_slots(ny, width)
    odd_z, odd_y = flags[2] == 1, flags[1] == 1
    lanes = lane_index((8, width))

    def take(row, wanted):
        group = thirds[...]
        from_a = [r_a[p, pl.ds(row, 8), :] for p in range(planes)]
        from_b = [r_b[p, pl.ds(row, 8), :] for p in range(planes)]
        low = [jnp.where(odd_z, a, b) for a, b in zip(from_a, from_b)]
        high = [jnp.where(odd_z, b, a) for a, b in zip(from_a, from_b)]
        for (plane, pos), store in wanted:
            store(roll(jnp.where(group == pos, low[plane], high[plane]), -(HALO * pos + HALO)))

    def unpack(i, carry):
        row = pl.multiple_of(i * 8, 8)

        def store_to(ref, c, y, shift):
            def store(value):
                ref[c, 1, y, pl.ds(row + shift, 8), :] = value

            return store

        wanted = []
        for f, (kind, c) in enumerate(FIELDS):
            shift = 0 if kind == "m" else PAD
            for y in range(ny):
                wanted.append((slots[f, y], store_to(field_ref(kind, v, s, m), c, y, shift)))
        take(row, wanted)
        return carry

    lax.fori_loop(0, nx // 8, unpack, 0)

    def store_fault(k):
        def store(value):
            fault[k, 1, 0:8, :] = value

        return store

    take(nx, [((0, k), store_fault(k)) for k in range(6)])
    partial_trials(v, s, m, nx, lanes)
    for row in range(0, nx, 8):
        write_messages(v, s, eighths[...], odd_y, row, y_a, y_b, m)
    for k in range(6):
        for t in range(2):
            line = fault[k, t, 0:1, :]
            y_a[t, nx + k : nx + k + 1, :] = line
            y_b[t, nx + k : nx + k + 1, :] = line


def inner_kernel(s_in, v_in, m, v, s):
    ny, nx, width = m.shape[2:]
    lanes = lane_index((8, width))

    def trials(y, carry):
        for row in range(0, nx, 8):
            new = trial_tile(
                v, s, m, y, row, lambda c, t, row=row: at(s, c, t, y - 1, row), lanes
            )
            for t in range(2):
                for c in range(3):
                    v[c, t, y, pl.ds(PAD + row, 8), :] = new[t][c]
        return carry

    lax.fori_loop(1, ny, trials, 0)

    def stresses(y, carry):
        for row in range(8, nx - 8, 8):
            stress_tile(v, s, m, y, row, lanes)
        return carry

    lax.fori_loop(1, ny - 1, stresses, 0)


def finish_kernel(first, flags, eighths, r_a, r_b, s, m, *rest):
    if first:
        v_in, f_in, v, fault, ahead_b, f_msg, rows = rest
    else:
        v_in, ahead_b, v, f_msg, rows = rest
    ny, nx, width = m.shape[2:]
    minus, odd = flags[0] == 0, flags[1] == 1
    n = 4 if first else 3

    if first:
        for t in range(2):
            line = jnp.where(odd, r_b[t, nx : nx + 8, :], r_a[t, nx : nx + 8, :])
            for k in range(6):
                fault[k, t, ny : ny + 1, :] = line[k : k + 1, :]
    for row in range(0, nx, 8):
        from_a = [r_a[k, pl.ds(row, 8), :] for k in range(n + 1)]
        from_b = [r_b[k, pl.ds(row, 8), :] for k in range(n + 1)]
        low = [jnp.where(odd, a, b) for a, b in zip(from_a, from_b)]
        high = [jnp.where(odd, b, a) for a, b in zip(from_a, from_b)]
        if first:
            ahead_b[0, pl.ds(row, 8), :] = high[3]
            ahead_b[1, pl.ds(row, 8), :] = strip_take(high[n], 3)
        for t in range(2):
            scale = DT * m[B, t, 0, pl.ds(row, 8), :]
            scale_ahead = DT * ahead_b[t, pl.ds(row, 8), :]
            for c in range(3):
                low_c = low[c] if t == 0 else strip_take(low[n], c)
                high_c = high[c] if t == 0 else strip_take(high[n], c)
                v[c, t, 0, pl.ds(PAD + row, 8), :] = at(v, c, t, 0, row) - scale * low_c
                v[c, t, ny, pl.ds(PAD + row, 8), :] = high_c - scale_ahead * at(
                    s, ALONG_Y[c], t, ny - 1, row
                )
    f_msg[...] = jnp.zeros_like(f_msg)
    rows[...] = jnp.zeros_like(rows)
    for c in range(3):
        for y in range(ny + 1):
            for t in range(2):
                line = jnp.where(
                    minus,
                    v[c, t, y, PAD + nx - 1 : PAD + nx, :],
                    v[c, t, y, PAD : PAD + 1, :],
                )
                if t == 0:
                    f_msg[c, y : y + 1, :] = line
                else:
                    rows[c, y : y + 1, :] = line
    if first:
        for t in range(2):
            for y in range(ny + 1):
                if y < ny:
                    line = jnp.where(minus, m[B, t, y, nx - 1 : nx, :], m[B, t, y, 0:1, :])
                else:
                    line = jnp.where(minus, ahead_b[t, nx - 1 : nx, :], ahead_b[t, 0:1, :])
                fault[OWN_B, t, y : y + 1, :] = line
                if t == 0:
                    f_msg[3, y : y + 1, :] = line
                else:
                    rows[3, y : y + 1, :] = line
    for half in range(0, f_msg.shape[1], 8):
        f_msg[n, half : half + 8, :] = strip_pack(
            [rows[k, half : half + 8, :] for k in range(n)], eighths[...]
        )


def rim_kernel(v, m, s_in, s):
    ny, nx, width = m.shape[2:]
    lanes = lane_index((8, width))

    def planes(i, carry):
        for row in range(8, nx - 8, 8):
            stress_tile(v, s, m, i * (ny - 1), row, lanes)
        return carry

    lax.fori_loop(0, 2, planes, 0)


def inverse_sinh(values):
    size = jnp.abs(values)
    sign = jnp.where(values > 0.0, 1.0, jnp.where(values < 0.0, -1.0, 0.0))
    return sign * jnp.log(size + jnp.sqrt(size * size + 1.0))


def friction(minus_side, plus_side, minus_b, plus_b, par):
    total = DT * (minus_b + plus_b)
    impedance = 1.0 / jnp.where(total > 0.0, total, 1.0)
    jump = [p - q for p, q in zip(plus_side, minus_side)]
    locked_y = par[PRE_Y] + impedance * jump[1]
    locked_z = par[PRE_Z] + impedance * jump[2]
    magnitude = jnp.sqrt(locked_y * locked_y + locked_z * locked_z + 1.0)
    rate, strength, slip = par[RATE], par[STRENGTH], par[SLIP]
    for _ in range(NEWTON):
        scaled = rate * slip
        residual = magnitude - impedance * slip - strength * inverse_sinh(scaled)
        tangent = -impedance - strength * rate / jnp.sqrt(1.0 + scaled * scaled)
        slip = slip - residual / tangent
    slip = slip * par[MASK]
    retained = 1.0 - impedance * slip / magnitude
    traction = (
        impedance * jump[0],
        retained * locked_y - par[PRE_Y],
        retained * locked_z - par[PRE_Z],
    )
    return traction, slip


def fault_kernel(first, final, flags, eighths, f_own, f_other, m, *rest):
    v_in, s_in, fault_in, v, s, fault = rest[:6]
    if final:
        new_v, new_s, slip_out, rows, sems = rest[6:]
    else:
        y_a, y_b, rows = rest[6:]
    ny, nx, width = m.shape[2:]
    minus, odd = flags[0] == 0, flags[1] == 1
    lanes = lane_index((8, width))
    n = 4 if first else 3
    high = f_own.shape[1]
    sign = jnp.where(minus, DT, -DT)
    for t in range(2):
        for half in range(0, high, 8):
            span = slice(half, half + 8)

            def piece(ref, k):
                return ref[k, span, :] if t == 0 else strip_take(ref[n, span, :], k)

            if first:
                fault[OTHER_B, t, span, :] = piece(f_other, 3)
            own = [piece(f_own, c) for c in range(3)]
            other = [piece(f_other, c) for c in range(3)]
            par = [fault[k, t, span, :] for k in range(8)]
            m_side = [jnp.where(minus, a, b) for a, b in zip(own, other)]
            p_side = [jnp.where(minus, b, a) for a, b in zip(own, other)]
            m_b = jnp.where(minus, par[OWN_B], par[OTHER_B])
            p_b = jnp.where(minus, par[OTHER_B], par[OWN_B])
            traction, slip = friction(m_side, p_side, m_b, p_b, par)
            fault[SLIP, t, span, :] = slip
            for c in range(3):
                rows[c, t, span, :] = own[c] + sign * par[OWN_B] * traction[c]
    for side, row in ((0, PAD + nx - 1), (1, PAD)):

        @pl.when(flags[0] == side)
        def _(row=row):
            for c in range(3):
                for t in range(2):
                    for y in range(ny + 1):
                        v[c, t, y, row : row + 1, :] = rows[c, t, y : y + 1, :]

    def ends(y, carry):
        for row in (0, nx - 8):
            stress_tile(v, s, m, y, row, lanes)
        return carry

    lax.fori_loop(0, ny, ends, 0)
    if final:
        slip_out[...] = fault[SLIP, 0, 0:ny, :]
        copies = []
        for c in range(3):
            copies.append((v.at[c, 0, pl.ds(0, ny), pl.ds(PAD, nx), :], new_v.at[c]))
        for c in range(6):
            copies.append((s.at[c, 0, :, pl.ds(PAD, nx), :], new_s.at[c]))
        copies = [pltpu.make_async_copy(a, b, sems.at[k]) for k, (a, b) in enumerate(copies)]
        for copy in copies:
            copy.start()
        for copy in copies:
            copy.wait()
    else:
        partial_trials(v, s, m, nx, lanes)
        for row in range(0, nx, 8):
            write_messages(v, s, eighths[...], odd, row, y_a, y_b, None)


def f32(*shape):
    return VMEM(shape, jnp.float32)


def call(kernel, name, outs, in_specs, aliases, scratch=(), flops=0, out_specs=None):
    return pl.pallas_call(
        kernel,
        out_shape=tuple(outs),
        in_specs=in_specs,
        out_specs=tuple(out_specs or [in_vmem() for _ in outs]),
        input_output_aliases=aliases,
        scratch_shapes=list(scratch),
        compiler_params=pltpu.CompilerParams(vmem_limit_bytes=8 << 20),
        cost_estimate=pl.CostEstimate(flops=flops, bytes_accessed=0, transcendentals=0),
        name=name,
    )


def pair_swaps(a, b, axis):
    size = lax.axis_size(axis)
    out = []
    for value, start in ((a, 0), (b, 1)):
        pairs = []
        for i in range(start, size - 1, 2):
            pairs += [(i, i + 1), (i + 1, i)]
        out.append(lax.ppermute(value, axis, pairs))
    return out


def local(
    velocity,
    stress,
    buoyancy,
    stiff_xx,
    stiff_xz,
    stiff_zz,
    shear_vert,
    shear_horiz,
    prestress,
    fault_mask,
    region_ids,
    inverse_rate,
    slip_prev,
    region_a,
    region_normal,
):
    ny, nx, width = buoyancy.shape
    across, along, dip = (lax.axis_index(k) for k in ("gx", "gy", "gz"))
    flags = jnp.stack([across, along % 2, dip % 2]).astype(jnp.int32)
    lanes = jnp.broadcast_to(jnp.arange(width, dtype=jnp.int32), (8, width))
    thirds, eighths = lanes // HALO, lanes // STRIP
    rows = nx + 2 * PAD
    high = 8 * ((ny + 1 + 7) // 8)
    v_shape = f32(3, 2, ny + 1, rows, width)
    s_shape = f32(6, 2, ny, rows, width)
    m_shape = f32(6, 2, ny, nx, width)
    fault_shape = f32(8, 2, high, width)
    planes = z_slots(ny, width)[1]
    z_shape = f32(planes, nx + 8, width)
    unit = ny * nx * width
    vm, hb, sm = in_vmem(), in_hbm(), in_smem()

    v, s, m, fault, z_a, z_b = call(
        load_kernel,
        "load",
        (v_shape, s_shape, m_shape, fault_shape, z_shape, z_shape),
        [sm, sm, sm, vm, vm, vm, vm, vm, vm] + [hb] * 8,
        {},
        [pltpu.SemaphoreType.DMA((15,))],
        flops=100 * unit,
    )(
        flags,
        region_a,
        region_normal,
        region_ids,
        fault_mask,
        inverse_rate,
        slip_prev,
        prestress,
        thirds,
        velocity,
        stress,
        buoyancy,
        stiff_xx,
        stiff_xz,
        stiff_zz,
        shear_vert,
        shear_horiz,
    )
    z_a, z_b = pair_swaps(z_a, z_b, "gz")
    y_shape = f32(5, nx + 8, width)
    v, s, m, fault, y_a, y_b = call(
        widen_kernel,
        "widen",
        (v_shape, s_shape, m_shape, fault_shape, y_shape, y_shape),
        [sm] + [vm] * 8,
        {5: 0, 6: 1, 7: 2, 8: 3},
        flops=50 * unit,
    )(flags, thirds, eighths, z_a, z_b, v, s, m, fault)
    y_shape = f32(4, nx, width)
    ahead_b = None
    for step in range(STEPS):
        first, final = step == 0, step == STEPS - 1
        y_a, y_b = pair_swaps(y_a, y_b, "gy")
        v, s = call(
            inner_kernel, "inner", (v_shape, s_shape), [vm] * 3, {1: 0, 0: 1}, flops=200 * unit
        )(s, v, m)
        f_shape = f32(5 if first else 4, high, width)
        scratch = [pltpu.VMEM((4, high, width), jnp.float32)]
        if first:
            v, fault, ahead_b, f_own = call(
                functools.partial(finish_kernel, True),
                "finish",
                (v_shape, fault_shape, f32(2, nx, width), f_shape),
                [sm] + [vm] * 7,
                {6: 0, 7: 1},
                scratch,
                flops=unit,
            )(flags, eighths, y_a, y_b, s, m, v, fault)
        else:
            v, f_own = call(
                functools.partial(finish_kernel, False),
                "finish",
                (v_shape, f_shape),
                [sm] + [vm] * 7,
                {6: 0},
                scratch,
                flops=unit,
            )(flags, eighths, y_a, y_b, s, m, v, ahead_b)
        f_other = lax.ppermute(f_own, "gx", [(i, i ^ 1) for i in range(lax.axis_size("gx"))])
        (s,) = call(rim_kernel, "rim", (s_shape,), [vm] * 3, {2: 0}, flops=50 * unit)(v, m, s)
        outs = [v_shape, s_shape, fault_shape]
        specs = [vm, vm, vm]
        scratch = [pltpu.VMEM((3, 2, high, width), jnp.float32)]
        if final:
            outs += [
                jax.ShapeDtypeStruct((3, ny, nx, width), jnp.float32),
                jax.ShapeDtypeStruct((6, ny, nx, width), jnp.float32),
                jax.ShapeDtypeStruct((ny, width), jnp.float32),
            ]
            specs += [hb, hb, vm]
            scratch.append(pltpu.SemaphoreType.DMA((9,)))
        else:
            outs += [y_shape, y_shape]
            specs += [vm, vm]
        v, s, fault, *more = call(
            functools.partial(fault_kernel, first, final),
            "fault",
            outs,
            [sm] + [vm] * 7,
            {5: 0, 6: 1, 7: 2},
            scratch,
            flops=50 * unit,
            out_specs=specs,
        )(flags, eighths, f_own, f_other, m, v, s, fault)
        if final:
            return tuple(more)
        y_a, y_b = more


def solution(mesh):
    in_specs = (
        P(None, "gy", "gx", "gz"),
        P(None, "gy", "gx", "gz"),
        P("gy", "gx", "gz"),
        P("gy", "gx", "gz"),
        P("gy", "gx", "gz"),
        P("gy", "gx", "gz"),
        P("gy", "gx", "gz"),
        P("gy", "gx", "gz"),
        P(None, "gy", "gz"),
        P("gy", "gz"),
        P("gy", "gz"),
        P("gy", "gz"),
        P("gy", "gz"),
        P(),
        P(),
    )
    out_specs = (P(None, "gy", "gx", "gz"), P(None, "gy", "gx", "gz"), P("gy", "gz"))
    return jax.shard_map(local, mesh=mesh, in_specs=in_specs, out_specs=out_specs, check_vma=False)
```

time: 174 us -> 81.2 us (0.47)
  the two profiles are of different devices: /device:TPU:0 before, /device:TPU:10 now
where the time goes in v1:
time: 81.2 us; the launch traced here: 80 us
  Pallas kernels  29.5 us (36%)
  starting transfers between devices  20.5 us (25%)
  waiting for transfers between devices  14.6 us (18%)
  local copies, waits for them, and re-layouts  14.3 us (18%)
  between operations  0.9 us (1%)
    ppermute x8, starting transfers between devices, pair_swaps(): out.append(lax.ppermute(value, axis, pairs))  15.7 us
    unnamed x30, local copies, waits for them, and re-layouts  14.3 us
    pallas_call x3, Pallas kernels, local(): call(inner_kernel, 'inner', (v_shape, s_shape), [vm] * 3, {1: 0, 0: 1}, f...  9.39 us
    ppermute x8, waiting for transfers between devices, pair_swaps(): out.append(lax.ppermute(value, axis, pairs))  9.02 us
    pallas_call x3, Pallas kernels, local(): call(functools.partial(fault_kernel, first, final), 'fault', outs, [sm] +...  7.77 us
    ppermute x3, waiting for transfers between devices, local(): lax.ppermute(f_own, 'gx', [(i, i ^ 1) for i in range(lax.axis_size('gx'))])  5.62 us
    ppermute x3, starting transfers between devices, local(): lax.ppermute(f_own, 'gx', [(i, i ^ 1) for i in range(lax.axis_size('gx'))])  4.78 us
    pallas_call x1, Pallas kernels, local(): call(load_kernel, 'load', (v_shape, s_shape, m_shape, fault_shape, z_shap...  4.46 us
  transfers between devices with their start and end apart: 11, of which 7 were waited for; matrix products, arithmetic and copies ran while one was open for 0% of the time, Pallas kernels for 14%

profile of v1, /device:TPU:10, one launch (start us, length us, event | category | flops | bytes accessed | tf_op | source)
XLA Modules:
  0.0 80.0 jit_solution(2237425280383287798)
XLA Ops:
  0.7 0.1 pad_add_fusion.flags
  0.8 0.0 copy-start
  0.8 1.9 %copy-done = f32[6,8,128,128]{3,2,1,0:T(8,128)S(1)} copy-done((f32[6,8,128,128]{3,2,1,0:T(8,128)S(1)}, f32[6,8,128,128]{3,2,1,0:T(8,128)}, u32[]{:S(2)}) %copy-start) | copy-done | bytes 3145752
  2.7 0.0 copy-start.1
  2.7 1.4 %copy-done.1 = f32[3,8,128,128]{3,2,1,0:T(8,128)S(1)} copy-done((f32[3,8,128,128]{3,2,1,0:T(8,128)S(1)}, f32[3,8,128,128]{3,2,1,0:T(8,128)}, u32[]{:S(2)}) %copy-start.1) | copy-done | bytes 1572888
  4.1 0.0 copy-start.2
  4.1 1.0 %copy-done.2 = f32[8,128,128]{2,1,0:T(8,128)S(1)} copy-done((f32[8,128,128]{2,1,0:T(8,128)S(1)}, f32[8,128,128]{2,1,0:T(8,128)}, u32[]{:S(2)}) %copy-start.2) | copy-done | bytes 524312
  5.1 0.0 copy-start.3
  5.1 1.0 %copy-done.3 = f32[8,128,128]{2,1,0:T(8,128)S(1)} copy-done((f32[8,128,128]{2,1,0:T(8,128)S(1)}, f32[8,128,128]{2,1,0:T(8,128)}, u32[]{:S(2)}) %copy-start.3) | copy-done | bytes 524312
  6.2 0.0 copy-start.4
  6.2 1.0 %copy-done.4 = f32[8,128,128]{2,1,0:T(8,128)S(1)} copy-done((f32[8,128,128]{2,1,0:T(8,128)S(1)}, f32[8,128,128]{2,1,0:T(8,128)}, u32[]{:S(2)}) %copy-start.4) | copy-done | bytes 524312
  7.2 0.0 copy-start.5
  7.2 1.0 %copy-done.5 = f32[8,128,128]{2,1,0:T(8,128)S(1)} copy-done((f32[8,128,128]{2,1,0:T(8,128)S(1)}, f32[8,128,128]{2,1,0:T(8,128)}, u32[]{:S(2)}) %copy-start.5) | copy-done | bytes 524312
  8.2 0.0 copy-start.6
  8.2 1.0 %copy-done.6 = f32[8,128,128]{2,1,0:T(8,128)S(1)} copy-done((f32[8,128,128]{2,1,0:T(8,128)S(1)}, f32[8,128,128]{2,1,0:T(8,128)}, u32[]{:S(2)}) %copy-start.6) | copy-done | bytes 524312
  9.3 1.0 %copy-done.7 = f32[8,128,128]{2,1,0:T(8,128)S(1)} copy-done((f32[8,128,128]{2,1,0:T(8,128)S(1)}, f32[8,128,128]{2,1,0:T(8,128)}, u32[]{:S(2)}) %copy-start.7) | copy-done | bytes 524312
  10.3 0.0 copy-start.8
  10.3 0.7 copy-done.8
  11.0 0.0 copy-start.9
  11.0 0.7 copy-done.9
  11.7 0.0 copy-start.10
  11.7 0.7 copy-done.10
  12.4 0.0 copy-start.11
  12.4 0.7 copy-done.11
  13.1 0.0 copy-start.12
  13.1 0.7 copy-done.12
  13.8 0.7 copy-done.13
  14.4 0.7 copy-done.14
  15.1 4.5 %load.1 = (f32[3,2,9,144,128]{4,3,2,1,0:T(8,128)S(1)}, f32[6,2,8,144,128]{4,3,2,1,0:T(8,128)S(1)}, f32[6,2,8,128,128]{4,3,2,1,0:T(8,128)S(1)}, f32[8,2,16,128]{3...) custom-call(s32[3]{0:T(128)S(1)} %pad_add_fusion.flags, f32[8]{0:T(128)S(1)} %copy-done.13, ...), custom_call_target="tpu_custom_call" | custom-call | flops 13107200 | tf_op jit(solution)/shard_map/load/pallas_call | solution.py:554
  19.5 0.1 collective-permute-start
  19.6 2.5 %collective-permute-start.1 = (f32[3,136,128]{2,1,0:T(8,128)S(1)}, f32[3,136,128]{2,1,0:T(8,128)S(1)}, u32[]{:S(2)}, u32[]{:S(2)}) collective-permute-start(f32[3,136,128]{2,1,0:T(8,128)S(1)} %get-tuple-element.43), channel_id=1, source_target_pairs={{1,2},{2,1},{5,6},{6,5},{9,10},{10,9},{13,14},{14,13},{17,18},{18,... | collective-permute-start | bytes 626696 | tf_op jit(solution)/shard_map/ppermute | solution.py:517
  22.2 0.0 collective-permute-done.r_a
  22.2 4.5 %collective-permute-done.1.r_b = f32[3,136,128]{2,1,0:T(8,128)S(1)} collective-permute-done((f32[3,136,128]{2,1,0:T(8,128)S(1)}, f32[3,136,128]{2,1,0:T(8,128)S(1)}, u32[]{:S(2)}, u32[]{:S(2)}) %collective-permute-start.1) | collective-permute-done | bytes 208928 | tf_op jit(solution)/shard_map/ppermute | solution.py:517
  26.7 4.0 %widen.1 = (f32[3,2,9,144,128]{4,3,2,1,0:T(8,128)S(1)}, f32[6,2,8,144,128]{4,3,2,1,0:T(8,128)S(1)}, f32[6,2,8,128,128]{4,3,2,1,0:T(8,128)S(1)}, f32[8,2,16,128]{...) custom-call(s32[3]{0:T(128)S(1)} %pad_add_fusion.flags, ...), custom_call_target="tpu_custom_call", output_to_operand_aliasing={{0}: (5, {}), {1}: (6, {}), {2}: (7, {}), {3}: (8, {})} | custom-call | flops 6553600 | tf_op jit(solution)/shard_map/widen/pallas_call | solution.py:583
  30.7 0.5 collective-permute-start.2
  31.2 4.6 %collective-permute-start.3 = (f32[5,136,128]{2,1,0:T(8,128)S(1)}, f32[5,136,128]{2,1,0:T(8,128)S(1)}, u32[]{:S(2)}, u32[]{:S(2)}) collective-permute-start(f32[5,136,128]{2,1,0:T(8,128)S(1)} %get-tuple-element.49), channel_id=1, source_target_pairs={{4,8},{8,4},{5,9},{9,5},{6,10},{10,6},{7,11},{11,7},{20,24},{24,20... | collective-permute-start | bytes 1044488 | tf_op jit(solution)/shard_map/ppermute | solution.py:517
  35.9 3.1 %inner.3 = (f32[3,2,9,144,128]{4,3,2,1,0:T(8,128)S(1)}, f32[6,2,8,144,128]{4,3,2,1,0:T(8,128)S(1)}) custom-call(f32[6,2,8,144,128]{4,3,2,1,0:T(8,128)S(1)} %get-tuple-element.50.s_in, f32[3,2,9,144,128]{4,3,2,1,0:T(8,128)S(1)} %get-tuple-element.51.v_in, f32[6,2,8,128,128]{4,3,2,1,0:T(8,128)S(1)} %get-tuple-element.52.m), custom_call_target="tpu_custom_call", output_to_operand_aliasing={{0}: (1, {}), {1}: (0, {})} | custom-call | flops 26214400 | tf_op jit(solution)/shard_map/inner/pallas_call | solution.py:596
  39.0 0.0 collective-permute-done.2.r_a
  39.0 2.1 %collective-permute-done.3.r_b = f32[5,136,128]{2,1,0:T(8,128)S(1)} collective-permute-done((f32[5,136,128]{2,1,0:T(8,128)S(1)}, f32[5,136,128]{2,1,0:T(8,128)S(1)}, u32[]{:S(2)}, u32[]{:S(2)}) %collective-permute-start.3) | collective-permute-done | bytes 348192 | tf_op jit(solution)/shard_map/ppermute | solution.py:517
  41.1 0.8 finish.3
  41.9 1.6 %collective-permute-start.4 = (f32[5,16,128]{2,1,0:T(8,128)S(1)}, f32[5,16,128]{2,1,0:T(8,128)S(1)}, u32[]{:S(2)}, u32[]{:S(2)}) collective-permute-start(f32[5,16,128]{2,1,0:T(8,128)S(1)} %get-tuple-element.56.f_own), channel_id=1, source_target_pairs={{0,16},{16,0},{1,17},{17,1},{2,18},{18,2},{3,19},{19,3},{4,20},{20... | collective-permute-start | bytes 122888 | tf_op jit(solution)/shard_map/ppermute | solution.py:621
  43.5 0.5 rim.3.rest_1_
  44.0 1.9 %collective-permute-done.4.f_other = f32[5,16,128]{2,1,0:T(8,128)S(1)} collective-permute-done((f32[5,16,128]{2,1,0:T(8,128)S(1)}, f32[5,16,128]{2,1,0:T(8,128)S(1)}, u32[]{:S(2)}, u32[]{:S(2)}) %collective-permute-start.4) | collective-permute-done | bytes 40992 | tf_op jit(solution)/shard_map/ppermute | solution.py:621
  46.0 1.8 %fault.3 = (f32[3,2,9,144,128]{4,3,2,1,0:T(8,128)S(1)}, f32[6,2,8,144,128]{4,3,2,1,0:T(8,128)S(1)}, f32[8,2,16,128]{3,2,1,0:T(8,128)S(1)}, f32[4,128,128]{2,1,0:T(8,128)S(1)}, f32[4,128,128]{2,1,0:T(8,128)S(1)}) custom-call(s32[3]{0:T(128)S(1)} %pad_add_fusion.flags, ...), custom_call_target="tpu_custom_call", output_to_operand_aliasing={{0}: (5, {}), {1}: (6, {}), {2}: (7, {})} | custom-call | flops 6553600 | tf_op jit(solution)/shard_map/fault/pallas_call | solution.py:637
  47.8 0.1 collective-permute-start.5
  47.9 3.9 %collective-permute-start.6 = (f32[4,128,128]{2,1,0:T(8,128)S(1)}, f32[4,128,128]{2,1,0:T(8,128)S(1)}, u32[]{:S(2)}, u32[]{:S(2)}) collective-permute-start(f32[4,128,128]{2,1,0:T(8,128)S(1)} %get-tuple-element.60), channel_id=1, source_target_pairs={{4,8},{8,4},{5,9},{9,5},{6,10},{10,6},{7,11},{11,7},{20,24},{24,20... | collective-permute-start | bytes 786440 | tf_op jit(solution)/shard_map/ppermute | solution.py:517
  51.8 3.1 %inner.4 = (f32[3,2,9,144,128]{4,3,2,1,0:T(8,128)S(1)}, f32[6,2,8,144,128]{4,3,2,1,0:T(8,128)S(1)}) custom-call(f32[6,2,8,144,128]{4,3,2,1,0:T(8,128)S(1)} %get-tuple-element.61.s_in, f32[3,2,9,144,128]{4,3,2,1,0:T(8,128)S(1)} %get-tuple-element.62.v_in, f32[6,2,8,128,128]{4,3,2,1,0:T(8,128)S(1)} %get-tuple-element.52.m), custom_call_target="tpu_custom_call", output_to_operand_aliasing={{0}: (1, {}), {1}: (0, {})} | custom-call | flops 26214400 | tf_op jit(solution)/shard_map/inner/pallas_call | solution.py:596
  54.9 0.0 collective-permute-done.5.r_a
  54.9 1.2 %collective-permute-done.6.r_b = f32[4,128,128]{2,1,0:T(8,128)S(1)} collective-permute-done((f32[4,128,128]{2,1,0:T(8,128)S(1)}, f32[4,128,128]{2,1,0:T(8,128)S(1)}, u32[]{:S(2)}, u32[]{:S(2)}) %collective-permute-start.6) | collective-permute-done | bytes 262176 | tf_op jit(solution)/shard_map/ppermute | solution.py:517
  56.1 0.8 finish.4
  56.9 1.6 %collective-permute-start.7 = (f32[4,16,128]{2,1,0:T(8,128)S(1)}, f32[4,16,128]{2,1,0:T(8,128)S(1)}, u32[]{:S(2)}, u32[]{:S(2)}) collective-permute-start(f32[4,16,128]{2,1,0:T(8,128)S(1)} %get-tuple-element.66.f_own), channel_id=1, source_target_pairs={{0,16},{16,0},{1,17},{17,1},{2,18},{18,2},{3,19},{19,3},{4,20},{20... | collective-permute-start | bytes 98312 | tf_op jit(solution)/shard_map/ppermute | solution.py:621
  58.5 0.5 rim.4.rest_1_
  59.0 1.8 %collective-permute-done.7.f_other = f32[4,16,128]{2,1,0:T(8,128)S(1)} collective-permute-done((f32[4,16,128]{2,1,0:T(8,128)S(1)}, f32[4,16,128]{2,1,0:T(8,128)S(1)}, u32[]{:S(2)}, u32[]{:S(2)}) %collective-permute-start.7) | collective-permute-done | bytes 32800 | tf_op jit(solution)/shard_map/ppermute | solution.py:621
  60.9 1.8 %fault.4 = (f32[3,2,9,144,128]{4,3,2,1,0:T(8,128)S(1)}, f32[6,2,8,144,128]{4,3,2,1,0:T(8,128)S(1)}, f32[8,2,16,128]{3,2,1,0:T(8,128)S(1)}, f32[4,128,128]{2,1,0:T(8,128)S(1)}, f32[4,128,128]{2,1,0:T(8,128)S(1)}) custom-call(s32[3]{0:T(128)S(1)} %pad_add_fusion.flags, ...), custom_call_target="tpu_custom_call", output_to_operand_aliasing={{0}: (5, {}), {1}: (6, {}), {2}: (7, {})} | custom-call | flops 6553600 | tf_op jit(solution)/shard_map/fault/pallas_call | solution.py:637
  62.7 0.1 collective-permute-start.8
  62.7 3.9 %collective-permute-start.9 = (f32[4,128,128]{2,1,0:T(8,128)S(1)}, f32[4,128,128]{2,1,0:T(8,128)S(1)}, u32[]{:S(2)}, u32[]{:S(2)}) collective-permute-start(f32[4,128,128]{2,1,0:T(8,128)S(1)} %get-tuple-element.70), channel_id=1, source_target_pairs={{4,8},{8,4},{5,9},{9,5},{6,10},{10,6},{7,11},{11,7},{20,24},{24,20... | collective-permute-start | bytes 786440 | tf_op jit(solution)/shard_map/ppermute | solution.py:517
  66.7 3.1 %inner.5 = (f32[3,2,9,144,128]{4,3,2,1,0:T(8,128)S(1)}, f32[6,2,8,144,128]{4,3,2,1,0:T(8,128)S(1)}) custom-call(f32[6,2,8,144,128]{4,3,2,1,0:T(8,128)S(1)} %get-tuple-element.71.s_in, f32[3,2,9,144,128]{4,3,2,1,0:T(8,128)S(1)} %get-tuple-element.72.v_in, f32[6,2,8,128,128]{4,3,2,1,0:T(8,128)S(1)} %get-tuple-element.52.m), custom_call_target="tpu_custom_call", output_to_operand_aliasing={{0}: (1, {}), {1}: (0, {})} | custom-call | flops 26214400 | tf_op jit(solution)/shard_map/inner/pallas_call | solution.py:596
  69.8 0.0 collective-permute-done.8.r_a
  69.8 1.2 %collective-permute-done.9.r_b = f32[4,128,128]{2,1,0:T(8,128)S(1)} collective-permute-done((f32[4,128,128]{2,1,0:T(8,128)S(1)}, f32[4,128,128]{2,1,0:T(8,128)S(1)}, u32[]{:S(2)}, u32[]{:S(2)}) %collective-permute-start.9) | collective-permute-done | bytes 262176 | tf_op jit(solution)/shard_map/ppermute | solution.py:517
  71.0 0.8 finish.5
  71.8 1.6 %collective-permute-start.10 = (f32[4,16,128]{2,1,0:T(8,128)S(1)}, f32[4,16,128]{2,1,0:T(8,128)S(1)}, u32[]{:S(2)}, u32[]{:S(2)}) collective-permute-start(f32[4,16,128]{2,1,0:T(8,128)S(1)} %get-tuple-element.75.f_own), channel_id=1, source_target_pairs={{0,16},{16,0},{1,17},{17,1},{2,18},{18,2},{3,19},{19,3},{4,20},{20... | collective-permute-start | bytes 98312 | tf_op jit(solution)/shard_map/ppermute | solution.py:621
  73.4 0.5 rim.5.rest_1_
  73.9 1.8 %collective-permute-done.10.f_other = f32[4,16,128]{2,1,0:T(8,128)S(1)} collective-permute-done((f32[4,16,128]{2,1,0:T(8,128)S(1)}, f32[4,16,128]{2,1,0:T(8,128)S(1)}, u32[]{:S(2)}, u32[]{:S(2)}) %collective-permute-start.10) | collective-permute-done | bytes 32800 | tf_op jit(solution)/shard_map/ppermute | solution.py:621
  75.8 4.2 %fault.5 = (f32[3,2,9,144,128]{4,3,2,1,0:T(8,128)S(1)}, f32[6,2,8,144,128]{4,3,2,1,0:T(8,128)S(1)}, f32[8,2,16,128]{3,2,1,0:T(8,128)S(1)}, f32[3,8,128,128]{3,2,...) custom-call(s32[3]{0:T(128)S(1)} %pad_add_fusion.flags, ...), custom_call_target="tpu_custom_call", output_to_operand_aliasing={{0}: (5, {}), {1}: (6, {}), {2}: (7, {})} | custom-call | flops 6553600 | tf_op jit(solution)/shard_map/fault/pallas_call | solution.py:637
  (9 shorter events, 0.0 us)
Async XLA Ops:
  0.8 1.9 %copy-start = (f32[6,8,128,128]{3,2,1,0:T(8,128)S(1)}, f32[6,8,128,128]{3,2,1,0:T(8,128)}, u32[]{:S(2)}) copy-start(f32[6,8,128,128]{3,2,1,0:T(8,128)} %stress.1) | copy-start | bytes 9437188
  2.7 1.4 %copy-start.1 = (f32[3,8,128,128]{3,2,1,0:T(8,128)S(1)}, f32[3,8,128,128]{3,2,1,0:T(8,128)}, u32[]{:S(2)}) copy-start(f32[3,8,128,128]{3,2,1,0:T(8,128)} %velocity.1) | copy-start | bytes 4718596
  4.1 1.0 %copy-start.2 = (f32[8,128,128]{2,1,0:T(8,128)S(1)}, f32[8,128,128]{2,1,0:T(8,128)}, u32[]{:S(2)}) copy-start(f32[8,128,128]{2,1,0:T(8,128)} %rest_0_.1) | copy-start | bytes 1572868
  5.1 1.0 %copy-start.3 = (f32[8,128,128]{2,1,0:T(8,128)S(1)}, f32[8,128,128]{2,1,0:T(8,128)}, u32[]{:S(2)}) copy-start(f32[8,128,128]{2,1,0:T(8,128)} %rest_1_.1) | copy-start | bytes 1572868
  6.2 1.0 %copy-start.4 = (f32[8,128,128]{2,1,0:T(8,128)S(1)}, f32[8,128,128]{2,1,0:T(8,128)}, u32[]{:S(2)}) copy-start(f32[8,128,128]{2,1,0:T(8,128)} %rest_2_.1) | copy-start | bytes 1572868
  7.2 1.0 %copy-start.5 = (f32[8,128,128]{2,1,0:T(8,128)S(1)}, f32[8,128,128]{2,1,0:T(8,128)}, u32[]{:S(2)}) copy-start(f32[8,128,128]{2,1,0:T(8,128)} %rest_3_.1) | copy-start | bytes 1572868
  8.2 1.0 %copy-start.6 = (f32[8,128,128]{2,1,0:T(8,128)S(1)}, f32[8,128,128]{2,1,0:T(8,128)}, u32[]{:S(2)}) copy-start(f32[8,128,128]{2,1,0:T(8,128)} %rest_4_.1) | copy-start | bytes 1572868
  9.3 1.0 %copy-start.7 = (f32[8,128,128]{2,1,0:T(8,128)S(1)}, f32[8,128,128]{2,1,0:T(8,128)}, u32[]{:S(2)}) copy-start(f32[8,128,128]{2,1,0:T(8,128)} %rest_5_.1) | copy-start | bytes 1572868
  10.3 0.7 copy-start.8
  11.0 0.7 copy-start.9
  11.7 0.7 copy-start.10
  12.4 0.7 copy-start.11
  13.1 0.7 copy-start.12
  13.8 0.7 copy-start.13
  14.4 0.7 copy-start.14
  19.5 2.7 %collective-permute-start = (f32[3,136,128]{2,1,0:T(8,128)S(1)}, f32[3,136,128]{2,1,0:T(8,128)S(1)}, u32[]{:S(2)}, u32[]{:S(2)}) collective-permute-start(f32[3,136,128]{2,1,0:T(8,128)S(1)} %get-tuple-element.42), channel_id=1, source_target_pairs={{0,1},{1,0},{2,3},{3,2},{4,5},{5,4},{6,7},{7,6},{8,9},{9,8},{10,11... | collective-permute-start | bytes 626696 | tf_op jit(solution)/shard_map/ppermute | solution.py:517
  19.6 7.1 %collective-permute-start.1 = (f32[3,136,128]{2,1,0:T(8,128)S(1)}, f32[3,136,128]{2,1,0:T(8,128)S(1)}, u32[]{:S(2)}, u32[]{:S(2)}) collective-permute-start(f32[3,136,128]{2,1,0:T(8,128)S(1)} %get-tuple-element.43), channel_id=1, source_target_pairs={{1,2},{2,1},{5,6},{6,5},{9,10},{10,9},{13,14},{14,13},{17,18},{18,... | collective-permute-start | bytes 626696 | tf_op jit(solution)/shard_map/ppermute | solution.py:517
  30.7 8.3 %collective-permute-start.2 = (f32[5,136,128]{2,1,0:T(8,128)S(1)}, f32[5,136,128]{2,1,0:T(8,128)S(1)}, u32[]{:S(2)}, u32[]{:S(2)}) collective-permute-start(f32[5,136,128]{2,1,0:T(8,128)S(1)} %get-tuple-element.48), channel_id=1, source_target_pairs={{0,4},{4,0},{8,12},{12,8},{1,5},{5,1},{9,13},{13,9},{2,6},{6,2},{1... | collective-permute-start | bytes 1044488 | tf_op jit(solution)/shard_map/ppermute | solution.py:517
  31.2 9.9 %collective-permute-start.3 = (f32[5,136,128]{2,1,0:T(8,128)S(1)}, f32[5,136,128]{2,1,0:T(8,128)S(1)}, u32[]{:S(2)}, u32[]{:S(2)}) collective-permute-start(f32[5,136,128]{2,1,0:T(8,128)S(1)} %get-tuple-element.49), channel_id=1, source_target_pairs={{4,8},{8,4},{5,9},{9,5},{6,10},{10,6},{7,11},{11,7},{20,24},{24,20... | collective-permute-start | bytes 1044488 | tf_op jit(solution)/shard_map/ppermute | solution.py:517
  41.9 4.1 %collective-permute-start.4 = (f32[5,16,128]{2,1,0:T(8,128)S(1)}, f32[5,16,128]{2,1,0:T(8,128)S(1)}, u32[]{:S(2)}, u32[]{:S(2)}) collective-permute-start(f32[5,16,128]{2,1,0:T(8,128)S(1)} %get-tuple-element.56.f_own), channel_id=1, source_target_pairs={{0,16},{16,0},{1,17},{17,1},{2,18},{18,2},{3,19},{19,3},{4,20},{20... | collective-permute-start | bytes 122888 | tf_op jit(solution)/shard_map/ppermute | solution.py:621
  47.8 7.2 %collective-permute-start.5 = (f32[4,128,128]{2,1,0:T(8,128)S(1)}, f32[4,128,128]{2,1,0:T(8,128)S(1)}, u32[]{:S(2)}, u32[]{:S(2)}) collective-permute-start(f32[4,128,128]{2,1,0:T(8,128)S(1)} %get-tuple-element.59), channel_id=1, source_target_pairs={{0,4},{4,0},{8,12},{12,8},{1,5},{5,1},{9,13},{13,9},{2,6},{6,2},{1... | collective-permute-start | bytes 786440 | tf_op jit(solution)/shard_map/ppermute | solution.py:517
  47.9 8.3 %collective-permute-start.6 = (f32[4,128,128]{2,1,0:T(8,128)S(1)}, f32[4,128,128]{2,1,0:T(8,128)S(1)}, u32[]{:S(2)}, u32[]{:S(2)}) collective-permute-start(f32[4,128,128]{2,1,0:T(8,128)S(1)} %get-tuple-element.60), channel_id=1, source_target_pairs={{4,8},{8,4},{5,9},{9,5},{6,10},{10,6},{7,11},{11,7},{20,24},{24,20... | collective-permute-start | bytes 786440 | tf_op jit(solution)/shard_map/ppermute | solution.py:517
  56.9 4.0 %collective-permute-start.7 = (f32[4,16,128]{2,1,0:T(8,128)S(1)}, f32[4,16,128]{2,1,0:T(8,128)S(1)}, u32[]{:S(2)}, u32[]{:S(2)}) collective-permute-start(f32[4,16,128]{2,1,0:T(8,128)S(1)} %get-tuple-element.66.f_own), channel_id=1, source_target_pairs={{0,16},{16,0},{1,17},{17,1},{2,18},{18,2},{3,19},{19,3},{4,20},{20... | collective-permute-start | bytes 98312 | tf_op jit(solution)/shard_map/ppermute | solution.py:621
  62.7 7.2 %collective-permute-start.8 = (f32[4,128,128]{2,1,0:T(8,128)S(1)}, f32[4,128,128]{2,1,0:T(8,128)S(1)}, u32[]{:S(2)}, u32[]{:S(2)}) collective-permute-start(f32[4,128,128]{2,1,0:T(8,128)S(1)} %get-tuple-element.69), channel_id=1, source_target_pairs={{0,4},{4,0},{8,12},{12,8},{1,5},{5,1},{9,13},{13,9},{2,6},{6,2},{1... | collective-permute-start | bytes 786440 | tf_op jit(solution)/shard_map/ppermute | solution.py:517
  62.7 8.3 %collective-permute-start.9 = (f32[4,128,128]{2,1,0:T(8,128)S(1)}, f32[4,128,128]{2,1,0:T(8,128)S(1)}, u32[]{:S(2)}, u32[]{:S(2)}) collective-permute-start(f32[4,128,128]{2,1,0:T(8,128)S(1)} %get-tuple-element.70), channel_id=1, source_target_pairs={{4,8},{8,4},{5,9},{9,5},{6,10},{10,6},{7,11},{11,7},{20,24},{24,20... | collective-permute-start | bytes 786440 | tf_op jit(solution)/shard_map/ppermute | solution.py:517
  71.8 4.0 %collective-permute-start.10 = (f32[4,16,128]{2,1,0:T(8,128)S(1)}, f32[4,16,128]{2,1,0:T(8,128)S(1)}, u32[]{:S(2)}, u32[]{:S(2)}) collective-permute-start(f32[4,16,128]{2,1,0:T(8,128)S(1)} %get-tuple-element.75.f_own), channel_id=1, source_target_pairs={{0,16},{16,0},{1,17},{17,1},{2,18},{18,2},{3,19},{19,3},{4,20},{20... | collective-permute-start | bytes 98312 | tf_op jit(solution)/shard_map/ppermute | solution.py:621

commit v2 on v1

--- a/solution.py
+++ b/solution.py
@@ -123,46 +123,48 @@
     return {"v": v, "s": s, "m": m}[kind]
 
 
-def slot_of(index, width):
-    per_plane = (width - 5) // HALO
-    return index // per_plane, index % per_plane
+def fields_per_plane(ny, width):
+    return (width - 5) // HALO // ny
 
 
 def z_slots(ny, width):
+    per_plane = fields_per_plane(ny, width)
     slots = {}
     for f in range(len(FIELDS)):
         for y in range(ny):
-            slots[f, y] = slot_of(f * ny + y, width)
-    return slots, 1 + max(p for p, _ in slots.values())
+            slots[f, y] = (f // per_plane, f % per_plane * ny + y)
+    return slots, -(-len(FIELDS) // per_plane)
 
 
 def load_kernel(
     flags,
-    region_a,
-    region_normal,
-    ids,
-    mask,
-    inverse_rate,
-    slip,
-    prestress,
     thirds,
     velocity,
     stress,
     *rest,
 ):
-    raw_m = rest[:6]
-    v, s, m, fault, z_a, z_b = rest[6:12]
-    sems = rest[12]
+    raw_m, small = rest[:6], rest[6:13]
+    v, s, m, fault, z_a, z_b = rest[13:19]
+    pre, ids, mask, rate, slip, region_a, region_normal, sems = rest[19:]
     ny, nx, width = velocity.shape[1:]
-    copies = []
+    big = {}
     for c in range(3):
-        copies.append((velocity.at[c], v.at[c, 0, pl.ds(0, ny), pl.ds(PAD, nx), :]))
+        big["v", c] = (velocity.at[c], v.at[c, 0, pl.ds(0, ny), pl.ds(PAD, nx), :])
     for c in range(6):
-        copies.append((stress.at[c], s.at[c, 0, :, pl.ds(PAD, nx), :]))
+        big["s", c] = (stress.at[c], s.at[c, 0, :, pl.ds(PAD, nx), :])
     for c in range(6):
-        copies.append((raw_m[c], m.at[c, 0]))
-    copies = [pltpu.make_async_copy(a, b, sems.at[k]) for k, (a, b) in enumerate(copies)]
-    for copy in copies:
+        big["m", c] = (raw_m[c], m.at[c, 0])
+    big = {
+        key: pltpu.make_async_copy(a, b, sems.at[k]) for k, (key, (a, b)) in enumerate(big.items())
+    }
+    held = (pre, ids, mask, rate, slip, region_a, region_normal)
+    little = [
+        pltpu.make_async_copy(a, b, sems.at[len(big) + k])
+        for k, (a, b) in enumerate(zip(small, held))
+    ]
+    for copy in big.values():
+        copy.start()
+    for copy in little:
         copy.start()
     zeros = jnp.zeros((PAD, width), jnp.float32)
     for t in range(2):
@@ -171,49 +173,57 @@
                 s[c, t, y, 0:PAD, :] = zeros
             for c in range(3):
                 v[c, t, y, PAD + nx : PAD + nx + PAD, :] = zeros
+
+    slots, planes = z_slots(ny, width)
+    odd = flags[2] == 1
+    per_plane = fields_per_plane(ny, width)
+
+    def emit(pieces, plane, row):
+        group = thirds[...]
+        up = jnp.zeros((8, width), jnp.float32)
+        down = jnp.zeros((8, width), jnp.float32)
+        for pos, piece in pieces:
+            moved = roll(piece, HALO * pos + HALO)
+            up = jnp.where(group == pos, moved, up)
+            down = jnp.where(group == pos + 1, moved, down)
+        z_a[plane, pl.ds(row, 8), :] = jnp.where(odd, down, up)
+        z_b[plane, pl.ds(row, 8), :] = jnp.where(odd, up, down)
+
+    for plane in range(planes):
+        chosen = FIELDS[plane * per_plane : (plane + 1) * per_plane]
+        for key in chosen:
+            big[key].wait()
+
+        def pack(i, carry, plane=plane, chosen=chosen):
+            row = pl.multiple_of(i * 8, 8)
+            pieces = []
+            for f, (kind, c) in enumerate(chosen):
+                shift = 0 if kind == "m" else PAD
+                ref = field_ref(kind, v, s, m)
+                for y in range(ny):
+                    pieces.append((f * ny + y, ref[c, 0, y, pl.ds(row + shift, 8), :]))
+            emit(pieces, plane, row)
+            return carry
+
+        lax.fori_loop(0, nx // 8, pack, 0)
+    for copy in little:
+        copy.wait()
     kinds = ids[...]
     a_part = jnp.zeros((ny, width), jnp.float32)
     n_part = jnp.zeros((ny, width), jnp.float32)
     for k in range(region_a.shape[0]):
         a_part = jnp.where(kinds == k, region_a[k], a_part)
         n_part = jnp.where(kinds == k, region_normal[k], n_part)
-    fault[PRE_Y, 0, 0:ny, :] = prestress[0]
-    fault[PRE_Z, 0, 0:ny, :] = prestress[1]
+    fault[PRE_Y, 0, 0:ny, :] = pre[0]
+    fault[PRE_Z, 0, 0:ny, :] = pre[1]
     fault[MASK, 0, 0:ny, :] = mask[...].astype(jnp.float32)
     fault[STRENGTH, 0, 0:ny, :] = a_part * n_part
-    fault[RATE, 0, 0:ny, :] = inverse_rate[...]
+    fault[RATE, 0, 0:ny, :] = rate[...]
     fault[SLIP, 0, 0:ny, :] = slip[...]
-    for copy in copies:
-        copy.wait()
-
-    slots, planes = z_slots(ny, width)
-    odd = flags[2] == 1
-
-    def emit(pieces, row):
-        group = thirds[...]
-        up = [jnp.zeros((8, width), jnp.float32) for _ in range(planes)]
-        down = [jnp.zeros((8, width), jnp.float32) for _ in range(planes)]
-        for plane, pos, piece in pieces:
-            moved = roll(piece, HALO * pos + HALO)
-            up[plane] = jnp.where(group == pos, moved, up[plane])
-            down[plane] = jnp.where(group == pos + 1, moved, down[plane])
-        for plane in range(planes):
-            z_a[plane, pl.ds(row, 8), :] = jnp.where(odd, down[plane], up[plane])
-            z_b[plane, pl.ds(row, 8), :] = jnp.where(odd, up[plane], down[plane])
-
-    def pack(i, carry):
-        row = pl.multiple_of(i * 8, 8)
-        pieces = []
-        for f, (kind, c) in enumerate(FIELDS):
-            shift = 0 if kind == "m" else PAD
-            for y in range(ny):
-                ref = field_ref(kind, v, s, m)
-                pieces.append((*slots[f, y], ref[c, 0, y, pl.ds(row + shift, 8), :]))
-        emit(pieces, row)
-        return carry
-
-    lax.fori_loop(0, nx // 8, pack, 0)
-    emit([(0, k, fault[k, 0, 0:8, :]) for k in range(6)], nx)
+    emit([(k, fault[k, 0, 0:8, :]) for k in range(6)], 0, nx)
+    for plane in range(1, planes):
+        z_a[plane, pl.ds(nx, 8), :] = zeros
+        z_b[plane, pl.ds(nx, 8), :] = zeros
 
 
 def write_messages(v, s, eighths, odd, row, y_a, y_b, extra):
@@ -551,33 +561,27 @@
     unit = ny * nx * width
     vm, hb, sm = in_vmem(), in_hbm(), in_smem()
 
+    raw = [velocity, stress, buoyancy, stiff_xx, stiff_xz, stiff_zz, shear_vert, shear_horiz]
+    raw += [prestress, region_ids, fault_mask, inverse_rate, slip_prev, region_a, region_normal]
+    raw = [pltpu.with_memory_space_constraint(k, HBM) for k in raw]
     v, s, m, fault, z_a, z_b = call(
         load_kernel,
         "load",
         (v_shape, s_shape, m_shape, fault_shape, z_shape, z_shape),
-        [sm, sm, sm, vm, vm, vm, vm, vm, vm] + [hb] * 8,
+        [sm, vm] + [hb] * 15,
         {},
-        [pltpu.SemaphoreType.DMA((15,))],
+        [
+            pltpu.VMEM(prestress.shape, jnp.float32),
+            pltpu.VMEM(region_ids.shape, jnp.int32),
+            pltpu.VMEM(fault_mask.shape, jnp.int32),
+            pltpu.VMEM(inverse_rate.shape, jnp.float32),
+            pltpu.VMEM(slip_prev.shape, jnp.float32),
+            pltpu.SMEM(region_a.shape, jnp.float32),
+            pltpu.SMEM(region_normal.shape, jnp.float32),
+            pltpu.SemaphoreType.DMA((22,)),
+        ],
         flops=100 * unit,
-    )(
-        flags,
-        region_a,
-        region_normal,
-        region_ids,
-        fault_mask,
-        inverse_rate,
-        slip_prev,
-        prestress,
-        thirds,
-        velocity,
-        stress,
-        buoyancy,
-        stiff_xx,
-        stiff_xz,
-        stiff_zz,
-        shear_vert,
-        shear_horiz,
-    )
+    )(flags, thirds, *raw)
     z_a, z_b = pair_swaps(z_a, z_b, "gz")
     y_shape = f32(5, nx + 8, width)
     v, s, m, fault, y_a, y_b = call(

time: 81.2 us -> 69.7 us (0.86)
  local copies, waits for them, and re-layouts: 14.3 us -> 0 us
  Pallas kernels: 29.5 us -> 33.4 us
    unnamed x30 -> x0, local copies, waits for them, and re-layouts: 14.3 us -> none
    pallas_call x1, Pallas kernels: 4.46 us -> 7.83 us  [local(): call(load_kernel, 'load', (v_shape, s_shape, m_shape, fault_shape, z_shap...]
  transfers between devices with their start and end apart: 11 -> 11, of which waited for: 7 -> 7; matrix products, arithmetic and copies ran while one was open for 0% -> 0% of each run, Pallas kernels for 14% -> 17%
where the time goes in v2:
time: 69.7 us; the launch traced here: 69 us
  Pallas kernels  33.4 us (48%)
  starting transfers between devices  20.5 us (29%)
  waiting for transfers between devices  14.1 us (20%)
  between operations  0.88 us (1%)
    ppermute x8, starting transfers between devices, pair_swaps(): out.append(lax.ppermute(value, axis, pairs))  15.7 us
    pallas_call x3, Pallas kernels, local(): call(inner_kernel, 'inner', (v_shape, s_shape), [vm] * 3, {1: 0, 0: 1}, f...  9.83 us
    ppermute x8, waiting for transfers between devices, pair_swaps(): out.append(lax.ppermute(value, axis, pairs))  8.58 us
    pallas_call x1, Pallas kernels, local(): call(load_kernel, 'load', (v_shape, s_shape, m_shape, fault_shape, z_shap...  7.83 us
    pallas_call x3, Pallas kernels, local(): call(functools.partial(fault_kernel, first, final), 'fault', outs, [sm] +...  7.78 us
    ppermute x3, waiting for transfers between devices, local(): lax.ppermute(f_own, 'gx', [(i, i ^ 1) for i in range(lax.axis_size('gx'))])  5.56 us
    ppermute x3, starting transfers between devices, local(): lax.ppermute(f_own, 'gx', [(i, i ^ 1) for i in range(lax.axis_size('gx'))])  4.78 us
    pallas_call x1, Pallas kernels, local(): call(widen_kernel, 'widen', (v_shape, s_shape, m_shape, fault_shape, y_sh...  3.98 us
  transfers between devices with their start and end apart: 11, of which 7 were waited for; matrix products, arithmetic and copies ran while one was open for 0% of the time, Pallas kernels for 17%

profile of v2, /device:TPU:10, one launch (start us, length us, event | category | flops | bytes accessed | tf_op | source)
XLA Modules:
  0.0 69.0 jit_solution(11961618514297394637)
XLA Ops:
  0.7 0.1 pad_add_fusion.flags
  0.8 7.8 %load.1 = (f32[3,2,9,144,128]{4,3,2,1,0:T(8,128)S(1)}, f32[6,2,8,144,128]{4,3,2,1,0:T(8,128)S(1)}, f32[6,2,8,128,128]{4,3,2,1,0:T(8,128)S(1)}, f32[8,2,16,128]{3...) custom-call(s32[3]{0:T(128)S(1)} %pad_add_fusion.flags, ...), custom_call_target="tpu_custom_call" | custom-call | flops 13107200 | tf_op jit(solution)/shard_map/load/pallas_call | solution.py:567
  8.6 0.1 collective-permute-start
  8.7 2.5 %collective-permute-start.1 = (f32[3,136,128]{2,1,0:T(8,128)S(1)}, f32[3,136,128]{2,1,0:T(8,128)S(1)}, u32[]{:S(2)}, u32[]{:S(2)}) collective-permute-start(f32[3,136,128]{2,1,0:T(8,128)S(1)} %get-tuple-element.43), channel_id=1, source_target_pairs={{1,2},{2,1},{5,6},{6,5},{9,10},{10,9},{13,14},{14,13},{17,18},{18,... | collective-permute-start | bytes 626696 | tf_op jit(solution)/shard_map/ppermute | solution.py:527
  11.3 0.0 collective-permute-done.r_a
  11.3 4.5 %collective-permute-done.1.r_b = f32[3,136,128]{2,1,0:T(8,128)S(1)} collective-permute-done((f32[3,136,128]{2,1,0:T(8,128)S(1)}, f32[3,136,128]{2,1,0:T(8,128)S(1)}, u32[]{:S(2)}, u32[]{:S(2)}) %collective-permute-start.1) | collective-permute-done | bytes 208928 | tf_op jit(solution)/shard_map/ppermute | solution.py:527
  15.8 4.0 %widen.1 = (f32[3,2,9,144,128]{4,3,2,1,0:T(8,128)S(1)}, f32[6,2,8,144,128]{4,3,2,1,0:T(8,128)S(1)}, f32[6,2,8,128,128]{4,3,2,1,0:T(8,128)S(1)}, f32[8,2,16,128]{...) custom-call(s32[3]{0:T(128)S(1)} %pad_add_fusion.flags, ...), custom_call_target="tpu_custom_call", output_to_operand_aliasing={{0}: (5, {}), {1}: (6, {}), {2}: (7, {}), {3}: (8, {})} | custom-call | flops 6553600 | tf_op jit(solution)/shard_map/widen/pallas_call | solution.py:587
  19.8 0.5 collective-permute-start.2
  20.3 4.6 %collective-permute-start.3 = (f32[5,136,128]{2,1,0:T(8,128)S(1)}, f32[5,136,128]{2,1,0:T(8,128)S(1)}, u32[]{:S(2)}, u32[]{:S(2)}) collective-permute-start(f32[5,136,128]{2,1,0:T(8,128)S(1)} %get-tuple-element.49), channel_id=1, source_target_pairs={{4,8},{8,4},{5,9},{9,5},{6,10},{10,6},{7,11},{11,7},{20,24},{24,20... | collective-permute-start | bytes 1044488 | tf_op jit(solution)/shard_map/ppermute | solution.py:527
  24.9 3.3 %inner.3 = (f32[3,2,9,144,128]{4,3,2,1,0:T(8,128)S(1)}, f32[6,2,8,144,128]{4,3,2,1,0:T(8,128)S(1)}) custom-call(f32[6,2,8,144,128]{4,3,2,1,0:T(8,128)S(1)} %get-tuple-element.50.s_in, f32[3,2,9,144,128]{4,3,2,1,0:T(8,128)S(1)} %get-tuple-element.51.v_in, f32[6,2,8,128,128]{4,3,2,1,0:T(8,128)S(1)} %get-tuple-element.52.m), custom_call_target="tpu_custom_call", output_to_operand_aliasing={{0}: (1, {}), {1}: (0, {})} | custom-call | flops 26214400 | tf_op jit(solution)/shard_map/inner/pallas_call | solution.py:600
  28.2 0.0 collective-permute-done.2.r_a
  28.2 2.0 %collective-permute-done.3.r_b = f32[5,136,128]{2,1,0:T(8,128)S(1)} collective-permute-done((f32[5,136,128]{2,1,0:T(8,128)S(1)}, f32[5,136,128]{2,1,0:T(8,128)S(1)}, u32[]{:S(2)}, u32[]{:S(2)}) %collective-permute-start.3) | collective-permute-done | bytes 348192 | tf_op jit(solution)/shard_map/ppermute | solution.py:527
  30.2 0.8 %finish.3 = (f32[3,2,9,144,128]{4,3,2,1,0:T(8,128)S(1)}, f32[8,2,16,128]{3,2,1,0:T(8,128)S(1)}, f32[2,128,128]{2,1,0:T(8,128)S(1)}, f32[5,16,128]{2,1,0:T(8,128)S(1)}) custom-call(s32[3]{0:T(128)S(1)} %pad_add_fusion.flags, s32[8,128]{1,0:T(8,128)S(1)} %broadcast_select_fusion.1.eighths, ...), custom_call_target="tpu_custom_call", output_to_operand_aliasing={{0}: (6, {}), {1}: (7, {})} | custom-call | flops 131072 | tf_op jit(solution)/shard_map/finish/pallas_call | solution.py:606
  31.0 1.6 %collective-permute-start.4 = (f32[5,16,128]{2,1,0:T(8,128)S(1)}, f32[5,16,128]{2,1,0:T(8,128)S(1)}, u32[]{:S(2)}, u32[]{:S(2)}) collective-permute-start(f32[5,16,128]{2,1,0:T(8,128)S(1)} %get-tuple-element.56.f_own), channel_id=1, source_target_pairs={{0,16},{16,0},{1,17},{17,1},{2,18},{18,2},{3,19},{19,3},{4,20},{20... | collective-permute-start | bytes 122888 | tf_op jit(solution)/shard_map/ppermute | solution.py:625
  32.6 0.6 rim.3.rest_1_
  33.1 1.9 %collective-permute-done.4.f_other = f32[5,16,128]{2,1,0:T(8,128)S(1)} collective-permute-done((f32[5,16,128]{2,1,0:T(8,128)S(1)}, f32[5,16,128]{2,1,0:T(8,128)S(1)}, u32[]{:S(2)}, u32[]{:S(2)}) %collective-permute-start.4) | collective-permute-done | bytes 40992 | tf_op jit(solution)/shard_map/ppermute | solution.py:625
  35.0 1.8 %fault.3 = (f32[3,2,9,144,128]{4,3,2,1,0:T(8,128)S(1)}, f32[6,2,8,144,128]{4,3,2,1,0:T(8,128)S(1)}, f32[8,2,16,128]{3,2,1,0:T(8,128)S(1)}, f32[4,128,128]{2,1,0:T(8,128)S(1)}, f32[4,128,128]{2,1,0:T(8,128)S(1)}) custom-call(s32[3]{0:T(128)S(1)} %pad_add_fusion.flags, ...), custom_call_target="tpu_custom_call", output_to_operand_aliasing={{0}: (5, {}), {1}: (6, {}), {2}: (7, {})} | custom-call | flops 6553600 | tf_op jit(solution)/shard_map/fault/pallas_call | solution.py:641
  36.8 0.1 collective-permute-start.5
  36.9 3.9 %collective-permute-start.6 = (f32[4,128,128]{2,1,0:T(8,128)S(1)}, f32[4,128,128]{2,1,0:T(8,128)S(1)}, u32[]{:S(2)}, u32[]{:S(2)}) collective-permute-start(f32[4,128,128]{2,1,0:T(8,128)S(1)} %get-tuple-element.60), channel_id=1, source_target_pairs={{4,8},{8,4},{5,9},{9,5},{6,10},{10,6},{7,11},{11,7},{20,24},{24,20... | collective-permute-start | bytes 786440 | tf_op jit(solution)/shard_map/ppermute | solution.py:527
  40.8 3.3 %inner.4 = (f32[3,2,9,144,128]{4,3,2,1,0:T(8,128)S(1)}, f32[6,2,8,144,128]{4,3,2,1,0:T(8,128)S(1)}) custom-call(f32[6,2,8,144,128]{4,3,2,1,0:T(8,128)S(1)} %get-tuple-element.61.s_in, f32[3,2,9,144,128]{4,3,2,1,0:T(8,128)S(1)} %get-tuple-element.62.v_in, f32[6,2,8,128,128]{4,3,2,1,0:T(8,128)S(1)} %get-tuple-element.52.m), custom_call_target="tpu_custom_call", output_to_operand_aliasing={{0}: (1, {}), {1}: (0, {})} | custom-call | flops 26214400 | tf_op jit(solution)/shard_map/inner/pallas_call | solution.py:600
  44.1 0.0 collective-permute-done.5.r_a
  44.1 1.0 %collective-permute-done.6.r_b = f32[4,128,128]{2,1,0:T(8,128)S(1)} collective-permute-done((f32[4,128,128]{2,1,0:T(8,128)S(1)}, f32[4,128,128]{2,1,0:T(8,128)S(1)}, u32[]{:S(2)}, u32[]{:S(2)}) %collective-permute-start.6) | collective-permute-done | bytes 262176 | tf_op jit(solution)/shard_map/ppermute | solution.py:527
  45.2 0.8 %finish.4 = (f32[3,2,9,144,128]{4,3,2,1,0:T(8,128)S(1)}, f32[4,16,128]{2,1,0:T(8,128)S(1)}) custom-call(s32[3]{0:T(128)S(1)} %pad_add_fusion.flags, s32[8,128]{1,0:T(8,128)S(1)} %broadcast_select_fusion.1.eighths, f32[4,128,128]{2,1,0:T(8,128)S(1)} %collective-permute-done.5.r_a, ...), custom_call_target="tpu_custom_call", output_to_operand_aliasing={{0}: (6, {})} | custom-call | flops 131072 | tf_op jit(solution)/shard_map/finish/pallas_call | solution.py:616
  45.9 1.6 %collective-permute-start.7 = (f32[4,16,128]{2,1,0:T(8,128)S(1)}, f32[4,16,128]{2,1,0:T(8,128)S(1)}, u32[]{:S(2)}, u32[]{:S(2)}) collective-permute-start(f32[4,16,128]{2,1,0:T(8,128)S(1)} %get-tuple-element.66.f_own), channel_id=1, source_target_pairs={{0,16},{16,0},{1,17},{17,1},{2,18},{18,2},{3,19},{19,3},{4,20},{20... | collective-permute-start | bytes 98312 | tf_op jit(solution)/shard_map/ppermute | solution.py:625
  47.5 0.6 rim.4.rest_1_
  48.1 1.8 %collective-permute-done.7.f_other = f32[4,16,128]{2,1,0:T(8,128)S(1)} collective-permute-done((f32[4,16,128]{2,1,0:T(8,128)S(1)}, f32[4,16,128]{2,1,0:T(8,128)S(1)}, u32[]{:S(2)}, u32[]{:S(2)}) %collective-permute-start.7) | collective-permute-done | bytes 32800 | tf_op jit(solution)/shard_map/ppermute | solution.py:625
  49.9 1.8 %fault.4 = (f32[3,2,9,144,128]{4,3,2,1,0:T(8,128)S(1)}, f32[6,2,8,144,128]{4,3,2,1,0:T(8,128)S(1)}, f32[8,2,16,128]{3,2,1,0:T(8,128)S(1)}, f32[4,128,128]{2,1,0:T(8,128)S(1)}, f32[4,128,128]{2,1,0:T(8,128)S(1)}) custom-call(s32[3]{0:T(128)S(1)} %pad_add_fusion.flags, ...), custom_call_target="tpu_custom_call", output_to_operand_aliasing={{0}: (5, {}), {1}: (6, {}), {2}: (7, {})} | custom-call | flops 6553600 | tf_op jit(solution)/shard_map/fault/pallas_call | solution.py:641
  51.7 0.1 collective-permute-start.8
  51.8 3.9 %collective-permute-start.9 = (f32[4,128,128]{2,1,0:T(8,128)S(1)}, f32[4,128,128]{2,1,0:T(8,128)S(1)}, u32[]{:S(2)}, u32[]{:S(2)}) collective-permute-start(f32[4,128,128]{2,1,0:T(8,128)S(1)} %get-tuple-element.70), channel_id=1, source_target_pairs={{4,8},{8,4},{5,9},{9,5},{6,10},{10,6},{7,11},{11,7},{20,24},{24,20... | collective-permute-start | bytes 786440 | tf_op jit(solution)/shard_map/ppermute | solution.py:527
  55.7 3.3 %inner.5 = (f32[3,2,9,144,128]{4,3,2,1,0:T(8,128)S(1)}, f32[6,2,8,144,128]{4,3,2,1,0:T(8,128)S(1)}) custom-call(f32[6,2,8,144,128]{4,3,2,1,0:T(8,128)S(1)} %get-tuple-element.71.s_in, f32[3,2,9,144,128]{4,3,2,1,0:T(8,128)S(1)} %get-tuple-element.72.v_in, f32[6,2,8,128,128]{4,3,2,1,0:T(8,128)S(1)} %get-tuple-element.52.m), custom_call_target="tpu_custom_call", output_to_operand_aliasing={{0}: (1, {}), {1}: (0, {})} | custom-call | flops 26214400 | tf_op jit(solution)/shard_map/inner/pallas_call | solution.py:600
  59.0 0.0 collective-permute-done.8.r_a
  59.0 1.0 %collective-permute-done.9.r_b = f32[4,128,128]{2,1,0:T(8,128)S(1)} collective-permute-done((f32[4,128,128]{2,1,0:T(8,128)S(1)}, f32[4,128,128]{2,1,0:T(8,128)S(1)}, u32[]{:S(2)}, u32[]{:S(2)}) %collective-permute-start.9) | collective-permute-done | bytes 262176 | tf_op jit(solution)/shard_map/ppermute | solution.py:527
  60.1 0.8 %finish.5 = (f32[3,2,9,144,128]{4,3,2,1,0:T(8,128)S(1)}, f32[4,16,128]{2,1,0:T(8,128)S(1)}) custom-call(s32[3]{0:T(128)S(1)} %pad_add_fusion.flags, s32[8,128]{1,0:T(8,128)S(1)} %broadcast_select_fusion.1.eighths, f32[4,128,128]{2,1,0:T(8,128)S(1)} %collective-permute-done.8.r_a, ...), custom_call_target="tpu_custom_call", output_to_operand_aliasing={{0}: (6, {})} | custom-call | flops 131072 | tf_op jit(solution)/shard_map/finish/pallas_call | solution.py:616
  60.8 1.6 %collective-permute-start.10 = (f32[4,16,128]{2,1,0:T(8,128)S(1)}, f32[4,16,128]{2,1,0:T(8,128)S(1)}, u32[]{:S(2)}, u32[]{:S(2)}) collective-permute-start(f32[4,16,128]{2,1,0:T(8,128)S(1)} %get-tuple-element.75.f_own), channel_id=1, source_target_pairs={{0,16},{16,0},{1,17},{17,1},{2,18},{18,2},{3,19},{19,3},{4,20},{20... | collective-permute-start | bytes 98312 | tf_op jit(solution)/shard_map/ppermute | solution.py:625
  62.4 0.6 rim.5.rest_1_
  63.0 1.8 %collective-permute-done.10.f_other = f32[4,16,128]{2,1,0:T(8,128)S(1)} collective-permute-done((f32[4,16,128]{2,1,0:T(8,128)S(1)}, f32[4,16,128]{2,1,0:T(8,128)S(1)}, u32[]{:S(2)}, u32[]{:S(2)}) %collective-permute-start.10) | collective-permute-done | bytes 32800 | tf_op jit(solution)/shard_map/ppermute | solution.py:625
  64.8 4.2 %fault.5 = (f32[3,2,9,144,128]{4,3,2,1,0:T(8,128)S(1)}, f32[6,2,8,144,128]{4,3,2,1,0:T(8,128)S(1)}, f32[8,2,16,128]{3,2,1,0:T(8,128)S(1)}, f32[3,8,128,128]{3,2,...) custom-call(s32[3]{0:T(128)S(1)} %pad_add_fusion.flags, ...), custom_call_target="tpu_custom_call", output_to_operand_aliasing={{0}: (5, {}), {1}: (6, {}), {2}: (7, {})} | custom-call | flops 6553600 | tf_op jit(solution)/shard_map/fault/pallas_call | solution.py:641
  (6 shorter events, 0.0 us)
Async XLA Ops:
  8.6 2.7 %collective-permute-start = (f32[3,136,128]{2,1,0:T(8,128)S(1)}, f32[3,136,128]{2,1,0:T(8,128)S(1)}, u32[]{:S(2)}, u32[]{:S(2)}) collective-permute-start(f32[3,136,128]{2,1,0:T(8,128)S(1)} %get-tuple-element.42), channel_id=1, source_target_pairs={{0,1},{1,0},{2,3},{3,2},{4,5},{5,4},{6,7},{7,6},{8,9},{9,8},{10,11... | collective-permute-start | bytes 626696 | tf_op jit(solution)/shard_map/ppermute | solution.py:527
  8.7 7.1 %collective-permute-start.1 = (f32[3,136,128]{2,1,0:T(8,128)S(1)}, f32[3,136,128]{2,1,0:T(8,128)S(1)}, u32[]{:S(2)}, u32[]{:S(2)}) collective-permute-start(f32[3,136,128]{2,1,0:T(8,128)S(1)} %get-tuple-element.43), channel_id=1, source_target_pairs={{1,2},{2,1},{5,6},{6,5},{9,10},{10,9},{13,14},{14,13},{17,18},{18,... | collective-permute-start | bytes 626696 | tf_op jit(solution)/shard_map/ppermute | solution.py:527
  19.8 8.4 %collective-permute-start.2 = (f32[5,136,128]{2,1,0:T(8,128)S(1)}, f32[5,136,128]{2,1,0:T(8,128)S(1)}, u32[]{:S(2)}, u32[]{:S(2)}) collective-permute-start(f32[5,136,128]{2,1,0:T(8,128)S(1)} %get-tuple-element.48), channel_id=1, source_target_pairs={{0,4},{4,0},{8,12},{12,8},{1,5},{5,1},{9,13},{13,9},{2,6},{6,2},{1... | collective-permute-start | bytes 1044488 | tf_op jit(solution)/shard_map/ppermute | solution.py:527
  20.3 9.9 %collective-permute-start.3 = (f32[5,136,128]{2,1,0:T(8,128)S(1)}, f32[5,136,128]{2,1,0:T(8,128)S(1)}, u32[]{:S(2)}, u32[]{:S(2)}) collective-permute-start(f32[5,136,128]{2,1,0:T(8,128)S(1)} %get-tuple-element.49), channel_id=1, source_target_pairs={{4,8},{8,4},{5,9},{9,5},{6,10},{10,6},{7,11},{11,7},{20,24},{24,20... | collective-permute-start | bytes 1044488 | tf_op jit(solution)/shard_map/ppermute | solution.py:527
  31.0 4.1 %collective-permute-start.4 = (f32[5,16,128]{2,1,0:T(8,128)S(1)}, f32[5,16,128]{2,1,0:T(8,128)S(1)}, u32[]{:S(2)}, u32[]{:S(2)}) collective-permute-start(f32[5,16,128]{2,1,0:T(8,128)S(1)} %get-tuple-element.56.f_own), channel_id=1, source_target_pairs={{0,16},{16,0},{1,17},{17,1},{2,18},{18,2},{3,19},{19,3},{4,20},{20... | collective-permute-start | bytes 122888 | tf_op jit(solution)/shard_map/ppermute | solution.py:625
  36.8 7.3 %collective-permute-start.5 = (f32[4,128,128]{2,1,0:T(8,128)S(1)}, f32[4,128,128]{2,1,0:T(8,128)S(1)}, u32[]{:S(2)}, u32[]{:S(2)}) collective-permute-start(f32[4,128,128]{2,1,0:T(8,128)S(1)} %get-tuple-element.59), channel_id=1, source_target_pairs={{0,4},{4,0},{8,12},{12,8},{1,5},{5,1},{9,13},{13,9},{2,6},{6,2},{1... | collective-permute-start | bytes 786440 | tf_op jit(solution)/shard_map/ppermute | solution.py:527
  36.9 8.3 %collective-permute-start.6 = (f32[4,128,128]{2,1,0:T(8,128)S(1)}, f32[4,128,128]{2,1,0:T(8,128)S(1)}, u32[]{:S(2)}, u32[]{:S(2)}) collective-permute-start(f32[4,128,128]{2,1,0:T(8,128)S(1)} %get-tuple-element.60), channel_id=1, source_target_pairs={{4,8},{8,4},{5,9},{9,5},{6,10},{10,6},{7,11},{11,7},{20,24},{24,20... | collective-permute-start | bytes 786440 | tf_op jit(solution)/shard_map/ppermute | solution.py:527
  45.9 4.0 %collective-permute-start.7 = (f32[4,16,128]{2,1,0:T(8,128)S(1)}, f32[4,16,128]{2,1,0:T(8,128)S(1)}, u32[]{:S(2)}, u32[]{:S(2)}) collective-permute-start(f32[4,16,128]{2,1,0:T(8,128)S(1)} %get-tuple-element.66.f_own), channel_id=1, source_target_pairs={{0,16},{16,0},{1,17},{17,1},{2,18},{18,2},{3,19},{19,3},{4,20},{20... | collective-permute-start | bytes 98312 | tf_op jit(solution)/shard_map/ppermute | solution.py:625
  51.7 7.3 %collective-permute-start.8 = (f32[4,128,128]{2,1,0:T(8,128)S(1)}, f32[4,128,128]{2,1,0:T(8,128)S(1)}, u32[]{:S(2)}, u32[]{:S(2)}) collective-permute-start(f32[4,128,128]{2,1,0:T(8,128)S(1)} %get-tuple-element.69), channel_id=1, source_target_pairs={{0,4},{4,0},{8,12},{12,8},{1,5},{5,1},{9,13},{13,9},{2,6},{6,2},{1... | collective-permute-start | bytes 786440 | tf_op jit(solution)/shard_map/ppermute | solution.py:527
  51.8 8.3 %collective-permute-start.9 = (f32[4,128,128]{2,1,0:T(8,128)S(1)}, f32[4,128,128]{2,1,0:T(8,128)S(1)}, u32[]{:S(2)}, u32[]{:S(2)}) collective-permute-start(f32[4,128,128]{2,1,0:T(8,128)S(1)} %get-tuple-element.70), channel_id=1, source_target_pairs={{4,8},{8,4},{5,9},{9,5},{6,10},{10,6},{7,11},{11,7},{20,24},{24,20... | collective-permute-start | bytes 786440 | tf_op jit(solution)/shard_map/ppermute | solution.py:527
  60.8 4.0 %collective-permute-start.10 = (f32[4,16,128]{2,1,0:T(8,128)S(1)}, f32[4,16,128]{2,1,0:T(8,128)S(1)}, u32[]{:S(2)}, u32[]{:S(2)}) collective-permute-start(f32[4,16,128]{2,1,0:T(8,128)S(1)} %get-tuple-element.75.f_own), channel_id=1, source_target_pairs={{0,16},{16,0},{1,17},{17,1},{2,18},{18,2},{3,19},{19,3},{4,20},{20... | collective-permute-start | bytes 98312 | tf_op jit(solution)/shard_map/ppermute | solution.py:625

commit v3 on v2

v3 whole, which is shorter than its diff:
```python
import functools

import jax
import jax.numpy as jnp
from jax import lax
from jax.experimental import pallas as pl
from jax.experimental.pallas import tpu as pltpu
from jax.sharding import PartitionSpec as P

STEPS = 3
NEWTON = 3
DT = 0.2

PAD = 8
HALO = 3
CROSS = 4
STRIP = 8

XX, YY, ZZ, YZ, XZ, XY = range(6)
ALONG_Y = (XY, YY, YZ)
B, C11, C13, C33, C44, C66 = range(6)
FIELDS = [("v", c) for c in range(3)] + [("s", c) for c in range(6)] + [("m", c) for c in range(6)]
PRE_Y, PRE_Z, MASK, STRENGTH, RATE, SLIP, OWN_B, OTHER_B = range(8)

VMEM = pltpu.MemorySpace.VMEM
HBM = pltpu.MemorySpace.HBM
SMEM = pltpu.MemorySpace.SMEM


def in_vmem():
    return pl.BlockSpec(memory_space=VMEM)


def in_hbm():
    return pl.BlockSpec(memory_space=HBM)


def in_smem():
    return pl.BlockSpec(memory_space=SMEM)


def roll(values, by):
    by = by % values.shape[-1]
    return values if by == 0 else pltpu.roll(values, by, values.ndim - 1)


def at(ref, field, tile, y, row):
    return ref[field, tile, y, pl.ds(PAD + row, 8), :]


def z_below(pair, lanes):
    one, two = roll(pair[0], 1), roll(pair[1], 1)
    first = lanes == 0
    return jnp.where(first, two, one), jnp.where(first, one, two)


def z_above(pair, lanes):
    one, two = roll(pair[0], -1), roll(pair[1], -1)
    last = lanes == pair[0].shape[-1] - 1
    return jnp.where(last, two, one), jnp.where(last, one, two)


def trial_tile(v, s, m, y, row, below, lanes):
    both = (0, 1)
    behind = {c: z_below([at(s, c, t, y, row) for t in both], lanes) for c in (XZ, YZ, ZZ)}
    out = []
    for t in both:
        own = {c: at(s, c, t, y, row) for c in range(6)}
        lower_x = {c: own[c] - at(s, c, t, y, row - 1) for c in (XX, XY, XZ)}
        if below is None:
            lower_y = {c: own[c] for c in ALONG_Y}
        else:
            lower_y = {c: own[c] - below(c, t) for c in ALONG_Y}
        scale = DT * m[B, t, y, pl.ds(row, 8), :]
        total = (
            lower_x[XX] + lower_y[XY] + (own[XZ] - behind[XZ][t]),
            lower_x[XY] + lower_y[YY] + (own[YZ] - behind[YZ][t]),
            lower_x[XZ] + lower_y[YZ] + (own[ZZ] - behind[ZZ][t]),
        )
        out.append([at(v, c, t, y, row) + scale * total[c] for c in range(3)])
    return out


def stress_tile(v, s, m, y, row, lanes):
    both = (0, 1)
    own = [[at(v, c, t, y, row) for t in both] for c in range(3)]
    ahead = [z_above(own[c], lanes) for c in range(3)]
    for t in both:
        vx, vy, vz = own[0][t], own[1][t], own[2][t]
        over_x = [at(v, c, t, y, row + 1) for c in range(3)]
        over_y = [at(v, c, t, y + 1, row) for c in range(3)]
        exx, eyy, ezz = over_x[0] - vx, over_y[1] - vy, ahead[2][t] - vz
        c11, c13, c33, c44, c66 = (m[k, t, y, pl.ds(row, 8), :] for k in (C11, C13, C33, C44, C66))
        c12 = c11 - 2.0 * c66
        third = c13 * ezz
        change = {
            XX: c11 * exx + c12 * eyy + third,
            YY: c12 * exx + c11 * eyy + third,
            ZZ: c13 * (exx + eyy) + c33 * ezz,
            YZ: c44 * ((ahead[1][t] - vy) + (over_y[2] - vz)),
            XZ: c44 * ((ahead[0][t] - vx) + (over_x[2] - vz)),
            XY: c66 * ((over_y[0] - vx) + (over_x[1] - vy)),
        }
        for c, gain in change.items():
            s[c, t, y, pl.ds(PAD + row, 8), :] = at(s, c, t, y, row) + DT * gain


def lane_index(like):
    return lax.broadcasted_iota(jnp.int32, like, len(like) - 1)


def strip_pack(pieces, eighths):
    packed = jnp.zeros_like(pieces[0])
    for k, piece in enumerate(pieces):
        packed = jnp.where(eighths == k, roll(piece, STRIP * k + HALO), packed)
    return packed


def strip_take(packed, k):
    return roll(packed, -(STRIP * k + HALO))


def field_ref(kind, v, s, m):
    return {"v": v, "s": s, "m": m}[kind]


def fields_per_plane(ny, width):
    return (width - 5) // HALO // ny


def z_slots(ny, width):
    per_plane = fields_per_plane(ny, width)
    slots = {}
    for f in range(len(FIELDS)):
        for y in range(ny):
            slots[f, y] = (f // per_plane, f % per_plane * ny + y)
    return slots, -(-len(FIELDS) // per_plane)


def row_tiles(nx):
    return [*range(0, nx, 8), cross_row(nx)]


def cross_row(nx):
    return nx + PAD


def packed_row(row, nx):
    return row if row < nx else nx


def edge_kernel(flags, velocity, stress, *rest):
    raw_m, out, sem = rest[:6], rest[6], rest[7]
    ny, nx = velocity.shape[1:3]
    sources = [velocity.at[c] for c in range(3)] + [stress.at[c] for c in range(6)] + list(raw_m)
    for side, row in ((0, nx - CROSS), (1, 0)):

        @pl.when(flags[0] == side)
        def _(row=row):
            copies = []
            for f, source in enumerate(sources):
                for half in range(2):
                    part = source.at[pl.ds(half * (ny // 2), ny // 2), pl.ds(row, CROSS), :]
                    to = out.at[f, :, pl.ds(half * CROSS, CROSS), :]
                    copies.append(pltpu.make_async_copy(part, to, sem.at[2 * f + half]))
            for copy in copies:
                copy.start()
            for copy in copies:
                copy.wait()


def load_kernel(flags, velocity, stress, *rest):
    raw_m, small = rest[:6], rest[6:13]
    v, s, m, fault, y_a, y_b = rest[13:19]
    pre, ids, mask, rate, slip, region_a, region_normal, sems = rest[19:]
    ny, nx, width = velocity.shape[1:]
    cross = cross_row(nx)
    big = {}
    for c in range(6):
        big["s", c] = (stress.at[c], s.at[c, 0, :, pl.ds(PAD, nx), :])
    for c in range(3):
        big["v", c] = (velocity.at[c], v.at[c, 0, pl.ds(0, ny), pl.ds(PAD, nx), :])
    for c in range(6):
        big["m", c] = (raw_m[c], m.at[c, 0, :, pl.ds(0, nx), :])
    big = {
        key: pltpu.make_async_copy(a, b, sems.at[k]) for k, (key, (a, b)) in enumerate(big.items())
    }
    held = (pre, ids, mask, rate, slip, region_a, region_normal)
    little = [
        pltpu.make_async_copy(a, b, sems.at[len(big) + k])
        for k, (a, b) in enumerate(zip(small, held))
    ]
    for copy in big.values():
        copy.start()
    for copy in little:
        copy.start()
    zeros = jnp.zeros((PAD, width), jnp.float32)
    for t in range(2):
        for y in range(ny):
            for c in (XX, XY, XZ):
                s[c, t, y, 0:PAD, :] = zeros
                s[c, t, y, cross : cross + PAD, :] = zeros
            for c in range(3):
                v[c, t, y, PAD + nx : PAD + nx + PAD, :] = zeros
                v[c, t, y, PAD + cross + 8 : 2 * PAD + cross + 8, :] = zeros
    for copy in little:
        copy.wait()
    kinds = ids[...]
    a_part = jnp.zeros((ny, width), jnp.float32)
    n_part = jnp.zeros((ny, width), jnp.float32)
    for k in range(region_a.shape[0]):
        a_part = jnp.where(kinds == k, region_a[k], a_part)
        n_part = jnp.where(kinds == k, region_normal[k], n_part)
    fault[PRE_Y, 0, 0:ny, :] = pre[0]
    fault[PRE_Z, 0, 0:ny, :] = pre[1]
    fault[MASK, 0, 0:ny, :] = mask[...].astype(jnp.float32)
    fault[STRENGTH, 0, 0:ny, :] = a_part * n_part
    fault[RATE, 0, 0:ny, :] = rate[...]
    fault[SLIP, 0, 0:ny, :] = slip[...]
    for copy in big.values():
        copy.wait()

    odd = flags[1] == 1
    lanes = lane_index((8, width))
    first = lanes == 0
    last = ny - 1
    for row in range(0, nx, 8):
        up = [at(s, c, 0, last, row) for c in ALONG_Y]
        own = {c: at(s, c, 0, 0, row) for c in range(6)}
        behind = {c: jnp.where(first, 0.0, roll(own[c], 1)) for c in (XZ, YZ, ZZ)}
        lower_x = {c: own[c] - at(s, c, 0, 0, row - 1) for c in (XX, XY, XZ)}
        buoyancy = m[B, 0, 0, pl.ds(row, 8), :]
        total = (
            lower_x[XX] + own[XY] + (own[XZ] - behind[XZ]),
            lower_x[XY] + own[YY] + (own[YZ] - behind[YZ]),
            lower_x[XZ] + own[YZ] + (own[ZZ] - behind[ZZ]),
        )
        for c in range(3):
            down = at(v, c, 0, 0, row) + DT * buoyancy * total[c]
            y_a[c, pl.ds(row, 8), :] = jnp.where(odd, down, up[c])
            y_b[c, pl.ds(row, 8), :] = jnp.where(odd, up[c], down)
        y_a[3, pl.ds(row, 8), :] = buoyancy
        y_b[3, pl.ds(row, 8), :] = buoyancy


def z_emit(z_a, z_b, odd, group, pieces, plane, row):
    up = jnp.zeros_like(pieces[0][1])
    down = up
    for pos, piece in pieces:
        moved = roll(piece, HALO * pos + HALO)
        up = jnp.where(group == pos, moved, up)
        down = jnp.where(group == pos + 1, moved, down)
    z_a[plane, pl.ds(row, 8), :] = jnp.where(odd, down, up)
    z_b[plane, pl.ds(row, 8), :] = jnp.where(odd, up, down)


def z_pieces(plane, v, s, m, row):
    ny, width = m.shape[2], m.shape[4]
    per_plane = fields_per_plane(ny, width)
    pieces = []
    for f, (kind, c) in enumerate(FIELDS[plane * per_plane : (plane + 1) * per_plane]):
        shift = 0 if kind == "m" else PAD
        ref = field_ref(kind, v, s, m)
        for y in range(ny):
            pieces.append((f * ny + y, ref[c, 0, y, pl.ds(row + shift, 8), :]))
    return pieces


UNROLL = 4


def pack_kernel(flags, thirds, v, s, m, z_a, z_b):
    ny, width = m.shape[2], m.shape[4]
    nx = z_a.shape[1] - 16
    planes = z_slots(ny, width)[1]
    odd = flags[2] == 1
    group = thirds[...]

    def pack(i, carry):
        for part in range(UNROLL):
            row = pl.multiple_of((i * UNROLL + part) * 8, 8)
            for plane in range(planes):
                z_emit(z_a, z_b, odd, group, z_pieces(plane, v, s, m, row), plane, row)
        return carry

    lax.fori_loop(0, nx // (8 * UNROLL), pack, 0)


def cross_kernel(flags, thirds, f_other, fault, v_in, s_in, m_in, za_in, zb_in, v, s, m, z_a, z_b):
    ny, width = m.shape[2], m.shape[4]
    nx = z_a.shape[1] - 16
    cross = cross_row(nx)
    odd = flags[2] == 1
    group = thirds[...]
    planes = z_slots(ny, width)[1]
    rows = lax.broadcasted_iota(jnp.int32, (8, width), 0)
    minus = flags[0] == 0
    keep = jnp.where(minus, 7 - rows, rows) >= 8 - CROSS
    for f, (kind, c) in enumerate(FIELDS):
        shift = 0 if kind == "m" else PAD
        ref = field_ref(kind, v, s, m)
        for y in range(ny // 2):
            tile = f_other[f, y]
            turned = pltpu.roll(tile, CROSS, 0)
            ref[c, 0, y, cross + shift : cross + shift + 8, :] = jnp.where(
                keep, jnp.where(minus, tile, turned), 0.0
            )
            ref[c, 0, y + ny // 2, cross + shift : cross + shift + 8, :] = jnp.where(
                keep, jnp.where(minus, turned, tile), 0.0
            )
    for plane in range(planes):
        z_emit(z_a, z_b, odd, group, z_pieces(plane, v, s, m, cross), plane, nx)
    z_emit(z_a, z_b, odd, group, [(k, fault[k, 0, 0:8, :]) for k in range(6)], 0, nx + 8)
    zeros = jnp.zeros((8, width), jnp.float32)
    for plane in range(1, planes):
        z_a[plane, pl.ds(nx + 8, 8), :] = zeros
        z_b[plane, pl.ds(nx + 8, 8), :] = zeros


def write_messages(v, s, eighths, odd, y_a, y_b, nx):
    last = s.shape[2] - 1
    span = nx + 8
    for row in row_tiles(nx):
        up = [at(s, c, 0, last, row) for c in ALONG_Y]
        down = [at(v, c, 0, 0, row) for c in range(3)]
        up.append(strip_pack([at(s, c, 1, last, row) for c in ALONG_Y], eighths))
        down.append(strip_pack([at(v, c, 1, 0, row) for c in range(3)], eighths))
        for k in range(4):
            to = pl.ds(k * span + packed_row(row, nx), 8)
            y_a[to, :] = jnp.where(odd, down[k], up[k])
            y_b[to, :] = jnp.where(odd, up[k], down[k])


def partial_trials(v, s, m, nx, lanes):
    for row in row_tiles(nx):
        new = trial_tile(v, s, m, 0, row, None, lanes)
        for t in range(2):
            for c in range(3):
                v[c, t, 0, pl.ds(PAD + row, 8), :] = new[t][c]


def widen_kernel(flags, thirds, eighths, r_a, r_b, v_in, s_in, m_in, f_in, v, s, m, fault, y_a, y_b):
    ny, width = m.shape[2], m.shape[4]
    nx = r_a.shape[1] - 16
    cross = cross_row(nx)
    slots, planes = z_slots(ny, width)
    odd_z, odd_y = flags[2] == 1, flags[1] == 1
    lanes = lane_index((8, width))
    group = thirds[...]

    def take(row, wanted):
        from_a = [r_a[p, pl.ds(row, 8), :] for p in range(planes)]
        from_b = [r_b[p, pl.ds(row, 8), :] for p in range(planes)]
        low = [jnp.where(odd_z, a, b) for a, b in zip(from_a, from_b)]
        high = [jnp.where(odd_z, b, a) for a, b in zip(from_a, from_b)]
        for (plane, pos), store in wanted:
            store(roll(jnp.where(group == pos, low[plane], high[plane]), -(HALO * pos + HALO)))

    def store_to(ref, c, y, row):
        def store(value):
            ref[c, 1, y, pl.ds(row, 8), :] = value

        return store

    def fields(row):
        wanted = []
        for f, (kind, c) in enumerate(FIELDS):
            shift = 0 if kind == "m" else PAD
            ref = field_ref(kind, v, s, m)
            for y in range(ny):
                wanted.append((slots[f, y], store_to(ref, c, y, row + shift)))
        return wanted

    def unpack(i, carry):
        for part in range(UNROLL):
            row = pl.multiple_of((i * UNROLL + part) * 8, 8)
            take(row, fields(row))
        return carry

    lax.fori_loop(0, nx // (8 * UNROLL), unpack, 0)
    take(nx, fields(cross))

    def store_fault(k):
        def store(value):
            fault[k, 1, 0:8, :] = value

        return store

    take(nx + 8, [((0, k), store_fault(k)) for k in range(6)])
    partial_trials(v, s, m, nx, lanes)
    last = ny - 1
    halos = eighths[...]
    for row in row_tiles(nx):
        buoyancy = m[B, 1, 0, pl.ds(row, 8), :]
        up = [at(s, c, 1, last, row) for c in ALONG_Y] + [buoyancy]
        down = [
            jnp.where(lanes == HALO, roll(at(v, c, 0, 0, row), HALO), at(v, c, 1, 0, row))
            for c in range(3)
        ] + [buoyancy]
        up, down = strip_pack(up, halos), strip_pack(down, halos)
        to = pl.ds(packed_row(row, nx), 8)
        y_a[to, :] = jnp.where(odd_y, down, up)
        y_b[to, :] = jnp.where(odd_y, up, down)
    up = [at(s, c, 0, last, cross) for c in ALONG_Y]
    down = [at(v, c, 0, 0, cross) for c in range(3)]
    buoyancy = m[B, 0, 0, pl.ds(cross, 8), :]
    for c in range(4):
        to = pl.ds(nx + 8 + 8 * c, 8)
        y_a[to, :] = buoyancy if c == 3 else jnp.where(odd_y, down[c], up[c])
        y_b[to, :] = buoyancy if c == 3 else jnp.where(odd_y, up[c], down[c])
    for t in range(2):
        for k in range(8):
            line = fault[min(k, 5), t, 0:1, :]
            row = nx + 40 + 8 * t + k
            y_a[row : row + 1, :] = line
            y_b[row : row + 1, :] = line


def inner_kernel(first, final, m, v_in, s_in, v, s, *outs):
    ny, width = m.shape[2], m.shape[4]
    nx = m.shape[3] - 16
    lanes = lane_index((8, width))

    if not first:

        def ends(y, carry):
            for row in (0, nx - 8, cross_row(nx)):
                stress_tile(v, s, m, y, row, lanes)
            return carry

        lax.fori_loop(1, ny - 1, ends, 0)

    def trials(y, carry):
        for row in row_tiles(nx):
            new = trial_tile(
                v, s, m, y, row, lambda c, t, row=row: at(s, c, t, y - 1, row), lanes
            )
            for t in range(2):
                for c in range(3):
                    v[c, t, y, pl.ds(PAD + row, 8), :] = new[t][c]
        return carry

    lax.fori_loop(1, ny, trials, 0)
    copies = []
    if final:
        new_v, new_s, sems = outs
        for c in range(3):
            part = v.at[c, 0, pl.ds(1, ny - 1), pl.ds(PAD + 8, nx - 16), :]
            to = new_v.at[c, pl.ds(1, ny - 1), pl.ds(8, nx - 16), :]
            copies.append(pltpu.make_async_copy(part, to, sems.at[c]))
            copies[-1].start()

    def stresses(y, carry):
        for row in range(8, nx - 8, 8):
            stress_tile(v, s, m, y, row, lanes)
        return carry

    lax.fori_loop(1, ny - 1, stresses, 0)
    if final:
        for c in range(6):
            part = s.at[c, 0, pl.ds(1, ny - 2), pl.ds(PAD + 8, nx - 16), :]
            to = new_s.at[c, pl.ds(1, ny - 2), pl.ds(8, nx - 16), :]
            copies.append(pltpu.make_async_copy(part, to, sems.at[3 + c]))
            copies[-1].start()
        for copy in copies:
            copy.wait()


def boundary_kernel(first, final, flags, eighths, *refs):
    refs = list(refs)

    def pop(n):
        out = refs[:n]
        del refs[:n]
        return out

    early_a, early_b = pop(2) if first else (None, None)
    r_a, r_b, m = pop(3)
    if not first:
        (ahead_b,) = pop(1)
    pop(3)
    if final:
        pop(2)
    v, s, fault = pop(3)
    if first:
        (ahead_b,) = pop(1)
    if final:
        new_v, new_s, slip_out, rows, sems = refs
    else:
        y_a, y_b, rows = refs
    ny, width = m.shape[2], m.shape[4]
    nx = m.shape[3] - 16
    cross = cross_row(nx)
    span = nx + 8
    odd = flags[1] == 1
    lanes = lane_index((8, width))
    halos = eighths[...]

    def received(row):
        at_row = packed_row(row, nx)
        if not first:
            from_a = [r_a[pl.ds(k * span + at_row, 8), :] for k in range(4)]
            from_b = [r_b[pl.ds(k * span + at_row, 8), :] for k in range(4)]
        else:
            if row < nx:
                from_a = [early_a[k, pl.ds(row, 8), :] for k in range(4)]
                from_b = [early_b[k, pl.ds(row, 8), :] for k in range(4)]
            else:
                from_a = [r_a[pl.ds(span + 8 * k, 8), :] for k in range(4)]
                from_b = [r_b[pl.ds(span + 8 * k, 8), :] for k in range(4)]
            from_a.append(r_a[pl.ds(at_row, 8), :])
            from_b.append(r_b[pl.ds(at_row, 8), :])
        low = [jnp.where(odd, a, b) for a, b in zip(from_a, from_b)]
        high = [jnp.where(odd, b, a) for a, b in zip(from_a, from_b)]
        if first and row < nx:
            for c in range(3):
                column = roll(high[-1], -(STRIP * c + 2 * HALO))
                high[c] = jnp.where(lanes == 0, column, high[c])
        return low, high

    if first:
        for t in range(2):
            to = pl.ds(span + 32 + 8 * t, 8)
            lines = jnp.where(odd, r_b[to, :], r_a[to, :])
            for k in range(6):
                fault[k, t, ny : ny + 1, :] = lines[k : k + 1, :]
    for row in row_tiles(nx):
        low, high = received(row)
        if first:
            ahead_b[0, pl.ds(row, 8), :] = high[3]
            ahead_b[1, pl.ds(row, 8), :] = strip_take(high[-1], 3)
        for t in range(2):
            scale = DT * m[B, t, 0, pl.ds(row, 8), :]
            scale_ahead = DT * ahead_b[t, pl.ds(row, 8), :]
            for c in range(3):
                low_c = low[c] if t == 0 else strip_take(low[-1], c)
                high_c = high[c] if t == 0 else strip_take(high[-1], c)
                v[c, t, 0, pl.ds(PAD + row, 8), :] = at(v, c, t, 0, row) - scale * low_c
                v[c, t, ny, pl.ds(PAD + row, 8), :] = high_c - scale_ahead * at(
                    s, ALONG_Y[c], t, ny - 1, row
                )

    places = ((0, (nx - 1, cross)), (1, (0, cross + 7)))
    for side, pair in places:

        @pl.when(flags[0] == side)
        def _(pair=pair):
            for which, row in enumerate(pair):
                for t in range(2):
                    for y in range(ny + 1):
                        for c in range(3):
                            rows[which, c, t, y : y + 1, :] = v[
                                c, t, y, PAD + row : PAD + row + 1, :
                            ]
                        if first:
                            if y < ny:
                                line = m[B, t, y, row : row + 1, :]
                            else:
                                line = ahead_b[t, row : row + 1, :]
                            fault[OWN_B + which, t, y : y + 1, :] = line

    minus = flags[0] == 0
    sign = jnp.where(minus, DT, -DT)
    for t in range(2):
        for half in range(0, fault.shape[2], 8):
            part = slice(half, half + 8)
            own = [rows[0, c, t, part, :] for c in range(3)]
            other = [rows[1, c, t, part, :] for c in range(3)]
            par = [fault[k, t, part, :] for k in range(8)]
            m_side = [jnp.where(minus, a, b) for a, b in zip(own, other)]
            p_side = [jnp.where(minus, b, a) for a, b in zip(own, other)]
            m_b = jnp.where(minus, par[OWN_B], par[OTHER_B])
            p_b = jnp.where(minus, par[OTHER_B], par[OWN_B])
            traction, slip = friction(m_side, p_side, m_b, p_b, par)
            fault[SLIP, t, part, :] = slip
            for c in range(3):
                rows[0, c, t, part, :] = own[c] + sign * par[OWN_B] * traction[c]
                rows[1, c, t, part, :] = other[c] - sign * par[OTHER_B] * traction[c]
    for side, pair in places:

        @pl.when(flags[0] == side)
        def _(pair=pair):
            for which, row in enumerate(pair):
                for c in range(3):
                    for t in range(2):
                        for y in range(ny + 1):
                            v[c, t, y, PAD + row : PAD + row + 1, :] = rows[
                                which, c, t, y : y + 1, :
                            ]

    def planes(i, carry):
        for row in row_tiles(nx)[:-1] if final else row_tiles(nx):
            stress_tile(v, s, m, i * (ny - 1), row, lanes)
        return carry

    lax.fori_loop(0, 2, planes, 0)
    if not final:
        partial_trials(v, s, m, nx, lanes)
        write_messages(v, s, halos, odd, y_a, y_b, nx)
        return

    def ends(y, carry):
        for row in (0, nx - 8):
            stress_tile(v, s, m, y, row, lanes)
        return carry

    lax.fori_loop(1, ny - 1, ends, 0)
    slip_out[...] = fault[SLIP, 0, 0:ny, :]
    copies = []
    for ref, out, fields, whole in ((v, new_v, 3, (0,)), (s, new_s, 6, (0, ny - 1))):
        inside = ny - len(whole)
        for c in range(fields):
            for y in whole:
                copies.append((ref.at[c, 0, y, pl.ds(PAD, nx), :], out.at[c, y]))
            for row in (0, nx - 8):
                copies.append(
                    (
                        ref.at[c, 0, pl.ds(1, inside), pl.ds(PAD + row, 8), :],
                        out.at[c, pl.ds(1, inside), pl.ds(row, 8), :],
                    )
                )
    copies = [pltpu.make_async_copy(a, b, sems.at[k]) for k, (a, b) in enumerate(copies)]
    for copy in copies:
        copy.start()
    for copy in copies:
        copy.wait()


def inverse_sinh(values):
    size = jnp.abs(values)
    sign = jnp.where(values > 0.0, 1.0, jnp.where(values < 0.0, -1.0, 0.0))
    return sign * jnp.log(size + jnp.sqrt(size * size + 1.0))


def friction(minus_side, plus_side, minus_b, plus_b, par):
    total = DT * (minus_b + plus_b)
    impedance = 1.0 / jnp.where(total > 0.0, total, 1.0)
    jump = [p - q for p, q in zip(plus_side, minus_side)]
    locked_y = par[PRE_Y] + impedance * jump[1]
    locked_z = par[PRE_Z] + impedance * jump[2]
    magnitude = jnp.sqrt(locked_y * locked_y + locked_z * locked_z + 1.0)
    rate, strength, slip = par[RATE], par[STRENGTH], par[SLIP]
    for _ in range(NEWTON):
        scaled = rate * slip
        residual = magnitude - impedance * slip - strength * inverse_sinh(scaled)
        tangent = -impedance - strength * rate / jnp.sqrt(1.0 + scaled * scaled)
        slip = slip - residual / tangent
    slip = slip * par[MASK]
    retained = 1.0 - impedance * slip / magnitude
    traction = (
        impedance * jump[0],
        retained * locked_y - par[PRE_Y],
        retained * locked_z - par[PRE_Z],
    )
    return traction, slip


def f32(*shape):
    return VMEM(shape, jnp.float32)


def call(kernel, name, outs, in_specs, aliases, scratch=(), flops=0, out_specs=None):
    return pl.pallas_call(
        kernel,
        out_shape=tuple(outs),
        in_specs=in_specs,
        out_specs=tuple(out_specs or [in_vmem() for _ in outs]),
        input_output_aliases=aliases,
        scratch_shapes=list(scratch),
        compiler_params=pltpu.CompilerParams(vmem_limit_bytes=8 << 20),
        cost_estimate=pl.CostEstimate(flops=flops, bytes_accessed=0, transcendentals=0),
        name=name,
    )


def pair_swaps(a, b, axis):
    size = lax.axis_size(axis)
    out = []
    for value, start in ((a, 0), (b, 1)):
        pairs = []
        for i in range(start, size - 1, 2):
            pairs += [(i, i + 1), (i + 1, i)]
        out.append(lax.ppermute(value, axis, pairs))
    return out


def local(
    velocity,
    stress,
    buoyancy,
    stiff_xx,
    stiff_xz,
    stiff_zz,
    shear_vert,
    shear_horiz,
    prestress,
    fault_mask,
    region_ids,
    inverse_rate,
    slip_prev,
    region_a,
    region_normal,
):
    ny, nx, width = buoyancy.shape
    across, along, dip = (lax.axis_index(k) for k in ("gx", "gy", "gz"))
    flags = jnp.stack([across, along % 2, dip % 2]).astype(jnp.int32)
    lanes = jnp.broadcast_to(jnp.arange(width, dtype=jnp.int32), (8, width))
    thirds, eighths = lanes // HALO, lanes // STRIP
    rows = cross_row(nx) + 8
    high = 8 * ((ny + 1 + 7) // 8)
    v_shape = f32(3, 2, ny + 1, rows + 2 * PAD, width)
    s_shape = f32(6, 2, ny, rows + 2 * PAD, width)
    m_shape = f32(6, 2, ny, rows, width)
    fault_shape = f32(8, 2, high, width)
    planes = z_slots(ny, width)[1]
    z_shape = f32(planes, nx + 16, width)
    unit = ny * nx * width
    vm, hb, sm = in_vmem(), in_hbm(), in_smem()
    raw = [velocity, stress, buoyancy, stiff_xx, stiff_xz, stiff_zz, shear_vert, shear_horiz]
    raw += [prestress, region_ids, fault_mask, inverse_rate, slip_prev, region_a, region_normal]
    raw = [pltpu.with_memory_space_constraint(k, HBM) for k in raw]

    f_shape = f32(len(FIELDS), ny // 2, 8, width)
    (f_own,) = call(
        edge_kernel,
        "edge",
        (f_shape,),
        [sm] + [hb] * 8,
        {},
        [pltpu.SemaphoreType.DMA((2 * len(FIELDS),))],
        flops=unit,
    )(flags, *raw[:8])
    f_other = lax.ppermute(f_own, "gx", [(i, i ^ 1) for i in range(lax.axis_size("gx"))])
    y_shape = f32(4, nx, width)
    v, s, m, fault, early_a, early_b = call(
        load_kernel,
        "load",
        (v_shape, s_shape, m_shape, fault_shape, y_shape, y_shape),
        [sm] + [hb] * 15,
        {},
        [
            pltpu.VMEM(prestress.shape, jnp.float32),
            pltpu.VMEM(region_ids.shape, jnp.int32),
            pltpu.VMEM(fault_mask.shape, jnp.int32),
            pltpu.VMEM(inverse_rate.shape, jnp.float32),
            pltpu.VMEM(slip_prev.shape, jnp.float32),
            pltpu.SMEM(region_a.shape, jnp.float32),
            pltpu.SMEM(region_normal.shape, jnp.float32),
            pltpu.SemaphoreType.DMA((22,)),
        ],
        flops=100 * unit,
    )(flags, *raw)
    early_a, early_b = pair_swaps(early_a, early_b, "gy")
    z_a, z_b = call(
        pack_kernel, "pack", (z_shape, z_shape), [sm] + [vm] * 4, {}, flops=50 * unit
    )(flags, thirds, v, s, m)
    v, s, m, z_a, z_b = call(
        cross_kernel,
        "cross",
        (v_shape, s_shape, m_shape, z_shape, z_shape),
        [sm] + [vm] * 8,
        {4: 0, 5: 1, 6: 2, 7: 3, 8: 4},
        flops=10 * unit,
    )(flags, thirds, f_other, fault, v, s, m, z_a, z_b)
    z_a, z_b = pair_swaps(z_a, z_b, "gz")
    y_shape = f32(nx + 8 + 32 + 16, width)
    v, s, m, fault, y_a, y_b = call(
        widen_kernel,
        "widen",
        (v_shape, s_shape, m_shape, fault_shape, y_shape, y_shape),
        [sm] + [vm] * 8,
        {5: 0, 6: 1, 7: 2, 8: 3},
        flops=50 * unit,
    )(flags, thirds, eighths, z_a, z_b, v, s, m, fault)
    y_shape = f32(4 * (nx + 8), width)
    ahead_b = None
    out_shapes = (HBM((3, ny, nx, width), jnp.float32), HBM((6, ny, nx, width), jnp.float32))
    for step in range(STEPS):
        first, final = step == 0, step == STEPS - 1
        y_a, y_b = pair_swaps(y_a, y_b, "gy")
        v, s, *outs = call(
            functools.partial(inner_kernel, first, final),
            "inner",
            (v_shape, s_shape) + (out_shapes if final else ()),
            [vm] * 3,
            {1: 0, 2: 1},
            [pltpu.SemaphoreType.DMA((9,))] if final else [],
            flops=200 * unit,
            out_specs=[vm, vm] + ([hb, hb] if final else []),
        )(m, v, s)
        args = [flags, eighths] + ([early_a, early_b] if first else []) + [y_a, y_b, m]
        args += ([] if first else [ahead_b]) + [v, s, fault] + outs
        at_state = len(args) - len(outs) - 3
        aliases = {at_state + k: k for k in range(3)}
        shapes, specs = [v_shape, s_shape, fault_shape], [vm, vm, vm]
        scratch = [pltpu.VMEM((2, 3, 2, high, width), jnp.float32)]
        if first:
            shapes.append(f32(2, rows, width))
            specs.append(vm)
        if final:
            shapes += [*out_shapes, jax.ShapeDtypeStruct((ny, width), jnp.float32)]
            specs += [hb, hb, vm]
            scratch.append(pltpu.SemaphoreType.DMA((3 * 3 + 6 * 4,)))
            aliases.update({at_state + 3: 3, at_state + 4: 4})
        else:
            shapes += [y_shape, y_shape]
            specs += [vm, vm]
        v, s, fault, *more = call(
            functools.partial(boundary_kernel, first, final),
            "boundary",
            shapes,
            [sm] + [vm] * (len(args) - 1 - len(outs)) + [hb] * len(outs),
            aliases,
            scratch,
            flops=50 * unit,
            out_specs=specs,
        )(*args)
        if final:
            return tuple(more)
        if first:
            ahead_b, *more = more
        y_a, y_b = more


def solution(mesh):
    in_specs = (
        P(None, "gy", "gx", "gz"),
        P(None, "gy", "gx", "gz"),
        P("gy", "gx", "gz"),
        P("gy", "gx", "gz"),
        P("gy", "gx", "gz"),
        P("gy", "gx", "gz"),
        P("gy", "gx", "gz"),
        P("gy", "gx", "gz"),
        P(None, "gy", "gz"),
        P("gy", "gz"),
        P("gy", "gz"),
        P("gy", "gz"),
        P("gy", "gz"),
        P(),
        P(),
    )
    out_specs = (P(None, "gy", "gx", "gz"), P(None, "gy", "gx", "gz"), P("gy", "gz"))
    return jax.shard_map(local, mesh=mesh, in_specs=in_specs, out_specs=out_specs, check_vma=False)
```

time: 69.7 us -> 61.7 us (0.89)
  starting transfers between devices: 20.5 us -> 15.9 us
  waiting for transfers between devices: 14.1 us -> 10.7 us
    ppermute x3 -> x1, waiting for transfers between devices: 5.56 us -> 0.01 us  [local(): lax.ppermute(f_own, 'gx', [(i, i ^ 1) for i in range(lax.axis_size('gx'))])]
    ppermute x3 -> x1, starting transfers between devices: 4.78 us -> 1.59 us  [local(): lax.ppermute(f_own, 'gx', [(i, i ^ 1) for i in range(lax.axis_size('gx'))])]
    ppermute x8 -> x10, waiting for transfers between devices: 8.58 us -> 10.7 us  [pair_swaps(): out.append(lax.ppermute(value, axis, pairs))]
    ppermute x8 -> x10, starting transfers between devices: 15.7 us -> 14.3 us  [pair_swaps(): out.append(lax.ppermute(value, axis, pairs))]
    pallas_call x13 -> x10, Pallas kernels: 29.4 us -> 29.8 us  [the longest x3 12.4 us: local(): call(functools.partial(inner_kernel, first, final), 'inner', (v_shape, s_...]
  transfers between devices with their start and end apart: 11 -> 11, of which waited for: 7 -> 5; matrix products, arithmetic and copies ran while one was open for 0% -> 0% of each run, Pallas kernels for 17% -> 39%
where the time goes in v3:
time: 61.7 us; the launch traced here: 61.4 us
  Pallas kernels  33.8 us (55%)
  starting transfers between devices  15.9 us (26%)
  waiting for transfers between devices  10.7 us (17%)
  between operations  0.88 us (1%)
    ppermute x10, starting transfers between devices, pair_swaps(): out.append(lax.ppermute(value, axis, pairs))  14.3 us
    pallas_call x3, Pallas kernels, local(): call(functools.partial(inner_kernel, first, final), 'inner', (v_shape, s_...  12.4 us
    ppermute x10, waiting for transfers between devices, pair_swaps(): out.append(lax.ppermute(value, axis, pairs))  10.7 us
    pallas_call x3, Pallas kernels, local(): call(functools.partial(boundary_kernel, first, final), 'boundary', shapes...  7.98 us
    pallas_call x1, Pallas kernels, local(): call(load_kernel, 'load', (v_shape, s_shape, m_shape, fault_shape, y_shap...  4.11 us
    pallas_call x1, Pallas kernels, local(): call(widen_kernel, 'widen', (v_shape, s_shape, m_shape, fault_shape, y_sh...  4.03 us
    pallas_call x1, Pallas kernels, local(): call(pack_kernel, 'pack', (z_shape, z_shape), [sm] + [vm] * 4, {}, flops=...  2.85 us
    pallas_call x1, Pallas kernels, local(): call(edge_kernel, 'edge', (f_shape,), [sm] + [hb] * 8, {}, [pltpu.Semapho...  1.73 us
  transfers between devices with their start and end apart: 11, of which 5 were waited for; matrix products, arithmetic and copies ran while one was open for 0% of the time, Pallas kernels for 39%

profile of v3, /device:TPU:10, one launch (start us, length us, event | category | flops | bytes accessed | tf_op | source)
XLA Modules:
  0.0 61.4 jit_solution(4351742893609243441)
XLA Ops:
  0.6 0.1 pad_add_fusion.flags
  0.7 1.7 %edge.1 = f32[15,4,8,128]{3,2,1,0:T(8,128)S(1)} custom-call(s32[3]{0:T(128)S(1)} %pad_add_fusion.flags, f32[3,8,128,128]{3,2,1,0:T(8,128)} %velocity.3, f32[6,8,128,128]{3,2,1,0:T(8,128)} %stress.3, f32[8,128,128]{2,1,0:T(8,128)} %rest_0_.3, f32[8,128,128]{2,1,0:T(8,128)} %rest_1_.3, f32[8,128,128]{2,1,0:T(8,128)} %rest_2_.3, f32[8,128,128]{2,1,0:T(8,128)} %rest_3_.3, ...), custom_call_target="tpu_custom_call" | custom-call | flops 131072 | tf_op jit(solution)/shard_map/edge/pallas_call | solution.py:724
  2.5 1.6 %collective-permute-start.2 = (f32[15,4,8,128]{3,2,1,0:T(8,128)S(1)}, f32[15,4,8,128]{3,2,1,0:T(8,128)S(1)}, u32[]{:S(2)}, u32[]{:S(2)}) collective-permute-start(f32[15,4,8,128]{3,2,1,0:T(8,128)S(1)} %edge.1), channel_id=1, source_target_pairs={{0,16},{16,0},{1,17},{17,1},{2,18},{18,2},{3,19},{19,3},{4,20},{20... | collective-permute-start | bytes 737288 | tf_op jit(solution)/shard_map/ppermute | solution.py:733
  4.1 4.1 %load.1 = (f32[3,2,9,160,128]{4,3,2,1,0:T(8,128)S(1)}, f32[6,2,8,160,128]{4,3,2,1,0:T(8,128)S(1)}, f32[6,2,8,144,128]{4,3,2,1,0:T(8,128)S(1)}, f32[8,2,16,128]{3...) custom-call(s32[3]{0:T(128)S(1)} %pad_add_fusion.flags, f32[3,8,128,128]{3,2,1,0:T(8,128)} %velocity.3, ...), custom_call_target="tpu_custom_call" | custom-call | flops 13107200 | tf_op jit(solution)/shard_map/load/pallas_call | solution.py:735
  8.2 0.5 collective-permute-start
  8.7 4.6 %collective-permute-start.1 = (f32[4,128,128]{2,1,0:T(8,128)S(1)}, f32[4,128,128]{2,1,0:T(8,128)S(1)}, u32[]{:S(2)}, u32[]{:S(2)}) collective-permute-start(f32[4,128,128]{2,1,0:T(8,128)S(1)} %get-tuple-element.45), channel_id=1, source_target_pairs={{4,8},{8,4},{5,9},{9,5},{6,10},{10,6},{7,11},{11,7},{20,24},{24,20... | collective-permute-start | bytes 786440 | tf_op jit(solution)/shard_map/ppermute | solution.py:683
  13.3 2.9 %pack.1 = (f32[3,144,128]{2,1,0:T(8,128)S(1)}, f32[3,144,128]{2,1,0:T(8,128)S(1)}) custom-call(s32[3]{0:T(128)S(1)} %pad_add_fusion.flags, s32[8,128]{1,0:T(8,128)S(1)} %broadcast_select_fusion.thirds, f32[3,2,9,160,128]{4,3,2,1,0:T(8,128)S(1)} %get-tuple-element.47.v.v_in, f32[6,2,8,160,128]{4,3,2,1,0:T(8,128)S(1)} %get-tuple-element.48.s.s_in, ...), custom_call_target="tpu_custom_call" | custom-call | flops 6553600 | tf_op jit(solution)/shard_map/pack/pallas_call | solution.py:754
  16.2 0.0 collective-permute-done.2.f_other
  16.2 0.8 %cross.1 = (f32[3,2,9,160,128]{4,3,2,1,0:T(8,128)S(1)}, f32[6,2,8,160,128]{4,3,2,1,0:T(8,128)S(1)}, f32[6,2,8,144,128]{4,3,2,1,0:T(8,128)S(1)}, f32[3,144,128]{2,1,0:T(8,128)S(1)}, f32[3,144,128]{2,1,0:T(8,128)S(1)}) custom-call(s32[3]{0:T(128)S(1)} %pad_add_fusion.flags, ...), custom_call_target="tpu_custom_call", output_to_operand_aliasing={{0}: (4, {}), {1}: (5, {}), {2}: (6, {}), {3}: (7, {}), {4}... | custom-call | flops 1310720 | tf_op jit(solution)/shard_map/cross/pallas_call | solution.py:757
  17.0 0.1 collective-permute-start.3
  17.1 2.5 %collective-permute-start.4 = (f32[3,144,128]{2,1,0:T(8,128)S(1)}, f32[3,144,128]{2,1,0:T(8,128)S(1)}, u32[]{:S(2)}, u32[]{:S(2)}) collective-permute-start(f32[3,144,128]{2,1,0:T(8,128)S(1)} %get-tuple-element.53), channel_id=1, source_target_pairs={{1,2},{2,1},{5,6},{6,5},{9,10},{10,9},{13,14},{14,13},{17,18},{18,... | collective-permute-start | bytes 663560 | tf_op jit(solution)/shard_map/ppermute | solution.py:683
  19.6 0.0 collective-permute-done.3.r_a
  19.6 4.7 %collective-permute-done.4.r_b = f32[3,144,128]{2,1,0:T(8,128)S(1)} collective-permute-done((f32[3,144,128]{2,1,0:T(8,128)S(1)}, f32[3,144,128]{2,1,0:T(8,128)S(1)}, u32[]{:S(2)}, u32[]{:S(2)}) %collective-permute-start.4) | collective-permute-done | bytes 221216 | tf_op jit(solution)/shard_map/ppermute | solution.py:683
  24.3 4.0 %widen.1 = (f32[3,2,9,160,128]{4,3,2,1,0:T(8,128)S(1)}, f32[6,2,8,160,128]{4,3,2,1,0:T(8,128)S(1)}, f32[6,2,8,144,128]{4,3,2,1,0:T(8,128)S(1)}, f32[8,2,16,128]{...) custom-call(s32[3]{0:T(128)S(1)} %pad_add_fusion.flags, ...), custom_call_target="tpu_custom_call", output_to_operand_aliasing={{0}: (5, {}), {1}: (6, {}), {2}: (7, {}), {3}: (8, {})} | custom-call | flops 6553600 | tf_op jit(solution)/shard_map/widen/pallas_call | solution.py:767
  28.4 0.1 collective-permute-start.5
  28.4 1.9 %collective-permute-start.6 = (f32[184,128]{1,0:T(8,128)S(1)}, f32[184,128]{1,0:T(8,128)S(1)}, u32[]{:S(2)}, u32[]{:S(2)}) collective-permute-start(f32[184,128]{1,0:T(8,128)S(1)} %get-tuple-element.58), channel_id=1, source_target_pairs={{4,8},{8,4},{5,9},{9,5},{6,10},{10,6},{7,11},{11,7},{20,24},{24,20... | collective-permute-start | bytes 282632 | tf_op jit(solution)/shard_map/ppermute | solution.py:683
  30.4 3.3 %inner.3 = (f32[3,2,9,160,128]{4,3,2,1,0:T(8,128)S(1)}, f32[6,2,8,160,128]{4,3,2,1,0:T(8,128)S(1)}) custom-call(f32[6,2,8,144,128]{4,3,2,1,0:T(8,128)S(1)} %get-tuple-element.59.m.refs_4_.refs_2_, f32[3,2,9,160,128]{4,3,2,1,0:T(8,128)S(1)} %get-tuple-element.60.v_in, ...), custom_call_target="tpu_custom_call", output_to_operand_aliasing={{0}: (1, {}), {1}: (2, {})} | custom-call | flops 26214400 | tf_op jit(solution)/shard_map/inner/pallas_call | solution.py:781
  33.6 0.0 collective-permute-done.refs_0_
  33.7 0.0 collective-permute-done.1.refs_1_
  33.7 0.0 collective-permute-done.5.refs_2_
  33.7 1.4 %collective-permute-done.6.refs_3_ = f32[184,128]{1,0:T(8,128)S(1)} collective-permute-done((f32[184,128]{1,0:T(8,128)S(1)}, f32[184,128]{1,0:T(8,128)S(1)}, u32[]{:S(2)}, u32[]{:S(2)}) %collective-permute-start.6) | collective-permute-done | bytes 94240 | tf_op jit(solution)/shard_map/ppermute | solution.py:683
  35.1 2.0 %boundary.3 = (f32[3,2,9,160,128]{4,3,2,1,0:T(8,128)S(1)}, f32[6,2,8,160,128]{4,3,2,1,0:T(8,128)S(1)}, f32[8,2,16,128]{3,2,1,0:T(8,128)S(1)}, f32[2,144,128]{2,1...) custom-call(s32[3]{0:T(128)S(1)} %pad_add_fusion.flags, ...), custom_call_target="tpu_custom_call", output_to_operand_aliasing={{0}: (7, {}), {1}: (8, {}), {2}: (9, {})} | custom-call | flops 6553600 | tf_op jit(solution)/shard_map/boundary/pallas_call | solution.py:808
  37.1 0.1 collective-permute-start.7
  37.1 2.6 %collective-permute-start.8 = (f32[544,128]{1,0:T(8,128)S(1)}, f32[544,128]{1,0:T(8,128)S(1)}, u32[]{:S(2)}, u32[]{:S(2)}) collective-permute-start(f32[544,128]{1,0:T(8,128)S(1)} %get-tuple-element.66), channel_id=1, source_target_pairs={{4,8},{8,4},{5,9},{9,5},{6,10},{10,6},{7,11},{11,7},{20,24},{24,20... | collective-permute-start | bytes 835592 | tf_op jit(solution)/shard_map/ppermute | solution.py:683
  39.7 3.9 %inner.4 = (f32[3,2,9,160,128]{4,3,2,1,0:T(8,128)S(1)}, f32[6,2,8,160,128]{4,3,2,1,0:T(8,128)S(1)}) custom-call(f32[6,2,8,144,128]{4,3,2,1,0:T(8,128)S(1)} %get-tuple-element.59.m.refs_4_.refs_2_, f32[3,2,9,160,128]{4,3,2,1,0:T(8,128)S(1)} %get-tuple-element.68.v_in, ...), custom_call_target="tpu_custom_call", output_to_operand_aliasing={{0}: (1, {}), {1}: (2, {})} | custom-call | flops 26214400 | tf_op jit(solution)/shard_map/inner/pallas_call | solution.py:781
  43.6 1.4 %collective-permute-done.7.refs_0_ = f32[544,128]{1,0:T(8,128)S(1)} collective-permute-done((f32[544,128]{1,0:T(8,128)S(1)}, f32[544,128]{1,0:T(8,128)S(1)}, u32[]{:S(2)}, u32[]{:S(2)}) %collective-permute-start.7) | collective-permute-done | bytes 278560 | tf_op jit(solution)/shard_map/ppermute | solution.py:683
  45.0 1.9 %collective-permute-done.8.refs_1_ = f32[544,128]{1,0:T(8,128)S(1)} collective-permute-done((f32[544,128]{1,0:T(8,128)S(1)}, f32[544,128]{1,0:T(8,128)S(1)}, u32[]{:S(2)}, u32[]{:S(2)}) %collective-permute-start.8) | collective-permute-done | bytes 278560 | tf_op jit(solution)/shard_map/ppermute | solution.py:683
  46.9 1.9 %boundary.4 = (f32[3,2,9,160,128]{4,3,2,1,0:T(8,128)S(1)}, f32[6,2,8,160,128]{4,3,2,1,0:T(8,128)S(1)}, f32[8,2,16,128]{3,2,1,0:T(8,128)S(1)}, f32[544,128]{1,0:T(8,128)S(1)}, f32[544,128]{1,0:T(8,128)S(1)}) custom-call(s32[3]{0:T(128)S(1)} %pad_add_fusion.flags, ...), custom_call_target="tpu_custom_call", output_to_operand_aliasing={{0}: (6, {}), {1}: (7, {}), {2}: (8, {})} | custom-call | flops 6553600 | tf_op jit(solution)/shard_map/boundary/pallas_call | solution.py:808
  48.9 0.1 collective-permute-start.9
  48.9 1.9 %collective-permute-start.10 = (f32[544,128]{1,0:T(8,128)S(1)}, f32[544,128]{1,0:T(8,128)S(1)}, u32[]{:S(2)}, u32[]{:S(2)}) collective-permute-start(f32[544,128]{1,0:T(8,128)S(1)} %get-tuple-element.74), channel_id=1, source_target_pairs={{4,8},{8,4},{5,9},{9,5},{6,10},{10,6},{7,11},{11,7},{20,24},{24,20... | collective-permute-start | bytes 835592 | tf_op jit(solution)/shard_map/ppermute | solution.py:683
  50.9 5.2 %inner.5 = (f32[3,2,9,160,128]{4,3,2,1,0:T(8,128)S(1)}, f32[6,2,8,160,128]{4,3,2,1,0:T(8,128)S(1)}, f32[3,8,128,128]{3,2,1,0:T(8,128)}, f32[6,8,128,128]{3,2,1,0:T(8,128)}) custom-call(f32[6,2,8,144,128]{4,3,2,1,0:T(8,128)S(1)} %get-tuple-element.59.m.refs_4_.refs_2_, ...), custom_call_target="tpu_custom_call", output_to_operand_aliasing={{0}: (1, {}), {1}: (2, {})} | custom-call | flops 26214400 | tf_op jit(solution)/shard_map/inner/pallas_call | solution.py:781
  56.1 0.0 collective-permute-done.9.refs_0_
  56.1 1.2 %collective-permute-done.10.refs_1_ = f32[544,128]{1,0:T(8,128)S(1)} collective-permute-done((f32[544,128]{1,0:T(8,128)S(1)}, f32[544,128]{1,0:T(8,128)S(1)}, u32[]{:S(2)}, u32[]{:S(2)}) %collective-permute-start.10) | collective-permute-done | bytes 278560 | tf_op jit(solution)/shard_map/ppermute | solution.py:683
  57.4 4.0 %boundary.5 = (f32[3,2,9,160,128]{4,3,2,1,0:T(8,128)S(1)}, f32[6,2,8,160,128]{4,3,2,1,0:T(8,128)S(1)}, f32[8,2,16,128]{3,2,1,0:T(8,128)S(1)}, f32[3,8,128,128]{3...) custom-call(s32[3]{0:T(128)S(1)} %pad_add_fusion.flags, ...), custom_call_target="tpu_custom_call", output_to_operand_aliasing={{0}: (6, {}), {1}: (7, {}), {2}: (8, {}), {3}: (9, {}), {4}... | custom-call | flops 6553600 | tf_op jit(solution)/shard_map/boundary/pallas_call | solution.py:808
  (6 shorter events, 0.0 us)
Async XLA Ops:
  2.5 13.8 %collective-permute-start.2 = (f32[15,4,8,128]{3,2,1,0:T(8,128)S(1)}, f32[15,4,8,128]{3,2,1,0:T(8,128)S(1)}, u32[]{:S(2)}, u32[]{:S(2)}) collective-permute-start(f32[15,4,8,128]{3,2,1,0:T(8,128)S(1)} %edge.1), channel_id=1, source_target_pairs={{0,16},{16,0},{1,17},{17,1},{2,18},{18,2},{3,19},{19,3},{4,20},{20... | collective-permute-start | bytes 737288 | tf_op jit(solution)/shard_map/ppermute | solution.py:733
  8.2 25.5 %collective-permute-start = (f32[4,128,128]{2,1,0:T(8,128)S(1)}, f32[4,128,128]{2,1,0:T(8,128)S(1)}, u32[]{:S(2)}, u32[]{:S(2)}) collective-permute-start(f32[4,128,128]{2,1,0:T(8,128)S(1)} %get-tuple-element.44), channel_id=1, source_target_pairs={{0,4},{4,0},{8,12},{12,8},{1,5},{5,1},{9,13},{13,9},{2,6},{6,2},{1... | collective-permute-start | bytes 786440 | tf_op jit(solution)/shard_map/ppermute | solution.py:683
  8.7 25.0 %collective-permute-start.1 = (f32[4,128,128]{2,1,0:T(8,128)S(1)}, f32[4,128,128]{2,1,0:T(8,128)S(1)}, u32[]{:S(2)}, u32[]{:S(2)}) collective-permute-start(f32[4,128,128]{2,1,0:T(8,128)S(1)} %get-tuple-element.45), channel_id=1, source_target_pairs={{4,8},{8,4},{5,9},{9,5},{6,10},{10,6},{7,11},{11,7},{20,24},{24,20... | collective-permute-start | bytes 786440 | tf_op jit(solution)/shard_map/ppermute | solution.py:683
  17.0 2.6 %collective-permute-start.3 = (f32[3,144,128]{2,1,0:T(8,128)S(1)}, f32[3,144,128]{2,1,0:T(8,128)S(1)}, u32[]{:S(2)}, u32[]{:S(2)}) collective-permute-start(f32[3,144,128]{2,1,0:T(8,128)S(1)} %get-tuple-element.52), channel_id=1, source_target_pairs={{0,1},{1,0},{2,3},{3,2},{4,5},{5,4},{6,7},{7,6},{8,9},{9,8},{10,11... | collective-permute-start | bytes 663560 | tf_op jit(solution)/shard_map/ppermute | solution.py:683
  17.1 7.3 %collective-permute-start.4 = (f32[3,144,128]{2,1,0:T(8,128)S(1)}, f32[3,144,128]{2,1,0:T(8,128)S(1)}, u32[]{:S(2)}, u32[]{:S(2)}) collective-permute-start(f32[3,144,128]{2,1,0:T(8,128)S(1)} %get-tuple-element.53), channel_id=1, source_target_pairs={{1,2},{2,1},{5,6},{6,5},{9,10},{10,9},{13,14},{14,13},{17,18},{18,... | collective-permute-start | bytes 663560 | tf_op jit(solution)/shard_map/ppermute | solution.py:683
  28.4 5.3 %collective-permute-start.5 = (f32[184,128]{1,0:T(8,128)S(1)}, f32[184,128]{1,0:T(8,128)S(1)}, u32[]{:S(2)}, u32[]{:S(2)}) collective-permute-start(f32[184,128]{1,0:T(8,128)S(1)} %get-tuple-element.57), channel_id=1, source_target_pairs={{0,4},{4,0},{8,12},{12,8},{1,5},{5,1},{9,13},{13,9},{2,6},{6,2},{1... | collective-permute-start | bytes 282632 | tf_op jit(solution)/shard_map/ppermute | solution.py:683
  28.4 6.6 %collective-permute-start.6 = (f32[184,128]{1,0:T(8,128)S(1)}, f32[184,128]{1,0:T(8,128)S(1)}, u32[]{:S(2)}, u32[]{:S(2)}) collective-permute-start(f32[184,128]{1,0:T(8,128)S(1)} %get-tuple-element.58), channel_id=1, source_target_pairs={{4,8},{8,4},{5,9},{9,5},{6,10},{10,6},{7,11},{11,7},{20,24},{24,20... | collective-permute-start | bytes 282632 | tf_op jit(solution)/shard_map/ppermute | solution.py:683
  37.1 7.9 %collective-permute-start.7 = (f32[544,128]{1,0:T(8,128)S(1)}, f32[544,128]{1,0:T(8,128)S(1)}, u32[]{:S(2)}, u32[]{:S(2)}) collective-permute-start(f32[544,128]{1,0:T(8,128)S(1)} %get-tuple-element.65), channel_id=1, source_target_pairs={{0,4},{4,0},{8,12},{12,8},{1,5},{5,1},{9,13},{13,9},{2,6},{6,2},{1... | collective-permute-start | bytes 835592 | tf_op jit(solution)/shard_map/ppermute | solution.py:683
  37.1 9.8 %collective-permute-start.8 = (f32[544,128]{1,0:T(8,128)S(1)}, f32[544,128]{1,0:T(8,128)S(1)}, u32[]{:S(2)}, u32[]{:S(2)}) collective-permute-start(f32[544,128]{1,0:T(8,128)S(1)} %get-tuple-element.66), channel_id=1, source_target_pairs={{4,8},{8,4},{5,9},{9,5},{6,10},{10,6},{7,11},{11,7},{20,24},{24,20... | collective-permute-start | bytes 835592 | tf_op jit(solution)/shard_map/ppermute | solution.py:683
  48.9 7.3 %collective-permute-start.9 = (f32[544,128]{1,0:T(8,128)S(1)}, f32[544,128]{1,0:T(8,128)S(1)}, u32[]{:S(2)}, u32[]{:S(2)}) collective-permute-start(f32[544,128]{1,0:T(8,128)S(1)} %get-tuple-element.73), channel_id=1, source_target_pairs={{0,4},{4,0},{8,12},{12,8},{1,5},{5,1},{9,13},{13,9},{2,6},{6,2},{1... | collective-permute-start | bytes 835592 | tf_op jit(solution)/shard_map/ppermute | solution.py:683
  48.9 8.4 %collective-permute-start.10 = (f32[544,128]{1,0:T(8,128)S(1)}, f32[544,128]{1,0:T(8,128)S(1)}, u32[]{:S(2)}, u32[]{:S(2)}) collective-permute-start(f32[544,128]{1,0:T(8,128)S(1)} %get-tuple-element.74), channel_id=1, source_target_pairs={{4,8},{8,4},{5,9},{9,5},{6,10},{10,6},{7,11},{11,7},{20,24},{24,20... | collective-permute-start | bytes 835592 | tf_op jit(solution)/shard_map/ppermute | solution.py:683

commit v4 on v3

--- a/solution.py
+++ b/solution.py
@@ -169,17 +169,17 @@
                 copy.wait()
 
 
-def load_kernel(flags, velocity, stress, *rest):
+def load_kernel(flags, thirds, velocity, stress, *rest):
     raw_m, small = rest[:6], rest[6:13]
-    v, s, m, fault, y_a, y_b = rest[13:19]
+    v, s, m, fault, z_a, z_b = rest[13:19]
     pre, ids, mask, rate, slip, region_a, region_normal, sems = rest[19:]
     ny, nx, width = velocity.shape[1:]
     cross = cross_row(nx)
     big = {}
+    for c in range(3):
+        big["v", c] = (velocity.at[c], v.at[c, 0, pl.ds(0, ny), pl.ds(PAD, nx), :])
     for c in range(6):
         big["s", c] = (stress.at[c], s.at[c, 0, :, pl.ds(PAD, nx), :])
-    for c in range(3):
-        big["v", c] = (velocity.at[c], v.at[c, 0, pl.ds(0, ny), pl.ds(PAD, nx), :])
     for c in range(6):
         big["m", c] = (raw_m[c], m.at[c, 0, :, pl.ds(0, nx), :])
     big = {
@@ -203,6 +203,21 @@
             for c in range(3):
                 v[c, t, y, PAD + nx : PAD + nx + PAD, :] = zeros
                 v[c, t, y, PAD + cross + 8 : 2 * PAD + cross + 8, :] = zeros
+
+    per_plane = fields_per_plane(ny, width)
+    odd = flags[2] == 1
+    group = thirds[...]
+    for plane in range(z_slots(ny, width)[1]):
+        for key in FIELDS[plane * per_plane : (plane + 1) * per_plane]:
+            big[key].wait()
+
+        def pack(i, carry, plane=plane):
+            for part in range(UNROLL):
+                row = pl.multiple_of((i * UNROLL + part) * 8, 8)
+                z_emit(z_a, z_b, odd, group, z_pieces(plane, v, s, m, row), plane, row)
+            return carry
+
+        lax.fori_loop(0, nx // (8 * UNROLL), pack, 0)
     for copy in little:
         copy.wait()
     kinds = ids[...]
@@ -217,15 +232,17 @@
     fault[STRENGTH, 0, 0:ny, :] = a_part * n_part
     fault[RATE, 0, 0:ny, :] = rate[...]
     fault[SLIP, 0, 0:ny, :] = slip[...]
-    for copy in big.values():
-        copy.wait()
-
+
+
+def early_kernel(flags, v, s, m, y_a, y_b):
+    ny, width = m.shape[2], m.shape[4]
+    nx = m.shape[3] - 16
     odd = flags[1] == 1
     lanes = lane_index((8, width))
     first = lanes == 0
-    last = ny - 1
-    for row in range(0, nx, 8):
-        up = [at(s, c, 0, last, row) for c in ALONG_Y]
+    span = nx + 8
+    for row in row_tiles(nx):
+        up = [at(s, c, 0, ny - 1, row) for c in ALONG_Y]
         own = {c: at(s, c, 0, 0, row) for c in range(6)}
         behind = {c: jnp.where(first, 0.0, roll(own[c], 1)) for c in (XZ, YZ, ZZ)}
         lower_x = {c: own[c] - at(s, c, 0, 0, row - 1) for c in (XX, XY, XZ)}
@@ -235,12 +252,18 @@
             lower_x[XY] + own[YY] + (own[YZ] - behind[YZ]),
             lower_x[XZ] + own[YZ] + (own[ZZ] - behind[ZZ]),
         )
+        at_row = packed_row(row, nx)
         for c in range(3):
             down = at(v, c, 0, 0, row) + DT * buoyancy * total[c]
-            y_a[c, pl.ds(row, 8), :] = jnp.where(odd, down, up[c])
-            y_b[c, pl.ds(row, 8), :] = jnp.where(odd, up[c], down)
-        y_a[3, pl.ds(row, 8), :] = buoyancy
-        y_b[3, pl.ds(row, 8), :] = buoyancy
+            to = pl.ds(c * span + at_row, 8)
+            y_a[to, :] = jnp.where(odd, down, up[c])
+            y_b[to, :] = jnp.where(odd, up[c], down)
+        to = pl.ds(3 * span + at_row, 8)
+        y_a[to, :] = buoyancy
+        y_b[to, :] = buoyancy
+
+
+UNROLL = 4
 
 
 def z_emit(z_a, z_b, odd, group, pieces, plane, row):
@@ -264,26 +287,6 @@
         for y in range(ny):
             pieces.append((f * ny + y, ref[c, 0, y, pl.ds(row + shift, 8), :]))
     return pieces
-
-
-UNROLL = 4
-
-
-def pack_kernel(flags, thirds, v, s, m, z_a, z_b):
-    ny, width = m.shape[2], m.shape[4]
-    nx = z_a.shape[1] - 16
-    planes = z_slots(ny, width)[1]
-    odd = flags[2] == 1
-    group = thirds[...]
-
-    def pack(i, carry):
-        for part in range(UNROLL):
-            row = pl.multiple_of((i * UNROLL + part) * 8, 8)
-            for plane in range(planes):
-                z_emit(z_a, z_b, odd, group, z_pieces(plane, v, s, m, row), plane, row)
-        return carry
-
-    lax.fori_loop(0, nx // (8 * UNROLL), pack, 0)
 
 
 def cross_kernel(flags, thirds, f_other, fault, v_in, s_in, m_in, za_in, zb_in, v, s, m, z_a, z_b):
@@ -339,22 +342,32 @@
                 v[c, t, 0, pl.ds(PAD + row, 8), :] = new[t][c]
 
 
-def widen_kernel(flags, thirds, eighths, r_a, r_b, v_in, s_in, m_in, f_in, v, s, m, fault, y_a, y_b):
+class ZHalo:
+    def __init__(self, odd, group, r_a, r_b, planes):
+        self.odd, self.group, self.r_a, self.r_b, self.planes = odd, group, r_a, r_b, planes
+
+    def take(self, row, wanted):
+        for plane in range(self.planes):
+            chosen = [(pos, store) for (p, pos), store in wanted if p == plane]
+            if chosen:
+                from_a = self.r_a[plane, pl.ds(row, 8), :]
+                from_b = self.r_b[plane, pl.ds(row, 8), :]
+                low = jnp.where(self.odd, from_a, from_b)
+                high = jnp.where(self.odd, from_b, from_a)
+                for pos, store in chosen:
+                    both = jnp.where(self.group == pos, low, high)
+                    store(roll(both, -(HALO * pos + HALO)))
+
+
+def needed_first(kind, c, y, ny):
+    if y == 0:
+        return kind != "m" or c == B
+    return y == ny - 1 and kind == "s" and c in ALONG_Y
+
+
+def unpack_fields(halo, v, s, m, nx, first):
     ny, width = m.shape[2], m.shape[4]
-    nx = r_a.shape[1] - 16
-    cross = cross_row(nx)
-    slots, planes = z_slots(ny, width)
-    odd_z, odd_y = flags[2] == 1, flags[1] == 1
-    lanes = lane_index((8, width))
-    group = thirds[...]
-
-    def take(row, wanted):
-        from_a = [r_a[p, pl.ds(row, 8), :] for p in range(planes)]
-        from_b = [r_b[p, pl.ds(row, 8), :] for p in range(planes)]
-        low = [jnp.where(odd_z, a, b) for a, b in zip(from_a, from_b)]
-        high = [jnp.where(odd_z, b, a) for a, b in zip(from_a, from_b)]
-        for (plane, pos), store in wanted:
-            store(roll(jnp.where(group == pos, low[plane], high[plane]), -(HALO * pos + HALO)))
+    slots = z_slots(ny, width)[0]
 
     def store_to(ref, c, y, row):
         def store(value):
@@ -368,17 +381,35 @@
             shift = 0 if kind == "m" else PAD
             ref = field_ref(kind, v, s, m)
             for y in range(ny):
-                wanted.append((slots[f, y], store_to(ref, c, y, row + shift)))
+                if needed_first(kind, c, y, ny) == first:
+                    wanted.append((slots[f, y], store_to(ref, c, y, row + shift)))
         return wanted
 
     def unpack(i, carry):
         for part in range(UNROLL):
             row = pl.multiple_of((i * UNROLL + part) * 8, 8)
-            take(row, fields(row))
+            halo.take(row, fields(row))
         return carry
 
     lax.fori_loop(0, nx // (8 * UNROLL), unpack, 0)
-    take(nx, fields(cross))
+    halo.take(nx, fields(cross_row(nx)))
+
+
+def rest_kernel(flags, thirds, r_a, r_b, v_in, s_in, m_in, v, s, m):
+    nx = r_a.shape[1] - 16
+    planes = z_slots(m.shape[2], m.shape[4])[1]
+    halo = ZHalo(flags[2] == 1, thirds[...], r_a, r_b, planes)
+    unpack_fields(halo, v, s, m, nx, False)
+
+
+def widen_kernel(flags, thirds, eighths, r_a, r_b, v_in, s_in, m_in, f_in, v, s, m, fault, y_a, y_b):
+    ny, width = m.shape[2], m.shape[4]
+    nx = r_a.shape[1] - 16
+    planes = z_slots(ny, width)[1]
+    odd_y = flags[1] == 1
+    lanes = lane_index((8, width))
+    halo = ZHalo(flags[2] == 1, thirds[...], r_a, r_b, planes)
+    unpack_fields(halo, v, s, m, nx, True)
 
     def store_fault(k):
         def store(value):
@@ -386,7 +417,7 @@
 
         return store
 
-    take(nx + 8, [((0, k), store_fault(k)) for k in range(6)])
+    halo.take(nx + 8, [((0, k), store_fault(k)) for k in range(6)])
     partial_trials(v, s, m, nx, lanes)
     last = ny - 1
     halos = eighths[...]
@@ -401,17 +432,10 @@
         to = pl.ds(packed_row(row, nx), 8)
         y_a[to, :] = jnp.where(odd_y, down, up)
         y_b[to, :] = jnp.where(odd_y, up, down)
-    up = [at(s, c, 0, last, cross) for c in ALONG_Y]
-    down = [at(v, c, 0, 0, cross) for c in range(3)]
-    buoyancy = m[B, 0, 0, pl.ds(cross, 8), :]
-    for c in range(4):
-        to = pl.ds(nx + 8 + 8 * c, 8)
-        y_a[to, :] = buoyancy if c == 3 else jnp.where(odd_y, down[c], up[c])
-        y_b[to, :] = buoyancy if c == 3 else jnp.where(odd_y, up[c], down[c])
     for t in range(2):
         for k in range(8):
             line = fault[min(k, 5), t, 0:1, :]
-            row = nx + 40 + 8 * t + k
+            row = nx + 8 + 8 * t + k
             y_a[row : row + 1, :] = line
             y_b[row : row + 1, :] = line
 
@@ -502,17 +526,13 @@
             from_a = [r_a[pl.ds(k * span + at_row, 8), :] for k in range(4)]
             from_b = [r_b[pl.ds(k * span + at_row, 8), :] for k in range(4)]
         else:
-            if row < nx:
-                from_a = [early_a[k, pl.ds(row, 8), :] for k in range(4)]
-                from_b = [early_b[k, pl.ds(row, 8), :] for k in range(4)]
-            else:
-                from_a = [r_a[pl.ds(span + 8 * k, 8), :] for k in range(4)]
-                from_b = [r_b[pl.ds(span + 8 * k, 8), :] for k in range(4)]
+            from_a = [early_a[pl.ds(k * span + at_row, 8), :] for k in range(4)]
+            from_b = [early_b[pl.ds(k * span + at_row, 8), :] for k in range(4)]
             from_a.append(r_a[pl.ds(at_row, 8), :])
             from_b.append(r_b[pl.ds(at_row, 8), :])
         low = [jnp.where(odd, a, b) for a, b in zip(from_a, from_b)]
         high = [jnp.where(odd, b, a) for a, b in zip(from_a, from_b)]
-        if first and row < nx:
+        if first:
             for c in range(3):
                 column = roll(high[-1], -(STRIP * c + 2 * HALO))
                 high[c] = jnp.where(lanes == 0, column, high[c])
@@ -520,7 +540,7 @@
 
     if first:
         for t in range(2):
-            to = pl.ds(span + 32 + 8 * t, 8)
+            to = pl.ds(span + 8 * t, 8)
             lines = jnp.where(odd, r_b[to, :], r_a[to, :])
             for k in range(6):
                 fault[k, t, ny : ny + 1, :] = lines[k : k + 1, :]
@@ -731,12 +751,11 @@
         flops=unit,
     )(flags, *raw[:8])
     f_other = lax.ppermute(f_own, "gx", [(i, i ^ 1) for i in range(lax.axis_size("gx"))])
-    y_shape = f32(4, nx, width)
-    v, s, m, fault, early_a, early_b = call(
+    v, s, m, fault, z_a, z_b = call(
         load_kernel,
         "load",
-        (v_shape, s_shape, m_shape, fault_shape, y_shape, y_shape),
-        [sm] + [hb] * 15,
+        (v_shape, s_shape, m_shape, fault_shape, z_shape, z_shape),
+        [sm, vm] + [hb] * 15,
         {},
         [
             pltpu.VMEM(prestress.shape, jnp.float32),
@@ -749,11 +768,7 @@
             pltpu.SemaphoreType.DMA((22,)),
         ],
         flops=100 * unit,
-    )(flags, *raw)
-    early_a, early_b = pair_swaps(early_a, early_b, "gy")
-    z_a, z_b = call(
-        pack_kernel, "pack", (z_shape, z_shape), [sm] + [vm] * 4, {}, flops=50 * unit
-    )(flags, thirds, v, s, m)
+    )(flags, thirds, *raw)
     v, s, m, z_a, z_b = call(
         cross_kernel,
         "cross",
@@ -763,7 +778,12 @@
         flops=10 * unit,
     )(flags, thirds, f_other, fault, v, s, m, z_a, z_b)
     z_a, z_b = pair_swaps(z_a, z_b, "gz")
-    y_shape = f32(nx + 8 + 32 + 16, width)
+    y_shape = f32(4 * (nx + 8), width)
+    early_a, early_b = call(
+        early_kernel, "early", (y_shape, y_shape), [sm] + [vm] * 3, {}, flops=10 * unit
+    )(flags, v, s, m)
+    early_a, early_b = pair_swaps(early_a, early_b, "gy")
+    y_shape = f32(nx + 8 + 16, width)
     v, s, m, fault, y_a, y_b = call(
         widen_kernel,
         "widen",
@@ -772,6 +792,14 @@
         {5: 0, 6: 1, 7: 2, 8: 3},
         flops=50 * unit,
     )(flags, thirds, eighths, z_a, z_b, v, s, m, fault)
+    v, s, m = call(
+        rest_kernel,
+        "rest",
+        (v_shape, s_shape, m_shape),
+        [sm] + [vm] * 6,
+        {4: 0, 5: 1, 6: 2},
+        flops=50 * unit,
+    )(flags, thirds, z_a, z_b, v, s, m)
     y_shape = f32(4 * (nx + 8), width)
     ahead_b = None
     out_shapes = (HBM((3, ny, nx, width), jnp.float32), HBM((6, ny, nx, width), jnp.float32))

time: 61.7 us -> 58 us (0.940)
  the two profiles are of different devices: /device:TPU:10 before, /device:TPU:21 now
where the time goes in v4:
time: 58 us; the launch traced here: 57.8 us
  Pallas kernels  33.1 us (57%)
  starting transfers between devices  17.3 us (30%)
  waiting for transfers between devices  6.35 us (11%)
  between operations  0.85 us (1%)
    ppermute x10, starting transfers between devices, pair_swaps(): out.append(lax.ppermute(value, axis, pairs))  17 us
    pallas_call x3, Pallas kernels, local(): call(functools.partial(inner_kernel, first, final), 'inner', (v_shape, s_...  11.8 us
    pallas_call x3, Pallas kernels, local(): call(functools.partial(boundary_kernel, first, final), 'boundary', shapes...  8 us
    pallas_call x1, Pallas kernels, local(): call(load_kernel, 'load', (v_shape, s_shape, m_shape, fault_shape, z_shap...  5.36 us
    ppermute x10, waiting for transfers between devices, pair_swaps(): out.append(lax.ppermute(value, axis, pairs))  5.14 us
    pallas_call x1, Pallas kernels, local(): call(rest_kernel, 'rest', (v_shape, s_shape, m_shape), [sm] + [vm] * 6, {...  2.79 us
    pallas_call x1, Pallas kernels, local(): call(widen_kernel, 'widen', (v_shape, s_shape, m_shape, fault_shape, y_sh...  2.03 us
    pallas_call x1, Pallas kernels, local(): call(edge_kernel, 'edge', (f_shape,), [sm] + [hb] * 8, {}, [pltpu.Semapho...  1.74 us
  transfers between devices with their start and end apart: 11, of which 6 were waited for; matrix products, arithmetic and copies ran while one was open for 0% of the time, Pallas kernels for 39%

profile of v4, /device:TPU:21, one launch (start us, length us, event | category | flops | bytes accessed | tf_op | source)
XLA Modules:
  0.0 57.8 jit_solution(10908561935830662551)
XLA Ops:
  0.6 0.1 pad_add_fusion.flags
  0.7 1.7 %edge.1 = f32[15,4,8,128]{3,2,1,0:T(8,128)S(1)} custom-call(s32[3]{0:T(128)S(1)} %pad_add_fusion.flags, f32[3,8,128,128]{3,2,1,0:T(8,128)} %velocity.3, f32[6,8,128,128]{3,2,1,0:T(8,128)} %stress.3, f32[8,128,128]{2,1,0:T(8,128)} %rest_0_.3, f32[8,128,128]{2,1,0:T(8,128)} %rest_1_.3, f32[8,128,128]{2,1,0:T(8,128)} %rest_2_.3, f32[8,128,128]{2,1,0:T(8,128)} %rest_3_.3, ...), custom_call_target="tpu_custom_call" | custom-call | flops 131072 | tf_op jit(solution)/shard_map/edge/pallas_call | solution.py:744
  2.5 0.3 collective-permute-start
  2.8 5.4 %load.1 = (f32[3,2,9,160,128]{4,3,2,1,0:T(8,128)S(1)}, f32[6,2,8,160,128]{4,3,2,1,0:T(8,128)S(1)}, f32[6,2,8,144,128]{4,3,2,1,0:T(8,128)S(1)}, f32[8,2,16,128]{3...) custom-call(s32[3]{0:T(128)S(1)} %pad_add_fusion.flags, ...), custom_call_target="tpu_custom_call" | custom-call | flops 13107200 | tf_op jit(solution)/shard_map/load/pallas_call | solution.py:754
  8.2 1.2 %collective-permute-done.f_other = f32[15,4,8,128]{3,2,1,0:T(8,128)S(1)} collective-permute-done((f32[15,4,8,128]{3,2,1,0:T(8,128)S(1)}, f32[15,4,8,128]{3,2,1,0:T(8,128)S(1)}, u32[]{:S(2)}, u32[]{:S(2)}) %collective-permute-start) | collective-permute-done | bytes 245792 | tf_op jit(solution)/shard_map/ppermute | solution.py:753
  9.4 0.8 %cross.1 = (f32[3,2,9,160,128]{4,3,2,1,0:T(8,128)S(1)}, f32[6,2,8,160,128]{4,3,2,1,0:T(8,128)S(1)}, f32[6,2,8,144,128]{4,3,2,1,0:T(8,128)S(1)}, f32[3,144,128]{2,1,0:T(8,128)S(1)}, f32[3,144,128]{2,1,0:T(8,128)S(1)}) custom-call(s32[3]{0:T(128)S(1)} %pad_add_fusion.flags, ...), custom_call_target="tpu_custom_call", output_to_operand_aliasing={{0}: (4, {}), {1}: (5, {}), {2}: (6, {}), {3}: (7, {}), {4}... | custom-call | flops 1310720 | tf_op jit(solution)/shard_map/cross/pallas_call | solution.py:772
  10.1 1.6 %collective-permute-start.3 = (f32[3,144,128]{2,1,0:T(8,128)S(1)}, f32[3,144,128]{2,1,0:T(8,128)S(1)}, u32[]{:S(2)}, u32[]{:S(2)}) collective-permute-start(f32[3,144,128]{2,1,0:T(8,128)S(1)} %get-tuple-element.58), channel_id=1, source_target_pairs={{0,1},{1,0},{2,3},{3,2},{4,5},{5,4},{6,7},{7,6},{8,9},{9,8},{10,11... | collective-permute-start | bytes 663560 | tf_op jit(solution)/shard_map/ppermute | solution.py:703
  11.7 3.0 %collective-permute-start.4 = (f32[3,144,128]{2,1,0:T(8,128)S(1)}, f32[3,144,128]{2,1,0:T(8,128)S(1)}, u32[]{:S(2)}, u32[]{:S(2)}) collective-permute-start(f32[3,144,128]{2,1,0:T(8,128)S(1)} %get-tuple-element.59), channel_id=1, source_target_pairs={{1,2},{2,1},{5,6},{6,5},{9,10},{10,9},{13,14},{14,13},{17,18},{18,... | collective-permute-start | bytes 663560 | tf_op jit(solution)/shard_map/ppermute | solution.py:703
  14.8 0.7 %early.1 = (f32[544,128]{1,0:T(8,128)S(1)}, f32[544,128]{1,0:T(8,128)S(1)}) custom-call(s32[3]{0:T(128)S(1)} %pad_add_fusion.flags, f32[3,2,9,160,128]{4,3,2,1,0:T(8,128)S(1)} %get-tuple-element.53.v.v_in, f32[6,2,8,160,128]{4,3,2,1,0:T(8,128)S(1)} %get-tuple-element.54.s.s_in, f32[6,2,8,144,128]{4,3,2,1,0:T(8,128)S(1)} %get-tuple-element.55.m.m_in), custom_call_target="tpu_custom_call" | custom-call | flops 1310720 | tf_op jit(solution)/shard_map/early/pallas_call | solution.py:782
  15.5 1.4 %collective-permute-start.1 = (f32[544,128]{1,0:T(8,128)S(1)}, f32[544,128]{1,0:T(8,128)S(1)}, u32[]{:S(2)}, u32[]{:S(2)}) collective-permute-start(f32[544,128]{1,0:T(8,128)S(1)} %get-tuple-element.56), channel_id=1, source_target_pairs={{0,4},{4,0},{8,12},{12,8},{1,5},{5,1},{9,13},{13,9},{2,6},{6,2},{1... | collective-permute-start | bytes 835592 | tf_op jit(solution)/shard_map/ppermute | solution.py:703
  16.8 1.9 %collective-permute-start.2 = (f32[544,128]{1,0:T(8,128)S(1)}, f32[544,128]{1,0:T(8,128)S(1)}, u32[]{:S(2)}, u32[]{:S(2)}) collective-permute-start(f32[544,128]{1,0:T(8,128)S(1)} %get-tuple-element.57), channel_id=1, source_target_pairs={{4,8},{8,4},{5,9},{9,5},{6,10},{10,6},{7,11},{11,7},{20,24},{24,20... | collective-permute-start | bytes 835592 | tf_op jit(solution)/shard_map/ppermute | solution.py:703
  18.7 0.0 collective-permute-done.3.r_a
  18.8 0.5 collective-permute-done.4.r_b
  19.3 2.0 %widen.1 = (f32[3,2,9,160,128]{4,3,2,1,0:T(8,128)S(1)}, f32[6,2,8,160,128]{4,3,2,1,0:T(8,128)S(1)}, f32[6,2,8,144,128]{4,3,2,1,0:T(8,128)S(1)}, f32[8,2,16,128]{...) custom-call(s32[3]{0:T(128)S(1)} %pad_add_fusion.flags, ...), custom_call_target="tpu_custom_call", output_to_operand_aliasing={{0}: (5, {}), {1}: (6, {}), {2}: (7, {}), {3}: (8, {})} | custom-call | flops 6553600 | tf_op jit(solution)/shard_map/widen/pallas_call | solution.py:787
  21.3 1.4 %collective-permute-start.5 = (f32[152,128]{1,0:T(8,128)S(1)}, f32[152,128]{1,0:T(8,128)S(1)}, u32[]{:S(2)}, u32[]{:S(2)}) collective-permute-start(f32[152,128]{1,0:T(8,128)S(1)} %get-tuple-element.60), channel_id=1, source_target_pairs={{0,4},{4,0},{8,12},{12,8},{1,5},{5,1},{9,13},{13,9},{2,6},{6,2},{1... | collective-permute-start | bytes 233480 | tf_op jit(solution)/shard_map/ppermute | solution.py:703
  22.7 1.9 %collective-permute-start.6 = (f32[152,128]{1,0:T(8,128)S(1)}, f32[152,128]{1,0:T(8,128)S(1)}, u32[]{:S(2)}, u32[]{:S(2)}) collective-permute-start(f32[152,128]{1,0:T(8,128)S(1)} %get-tuple-element.61), channel_id=1, source_target_pairs={{4,8},{8,4},{5,9},{9,5},{6,10},{10,6},{7,11},{11,7},{20,24},{24,20... | collective-permute-start | bytes 233480 | tf_op jit(solution)/shard_map/ppermute | solution.py:703
  24.6 2.8 %rest.1 = (f32[3,2,9,160,128]{4,3,2,1,0:T(8,128)S(1)}, f32[6,2,8,160,128]{4,3,2,1,0:T(8,128)S(1)}, f32[6,2,8,144,128]{4,3,2,1,0:T(8,128)S(1)}) custom-call(s32[3]{0:T(128)S(1)} %pad_add_fusion.flags, s32[8,128]{1,0:T(8,128)S(1)} %broadcast_select_fusion.thirds, ...), custom_call_target="tpu_custom_call", output_to_operand_aliasing={{0}: (4, {}), {1}: (5, {}), {2}: (6, {})} | custom-call | flops 6553600 | tf_op jit(solution)/shard_map/rest/pallas_call | solution.py:795
  27.4 3.1 %inner.3 = (f32[3,2,9,160,128]{4,3,2,1,0:T(8,128)S(1)}, f32[6,2,8,160,128]{4,3,2,1,0:T(8,128)S(1)}) custom-call(f32[6,2,8,144,128]{4,3,2,1,0:T(8,128)S(1)} %get-tuple-element.65.m.refs_4_.refs_2_, f32[3,2,9,160,128]{4,3,2,1,0:T(8,128)S(1)} %get-tuple-element.66.v_in, ...), custom_call_target="tpu_custom_call", output_to_operand_aliasing={{0}: (1, {}), {1}: (2, {})} | custom-call | flops 26214400 | tf_op jit(solution)/shard_map/inner/pallas_call | solution.py:809
  30.5 0.0 collective-permute-done.1.refs_0_
  30.5 0.0 collective-permute-done.2.refs_1_
  30.5 0.0 collective-permute-done.5.refs_2_
  30.5 0.0 collective-permute-done.6.refs_3_
  30.5 2.0 %boundary.3 = (f32[3,2,9,160,128]{4,3,2,1,0:T(8,128)S(1)}, f32[6,2,8,160,128]{4,3,2,1,0:T(8,128)S(1)}, f32[8,2,16,128]{3,2,1,0:T(8,128)S(1)}, f32[2,144,128]{2,1...) custom-call(s32[3]{0:T(128)S(1)} %pad_add_fusion.flags, ...), custom_call_target="tpu_custom_call", output_to_operand_aliasing={{0}: (7, {}), {1}: (8, {}), {2}: (9, {})} | custom-call | flops 6553600 | tf_op jit(solution)/shard_map/boundary/pallas_call | solution.py:836
  32.6 0.1 collective-permute-start.7
  32.6 3.4 %collective-permute-start.8 = (f32[544,128]{1,0:T(8,128)S(1)}, f32[544,128]{1,0:T(8,128)S(1)}, u32[]{:S(2)}, u32[]{:S(2)}) collective-permute-start(f32[544,128]{1,0:T(8,128)S(1)} %get-tuple-element.72), channel_id=1, source_target_pairs={{4,8},{8,4},{5,9},{9,5},{6,10},{10,6},{7,11},{11,7},{20,24},{24,20... | collective-permute-start | bytes 835592 | tf_op jit(solution)/shard_map/ppermute | solution.py:703
  36.0 3.7 %inner.4 = (f32[3,2,9,160,128]{4,3,2,1,0:T(8,128)S(1)}, f32[6,2,8,160,128]{4,3,2,1,0:T(8,128)S(1)}) custom-call(f32[6,2,8,144,128]{4,3,2,1,0:T(8,128)S(1)} %get-tuple-element.65.m.refs_4_.refs_2_, f32[3,2,9,160,128]{4,3,2,1,0:T(8,128)S(1)} %get-tuple-element.74.v_in, ...), custom_call_target="tpu_custom_call", output_to_operand_aliasing={{0}: (1, {}), {1}: (2, {})} | custom-call | flops 26214400 | tf_op jit(solution)/shard_map/inner/pallas_call | solution.py:809
  39.7 0.3 collective-permute-done.7.refs_0_
  39.9 1.6 %collective-permute-done.8.refs_1_ = f32[544,128]{1,0:T(8,128)S(1)} collective-permute-done((f32[544,128]{1,0:T(8,128)S(1)}, f32[544,128]{1,0:T(8,128)S(1)}, u32[]{:S(2)}, u32[]{:S(2)}) %collective-permute-start.8) | collective-permute-done | bytes 278560 | tf_op jit(solution)/shard_map/ppermute | solution.py:703
  41.6 1.9 %boundary.4 = (f32[3,2,9,160,128]{4,3,2,1,0:T(8,128)S(1)}, f32[6,2,8,160,128]{4,3,2,1,0:T(8,128)S(1)}, f32[8,2,16,128]{3,2,1,0:T(8,128)S(1)}, f32[544,128]{1,0:T(8,128)S(1)}, f32[544,128]{1,0:T(8,128)S(1)}) custom-call(s32[3]{0:T(128)S(1)} %pad_add_fusion.flags, ...), custom_call_target="tpu_custom_call", output_to_operand_aliasing={{0}: (6, {}), {1}: (7, {}), {2}: (8, {})} | custom-call | flops 6553600 | tf_op jit(solution)/shard_map/boundary/pallas_call | solution.py:836
  43.5 0.1 collective-permute-start.9
  43.6 2.4 %collective-permute-start.10 = (f32[544,128]{1,0:T(8,128)S(1)}, f32[544,128]{1,0:T(8,128)S(1)}, u32[]{:S(2)}, u32[]{:S(2)}) collective-permute-start(f32[544,128]{1,0:T(8,128)S(1)} %get-tuple-element.80), channel_id=1, source_target_pairs={{4,8},{8,4},{5,9},{9,5},{6,10},{10,6},{7,11},{11,7},{20,24},{24,20... | collective-permute-start | bytes 835592 | tf_op jit(solution)/shard_map/ppermute | solution.py:703
  46.0 5.0 %inner.5 = (f32[3,2,9,160,128]{4,3,2,1,0:T(8,128)S(1)}, f32[6,2,8,160,128]{4,3,2,1,0:T(8,128)S(1)}, f32[3,8,128,128]{3,2,1,0:T(8,128)}, f32[6,8,128,128]{3,2,1,0:T(8,128)}) custom-call(f32[6,2,8,144,128]{4,3,2,1,0:T(8,128)S(1)} %get-tuple-element.65.m.refs_4_.refs_2_, ...), custom_call_target="tpu_custom_call", output_to_operand_aliasing={{0}: (1, {}), {1}: (2, {})} | custom-call | flops 26214400 | tf_op jit(solution)/shard_map/inner/pallas_call | solution.py:809
  51.0 1.1 %collective-permute-done.9.refs_0_ = f32[544,128]{1,0:T(8,128)S(1)} collective-permute-done((f32[544,128]{1,0:T(8,128)S(1)}, f32[544,128]{1,0:T(8,128)S(1)}, u32[]{:S(2)}, u32[]{:S(2)}) %collective-permute-start.9) | collective-permute-done | bytes 278560 | tf_op jit(solution)/shard_map/ppermute | solution.py:703
  52.0 1.7 %collective-permute-done.10.refs_1_ = f32[544,128]{1,0:T(8,128)S(1)} collective-permute-done((f32[544,128]{1,0:T(8,128)S(1)}, f32[544,128]{1,0:T(8,128)S(1)}, u32[]{:S(2)}, u32[]{:S(2)}) %collective-permute-start.10) | collective-permute-done | bytes 278560 | tf_op jit(solution)/shard_map/ppermute | solution.py:703
  53.7 4.0 %boundary.5 = (f32[3,2,9,160,128]{4,3,2,1,0:T(8,128)S(1)}, f32[6,2,8,160,128]{4,3,2,1,0:T(8,128)S(1)}, f32[8,2,16,128]{3,2,1,0:T(8,128)S(1)}, f32[3,8,128,128]{3...) custom-call(s32[3]{0:T(128)S(1)} %pad_add_fusion.flags, ...), custom_call_target="tpu_custom_call", output_to_operand_aliasing={{0}: (6, {}), {1}: (7, {}), {2}: (8, {}), {3}: (9, {}), {4}... | custom-call | flops 6553600 | tf_op jit(solution)/shard_map/boundary/pallas_call | solution.py:836
  (6 shorter events, 0.0 us)
Async XLA Ops:
  2.5 6.9 %collective-permute-start = (f32[15,4,8,128]{3,2,1,0:T(8,128)S(1)}, f32[15,4,8,128]{3,2,1,0:T(8,128)S(1)}, u32[]{:S(2)}, u32[]{:S(2)}) collective-permute-start(f32[15,4,8,128]{3,2,1,0:T(8,128)S(1)} %edge.1), channel_id=1, source_target_pairs={{0,16},{16,0},{1,17},{17,1},{2,18},{18,2},{3,19},{19,3},{4,20},{20... | collective-permute-start | bytes 737288 | tf_op jit(solution)/shard_map/ppermute | solution.py:753
  10.1 8.6 %collective-permute-start.3 = (f32[3,144,128]{2,1,0:T(8,128)S(1)}, f32[3,144,128]{2,1,0:T(8,128)S(1)}, u32[]{:S(2)}, u32[]{:S(2)}) collective-permute-start(f32[3,144,128]{2,1,0:T(8,128)S(1)} %get-tuple-element.58), channel_id=1, source_target_pairs={{0,1},{1,0},{2,3},{3,2},{4,5},{5,4},{6,7},{7,6},{8,9},{9,8},{10,11... | collective-permute-start | bytes 663560 | tf_op jit(solution)/shard_map/ppermute | solution.py:703
  11.7 7.5 %collective-permute-start.4 = (f32[3,144,128]{2,1,0:T(8,128)S(1)}, f32[3,144,128]{2,1,0:T(8,128)S(1)}, u32[]{:S(2)}, u32[]{:S(2)}) collective-permute-start(f32[3,144,128]{2,1,0:T(8,128)S(1)} %get-tuple-element.59), channel_id=1, source_target_pairs={{1,2},{2,1},{5,6},{6,5},{9,10},{10,9},{13,14},{14,13},{17,18},{18,... | collective-permute-start | bytes 663560 | tf_op jit(solution)/shard_map/ppermute | solution.py:703
  15.5 15.0 %collective-permute-start.1 = (f32[544,128]{1,0:T(8,128)S(1)}, f32[544,128]{1,0:T(8,128)S(1)}, u32[]{:S(2)}, u32[]{:S(2)}) collective-permute-start(f32[544,128]{1,0:T(8,128)S(1)} %get-tuple-element.56), channel_id=1, source_target_pairs={{0,4},{4,0},{8,12},{12,8},{1,5},{5,1},{9,13},{13,9},{2,6},{6,2},{1... | collective-permute-start | bytes 835592 | tf_op jit(solution)/shard_map/ppermute | solution.py:703
  16.8 13.7 %collective-permute-start.2 = (f32[544,128]{1,0:T(8,128)S(1)}, f32[544,128]{1,0:T(8,128)S(1)}, u32[]{:S(2)}, u32[]{:S(2)}) collective-permute-start(f32[544,128]{1,0:T(8,128)S(1)} %get-tuple-element.57), channel_id=1, source_target_pairs={{4,8},{8,4},{5,9},{9,5},{6,10},{10,6},{7,11},{11,7},{20,24},{24,20... | collective-permute-start | bytes 835592 | tf_op jit(solution)/shard_map/ppermute | solution.py:703
  21.3 9.2 %collective-permute-start.5 = (f32[152,128]{1,0:T(8,128)S(1)}, f32[152,128]{1,0:T(8,128)S(1)}, u32[]{:S(2)}, u32[]{:S(2)}) collective-permute-start(f32[152,128]{1,0:T(8,128)S(1)} %get-tuple-element.60), channel_id=1, source_target_pairs={{0,4},{4,0},{8,12},{12,8},{1,5},{5,1},{9,13},{13,9},{2,6},{6,2},{1... | collective-permute-start | bytes 233480 | tf_op jit(solution)/shard_map/ppermute | solution.py:703
  22.7 7.9 %collective-permute-start.6 = (f32[152,128]{1,0:T(8,128)S(1)}, f32[152,128]{1,0:T(8,128)S(1)}, u32[]{:S(2)}, u32[]{:S(2)}) collective-permute-start(f32[152,128]{1,0:T(8,128)S(1)} %get-tuple-element.61), channel_id=1, source_target_pairs={{4,8},{8,4},{5,9},{9,5},{6,10},{10,6},{7,11},{11,7},{20,24},{24,20... | collective-permute-start | bytes 233480 | tf_op jit(solution)/shard_map/ppermute | solution.py:703
  32.6 7.4 %collective-permute-start.7 = (f32[544,128]{1,0:T(8,128)S(1)}, f32[544,128]{1,0:T(8,128)S(1)}, u32[]{:S(2)}, u32[]{:S(2)}) collective-permute-start(f32[544,128]{1,0:T(8,128)S(1)} %get-tuple-element.71), channel_id=1, source_target_pairs={{0,4},{4,0},{8,12},{12,8},{1,5},{5,1},{9,13},{13,9},{2,6},{6,2},{1... | collective-permute-start | bytes 835592 | tf_op jit(solution)/shard_map/ppermute | solution.py:703
  32.6 8.9 %collective-permute-start.8 = (f32[544,128]{1,0:T(8,128)S(1)}, f32[544,128]{1,0:T(8,128)S(1)}, u32[]{:S(2)}, u32[]{:S(2)}) collective-permute-start(f32[544,128]{1,0:T(8,128)S(1)} %get-tuple-element.72), channel_id=1, source_target_pairs={{4,8},{8,4},{5,9},{9,5},{6,10},{10,6},{7,11},{11,7},{20,24},{24,20... | collective-permute-start | bytes 835592 | tf_op jit(solution)/shard_map/ppermute | solution.py:703
  43.5 8.5 %collective-permute-start.9 = (f32[544,128]{1,0:T(8,128)S(1)}, f32[544,128]{1,0:T(8,128)S(1)}, u32[]{:S(2)}, u32[]{:S(2)}) collective-permute-start(f32[544,128]{1,0:T(8,128)S(1)} %get-tuple-element.79), channel_id=1, source_target_pairs={{0,4},{4,0},{8,12},{12,8},{1,5},{5,1},{9,13},{13,9},{2,6},{6,2},{1... | collective-permute-start | bytes 835592 | tf_op jit(solution)/shard_map/ppermute | solution.py:703
  43.6 10.1 %collective-permute-start.10 = (f32[544,128]{1,0:T(8,128)S(1)}, f32[544,128]{1,0:T(8,128)S(1)}, u32[]{:S(2)}, u32[]{:S(2)}) collective-permute-start(f32[544,128]{1,0:T(8,128)S(1)} %get-tuple-element.80), channel_id=1, source_target_pairs={{4,8},{8,4},{5,9},{9,5},{6,10},{10,6},{7,11},{11,7},{20,24},{24,20... | collective-permute-start | bytes 835592 | tf_op jit(solution)/shard_map/ppermute | solution.py:703

commit v5 on v4

--- a/solution.py
+++ b/solution.py
@@ -81,11 +81,11 @@
     return out
 
 
-def stress_tile(v, s, m, y, row, lanes):
+def stress_tile(v, s, m, y, row, lanes, tiles=(0, 1)):
     both = (0, 1)
     own = [[at(v, c, t, y, row) for t in both] for c in range(3)]
     ahead = [z_above(own[c], lanes) for c in range(3)]
-    for t in both:
+    for t in tiles:
         vx, vy, vz = own[0][t], own[1][t], own[2][t]
         over_x = [at(v, c, t, y, row + 1) for c in range(3)]
         over_y = [at(v, c, t, y + 1, row) for c in range(3)]
@@ -109,15 +109,47 @@
     return lax.broadcasted_iota(jnp.int32, like, len(like) - 1)
 
 
-def strip_pack(pieces, eighths):
-    packed = jnp.zeros_like(pieces[0])
-    for k, piece in enumerate(pieces):
-        packed = jnp.where(eighths == k, roll(piece, STRIP * k + HALO), packed)
+SLOTS = 4
+
+
+def strip_tile(up, down, eighths):
+    packed = jnp.zeros_like(up[0])
+    for start, pieces in ((0, up), (SLOTS, down)):
+        for k, piece in enumerate(pieces):
+            moved = roll(piece, STRIP * (start + k) + HALO)
+            packed = jnp.where(eighths == start + k, moved, packed)
     return packed
 
 
-def strip_take(packed, k):
-    return roll(packed, -(STRIP * k + HALO))
+def strip_take(packed, slot):
+    return roll(packed, -(STRIP * slot + HALO))
+
+
+def strip_send(strips, cross_tile, count, odd, y_a, y_b, base):
+    turned = strips[...].T
+    for j in range(0, STRIP * count, 8):
+        up = turned[j : j + 8, :]
+        down = turned[STRIP * SLOTS + j : STRIP * SLOTS + j + 8, :]
+        y_a[base + j : base + j + 8, :] = jnp.where(odd, down, up)
+        y_b[base + j : base + j + 8, :] = jnp.where(odd, up, down)
+    other = roll(cross_tile, -STRIP * SLOTS)
+    last = base + STRIP * count
+    y_a[last : last + 8, :] = jnp.where(odd, other, cross_tile)
+    y_b[last : last + 8, :] = jnp.where(odd, cross_tile, other)
+
+
+def strip_receive(r_a, r_b, base, count, odd, turned, strips, lanes):
+    turned[...] = jnp.zeros_like(turned)
+    for j in range(0, STRIP * count, 8):
+        from_a, from_b = r_a[base + j : base + j + 8, :], r_b[base + j : base + j + 8, :]
+        turned[j : j + 8, :] = jnp.where(odd, from_a, from_b)
+        start = STRIP * SLOTS + j
+        turned[start : start + 8, :] = jnp.where(odd, from_b, from_a)
+    strips[...] = turned[...].T
+    last = base + STRIP * count
+    from_a, from_b = r_a[last : last + 8, :], r_b[last : last + 8, :]
+    low, high = jnp.where(odd, from_a, from_b), jnp.where(odd, from_b, from_a)
+    return jnp.where(lanes < STRIP * SLOTS, low, roll(high, STRIP * SLOTS))
 
 
 def field_ref(kind, v, s, m):
@@ -320,18 +352,22 @@
         z_b[plane, pl.ds(nx + 8, 8), :] = zeros
 
 
-def write_messages(v, s, eighths, odd, y_a, y_b, nx):
+def write_messages(v, s, eighths, odd, y_a, y_b, strips, nx):
     last = s.shape[2] - 1
     span = nx + 8
     for row in row_tiles(nx):
         up = [at(s, c, 0, last, row) for c in ALONG_Y]
         down = [at(v, c, 0, 0, row) for c in range(3)]
-        up.append(strip_pack([at(s, c, 1, last, row) for c in ALONG_Y], eighths))
-        down.append(strip_pack([at(v, c, 1, 0, row) for c in range(3)], eighths))
-        for k in range(4):
+        for k in range(3):
             to = pl.ds(k * span + packed_row(row, nx), 8)
             y_a[to, :] = jnp.where(odd, down[k], up[k])
             y_b[to, :] = jnp.where(odd, up[k], down[k])
+        up = [at(s, c, 1, last, row) for c in ALONG_Y]
+        down = [at(v, c, 1, 0, row) for c in range(3)]
+        tile = strip_tile(up, down, eighths)
+        if row < nx:
+            strips[row : row + 8, :] = tile
+    strip_send(strips, tile, 3, odd, y_a, y_b, 3 * span)
 
 
 def partial_trials(v, s, m, nx, lanes):
@@ -402,7 +438,9 @@
     unpack_fields(halo, v, s, m, nx, False)
 
 
-def widen_kernel(flags, thirds, eighths, r_a, r_b, v_in, s_in, m_in, f_in, v, s, m, fault, y_a, y_b):
+def widen_kernel(
+    flags, thirds, eighths, r_a, r_b, v_in, s_in, m_in, f_in, v, s, m, fault, y_a, y_b, strips
+):
     ny, width = m.shape[2], m.shape[4]
     nx = r_a.shape[1] - 16
     planes = z_slots(ny, width)[1]
@@ -428,14 +466,14 @@
             jnp.where(lanes == HALO, roll(at(v, c, 0, 0, row), HALO), at(v, c, 1, 0, row))
             for c in range(3)
         ] + [buoyancy]
-        up, down = strip_pack(up, halos), strip_pack(down, halos)
-        to = pl.ds(packed_row(row, nx), 8)
-        y_a[to, :] = jnp.where(odd_y, down, up)
-        y_b[to, :] = jnp.where(odd_y, up, down)
+        tile = strip_tile(up, down, halos)
+        if row < nx:
+            strips[row : row + 8, :] = tile
+    strip_send(strips, tile, SLOTS, odd_y, y_a, y_b, 0)
     for t in range(2):
         for k in range(8):
             line = fault[min(k, 5), t, 0:1, :]
-            row = nx + 8 + 8 * t + k
+            row = STRIP * SLOTS + 8 + 8 * t + k
             y_a[row : row + 1, :] = line
             y_b[row : row + 1, :] = line
 
@@ -474,20 +512,30 @@
             copies.append(pltpu.make_async_copy(part, to, sems.at[c]))
             copies[-1].start()
 
+    def out_copy(c, y):
+        part = s.at[c, 0, y, pl.ds(PAD + 8, nx - 16), :]
+        to = new_s.at[c, y, pl.ds(8, nx - 16), :]
+        return pltpu.make_async_copy(part, to, sems.at[3 + c * ny + y])
+
     def stresses(y, carry):
         for row in range(8, nx - 8, 8):
-            stress_tile(v, s, m, y, row, lanes)
+            stress_tile(v, s, m, y, row, lanes, (0,) if final else (0, 1))
+        if final:
+            for c in range(6):
+                out_copy(c, y).start()
         return carry
 
     lax.fori_loop(1, ny - 1, stresses, 0)
     if final:
-        for c in range(6):
-            part = s.at[c, 0, pl.ds(1, ny - 2), pl.ds(PAD + 8, nx - 16), :]
-            to = new_s.at[c, pl.ds(1, ny - 2), pl.ds(8, nx - 16), :]
-            copies.append(pltpu.make_async_copy(part, to, sems.at[3 + c]))
-            copies[-1].start()
         for copy in copies:
             copy.wait()
+
+        def wait(y, carry):
+            for c in range(6):
+                out_copy(c, y).wait()
+            return carry
+
+        lax.fori_loop(1, ny - 1, wait, 0)
 
 
 def boundary_kernel(first, final, flags, eighths, *refs):
@@ -509,9 +557,9 @@
     if first:
         (ahead_b,) = pop(1)
     if final:
-        new_v, new_s, slip_out, rows, sems = refs
+        new_v, new_s, slip_out, rows, turned, strips, sems = refs
     else:
-        y_a, y_b, rows = refs
+        y_a, y_b, rows, turned, strips = refs
     ny, width = m.shape[2], m.shape[4]
     nx = m.shape[3] - 16
     cross = cross_row(nx)
@@ -520,41 +568,42 @@
     lanes = lane_index((8, width))
     halos = eighths[...]
 
+    count = SLOTS if first else 3
+    main_a, main_b = (early_a, early_b) if first else (r_a, r_b)
+    cross_tile = strip_receive(
+        r_a, r_b, 0 if first else 3 * span, count, odd, turned, strips, lanes
+    )
+
     def received(row):
         at_row = packed_row(row, nx)
-        if not first:
-            from_a = [r_a[pl.ds(k * span + at_row, 8), :] for k in range(4)]
-            from_b = [r_b[pl.ds(k * span + at_row, 8), :] for k in range(4)]
-        else:
-            from_a = [early_a[pl.ds(k * span + at_row, 8), :] for k in range(4)]
-            from_b = [early_b[pl.ds(k * span + at_row, 8), :] for k in range(4)]
-            from_a.append(r_a[pl.ds(at_row, 8), :])
-            from_b.append(r_b[pl.ds(at_row, 8), :])
+        from_a = [main_a[pl.ds(k * span + at_row, 8), :] for k in range(count)]
+        from_b = [main_b[pl.ds(k * span + at_row, 8), :] for k in range(count)]
         low = [jnp.where(odd, a, b) for a, b in zip(from_a, from_b)]
         high = [jnp.where(odd, b, a) for a, b in zip(from_a, from_b)]
+        packed = strips[row : row + 8, :] if row < nx else cross_tile
         if first:
             for c in range(3):
-                column = roll(high[-1], -(STRIP * c + 2 * HALO))
+                column = roll(packed, -(STRIP * (SLOTS + c) + 2 * HALO))
                 high[c] = jnp.where(lanes == 0, column, high[c])
-        return low, high
+        return low, high, packed
 
     if first:
         for t in range(2):
-            to = pl.ds(span + 8 * t, 8)
+            to = pl.ds(STRIP * SLOTS + 8 + 8 * t, 8)
             lines = jnp.where(odd, r_b[to, :], r_a[to, :])
             for k in range(6):
                 fault[k, t, ny : ny + 1, :] = lines[k : k + 1, :]
     for row in row_tiles(nx):
-        low, high = received(row)
+        low, high, packed = received(row)
         if first:
             ahead_b[0, pl.ds(row, 8), :] = high[3]
-            ahead_b[1, pl.ds(row, 8), :] = strip_take(high[-1], 3)
+            ahead_b[1, pl.ds(row, 8), :] = strip_take(packed, SLOTS + 3)
         for t in range(2):
             scale = DT * m[B, t, 0, pl.ds(row, 8), :]
             scale_ahead = DT * ahead_b[t, pl.ds(row, 8), :]
             for c in range(3):
-                low_c = low[c] if t == 0 else strip_take(low[-1], c)
-                high_c = high[c] if t == 0 else strip_take(high[-1], c)
+                low_c = low[c] if t == 0 else strip_take(packed, c)
+                high_c = high[c] if t == 0 else strip_take(packed, SLOTS + c)
                 v[c, t, 0, pl.ds(PAD + row, 8), :] = at(v, c, t, 0, row) - scale * low_c
                 v[c, t, ny, pl.ds(PAD + row, 8), :] = high_c - scale_ahead * at(
                     s, ALONG_Y[c], t, ny - 1, row
@@ -596,6 +645,9 @@
             for c in range(3):
                 rows[0, c, t, part, :] = own[c] + sign * par[OWN_B] * traction[c]
                 rows[1, c, t, part, :] = other[c] - sign * par[OTHER_B] * traction[c]
+    for y in (0, ny - 1):
+        for row in range(8, nx - 8, 8):
+            stress_tile(v, s, m, y, row, lanes, (0,) if final else (0, 1))
     for side, pair in places:
 
         @pl.when(flags[0] == side)
@@ -608,40 +660,42 @@
                                 which, c, t, y : y + 1, :
                             ]
 
-    def planes(i, carry):
-        for row in row_tiles(nx)[:-1] if final else row_tiles(nx):
-            stress_tile(v, s, m, i * (ny - 1), row, lanes)
-        return carry
-
-    lax.fori_loop(0, 2, planes, 0)
+    if final:
+        copies = []
+
+        def send(pairs):
+            for part, to in pairs:
+                copies.append(pltpu.make_async_copy(part, to, sems.at[len(copies)]))
+                copies[-1].start()
+
+        def plane(ref, out, c, y):
+            return ref.at[c, 0, y, pl.ds(PAD, nx), :], out.at[c, y]
+
+        def edge(ref, out, c, inside, row):
+            part = ref.at[c, 0, pl.ds(1, inside), pl.ds(PAD + row, 8), :]
+            return part, out.at[c, pl.ds(1, inside), pl.ds(row, 8), :]
+
+        send([plane(v, new_v, c, 0) for c in range(3)])
+        send([edge(v, new_v, c, ny - 1, row) for c in range(3) for row in (0, nx - 8)])
+    tiles = (0,) if final else (0, 1)
+    for y in (0, ny - 1):
+        for row in (0, nx - 8) if final else (0, nx - 8, cross):
+            stress_tile(v, s, m, y, row, lanes, tiles)
     if not final:
         partial_trials(v, s, m, nx, lanes)
-        write_messages(v, s, halos, odd, y_a, y_b, nx)
+        write_messages(v, s, halos, odd, y_a, y_b, strips, nx)
         return
+
+    send([plane(s, new_s, c, y) for c in range(6) for y in (0, ny - 1)])
 
     def ends(y, carry):
         for row in (0, nx - 8):
-            stress_tile(v, s, m, y, row, lanes)
+            stress_tile(v, s, m, y, row, lanes, tiles)
         return carry
 
     lax.fori_loop(1, ny - 1, ends, 0)
+    send([edge(s, new_s, c, ny - 2, row) for c in range(6) for row in (0, nx - 8)])
     slip_out[...] = fault[SLIP, 0, 0:ny, :]
-    copies = []
-    for ref, out, fields, whole in ((v, new_v, 3, (0,)), (s, new_s, 6, (0, ny - 1))):
-        inside = ny - len(whole)
-        for c in range(fields):
-            for y in whole:
-                copies.append((ref.at[c, 0, y, pl.ds(PAD, nx), :], out.at[c, y]))
-            for row in (0, nx - 8):
-                copies.append(
-                    (
-                        ref.at[c, 0, pl.ds(1, inside), pl.ds(PAD + row, 8), :],
-                        out.at[c, pl.ds(1, inside), pl.ds(row, 8), :],
-                    )
-                )
-    copies = [pltpu.make_async_copy(a, b, sems.at[k]) for k, (a, b) in enumerate(copies)]
-    for copy in copies:
-        copy.start()
     for copy in copies:
         copy.wait()
 
@@ -722,6 +776,7 @@
     region_normal,
 ):
     ny, nx, width = buoyancy.shape
+    assert nx == width
     across, along, dip = (lax.axis_index(k) for k in ("gx", "gy", "gz"))
     flags = jnp.stack([across, along % 2, dip % 2]).astype(jnp.int32)
     lanes = jnp.broadcast_to(jnp.arange(width, dtype=jnp.int32), (8, width))
@@ -783,13 +838,14 @@
         early_kernel, "early", (y_shape, y_shape), [sm] + [vm] * 3, {}, flops=10 * unit
     )(flags, v, s, m)
     early_a, early_b = pair_swaps(early_a, early_b, "gy")
-    y_shape = f32(nx + 8 + 16, width)
+    y_shape = f32(STRIP * SLOTS + 8 + 16, width)
     v, s, m, fault, y_a, y_b = call(
         widen_kernel,
         "widen",
         (v_shape, s_shape, m_shape, fault_shape, y_shape, y_shape),
         [sm] + [vm] * 8,
         {5: 0, 6: 1, 7: 2, 8: 3},
+        [pltpu.VMEM((nx, width), jnp.float32)],
         flops=50 * unit,
     )(flags, thirds, eighths, z_a, z_b, v, s, m, fault)
     v, s, m = call(
@@ -800,7 +856,7 @@
         {4: 0, 5: 1, 6: 2},
         flops=50 * unit,
     )(flags, thirds, z_a, z_b, v, s, m)
-    y_shape = f32(4 * (nx + 8), width)
+    y_shape = f32(3 * (nx + 8) + STRIP * 3 + 8, width)
     ahead_b = None
     out_shapes = (HBM((3, ny, nx, width), jnp.float32), HBM((6, ny, nx, width), jnp.float32))
     for step in range(STEPS):
@@ -812,7 +868,7 @@
             (v_shape, s_shape) + (out_shapes if final else ()),
             [vm] * 3,
             {1: 0, 2: 1},
-            [pltpu.SemaphoreType.DMA((9,))] if final else [],
+            [pltpu.SemaphoreType.DMA((3 + 6 * ny,))] if final else [],
             flops=200 * unit,
             out_specs=[vm, vm] + ([hb, hb] if final else []),
         )(m, v, s)
@@ -822,6 +878,7 @@
         aliases = {at_state + k: k for k in range(3)}
         shapes, specs = [v_shape, s_shape, fault_shape], [vm, vm, vm]
         scratch = [pltpu.VMEM((2, 3, 2, high, width), jnp.float32)]
+        scratch += [pltpu.VMEM((width, nx), jnp.float32), pltpu.VMEM((nx, width), jnp.float32)]
         if first:
             shapes.append(f32(2, rows, width))
             specs.append(vm)

time: 58 us -> 59.4 us (1.024)
  the two profiles are of different devices: /device:TPU:21 before, /device:TPU:10 now
where the time goes in v5:
time: 59.4 us; the launch traced here: 59 us
  Pallas kernels  31.7 us (53%)
  starting transfers between devices  18.4 us (31%)
  waiting for transfers between devices  7.97 us (13%)
  between operations  0.86 us (1%)
    ppermute x10, starting transfers between devices, pair_swaps(): out.append(lax.ppermute(value, axis, pairs))  16.8 us
    pallas_call x3, Pallas kernels, local(): call(functools.partial(inner_kernel, first, final), 'inner', (v_shape, s_...  10.8 us
    pallas_call x3, Pallas kernels, local(): call(functools.partial(boundary_kernel, first, final), 'boundary', shapes...  7.51 us
    ppermute x10, waiting for transfers between devices, pair_swaps(): out.append(lax.ppermute(value, axis, pairs))  7.2 us
    pallas_call x1, Pallas kernels, local(): call(load_kernel, 'load', (v_shape, s_shape, m_shape, fault_shape, z_shap...  5.36 us
    pallas_call x1, Pallas kernels, local(): call(rest_kernel, 'rest', (v_shape, s_shape, m_shape), [sm] + [vm] * 6, {...  2.79 us
    pallas_call x1, Pallas kernels, local(): call(widen_kernel, 'widen', (v_shape, s_shape, m_shape, fault_shape, y_sh...  2.12 us
    pallas_call x1, Pallas kernels, local(): call(edge_kernel, 'edge', (f_shape,), [sm] + [hb] * 8, {}, [pltpu.Semapho...  1.73 us
  transfers between devices with their start and end apart: 11, of which 4 were waited for; matrix products, arithmetic and copies ran while one was open for 0% of the time, Pallas kernels for 36%

profile of v5, /device:TPU:10, one launch (start us, length us, event | category | flops | bytes accessed | tf_op | source)
XLA Modules:
  0.0 59.0 jit_solution(9098945884102532189)
XLA Ops:
  0.6 0.1 pad_add_fusion.flags
  0.7 1.7 %edge.1 = f32[15,4,8,128]{3,2,1,0:T(8,128)S(1)} custom-call(s32[3]{0:T(128)S(1)} %pad_add_fusion.flags, f32[3,8,128,128]{3,2,1,0:T(8,128)} %velocity.3, f32[6,8,128,128]{3,2,1,0:T(8,128)} %stress.3, f32[8,128,128]{2,1,0:T(8,128)} %rest_0_.3, f32[8,128,128]{2,1,0:T(8,128)} %rest_1_.3, f32[8,128,128]{2,1,0:T(8,128)} %rest_2_.3, f32[8,128,128]{2,1,0:T(8,128)} %rest_3_.3, ...), custom_call_target="tpu_custom_call" | custom-call | flops 131072 | tf_op jit(solution)/shard_map/edge/pallas_call | solution.py:799
  2.5 1.6 %collective-permute-start = (f32[15,4,8,128]{3,2,1,0:T(8,128)S(1)}, f32[15,4,8,128]{3,2,1,0:T(8,128)S(1)}, u32[]{:S(2)}, u32[]{:S(2)}) collective-permute-start(f32[15,4,8,128]{3,2,1,0:T(8,128)S(1)} %edge.1), channel_id=1, source_target_pairs={{0,16},{16,0},{1,17},{17,1},{2,18},{18,2},{3,19},{19,3},{4,20},{20... | collective-permute-start | bytes 737288 | tf_op jit(solution)/shard_map/ppermute | solution.py:808
  4.1 5.4 %load.1 = (f32[3,2,9,160,128]{4,3,2,1,0:T(8,128)S(1)}, f32[6,2,8,160,128]{4,3,2,1,0:T(8,128)S(1)}, f32[6,2,8,144,128]{4,3,2,1,0:T(8,128)S(1)}, f32[8,2,16,128]{3...) custom-call(s32[3]{0:T(128)S(1)} %pad_add_fusion.flags, ...), custom_call_target="tpu_custom_call" | custom-call | flops 13107200 | tf_op jit(solution)/shard_map/load/pallas_call | solution.py:809
  9.5 0.8 %collective-permute-done.f_other = f32[15,4,8,128]{3,2,1,0:T(8,128)S(1)} collective-permute-done((f32[15,4,8,128]{3,2,1,0:T(8,128)S(1)}, f32[15,4,8,128]{3,2,1,0:T(8,128)S(1)}, u32[]{:S(2)}, u32[]{:S(2)}) %collective-permute-start) | collective-permute-done | bytes 245792 | tf_op jit(solution)/shard_map/ppermute | solution.py:808
  10.2 0.8 %cross.1 = (f32[3,2,9,160,128]{4,3,2,1,0:T(8,128)S(1)}, f32[6,2,8,160,128]{4,3,2,1,0:T(8,128)S(1)}, f32[6,2,8,144,128]{4,3,2,1,0:T(8,128)S(1)}, f32[3,144,128]{2,1,0:T(8,128)S(1)}, f32[3,144,128]{2,1,0:T(8,128)S(1)}) custom-call(s32[3]{0:T(128)S(1)} %pad_add_fusion.flags, ...), custom_call_target="tpu_custom_call", output_to_operand_aliasing={{0}: (4, {}), {1}: (5, {}), {2}: (6, {}), {3}: (7, {}), {4}... | custom-call | flops 1310720 | tf_op jit(solution)/shard_map/cross/pallas_call | solution.py:827
  11.0 0.7 %early.1 = (f32[544,128]{1,0:T(8,128)S(1)}, f32[544,128]{1,0:T(8,128)S(1)}) custom-call(s32[3]{0:T(128)S(1)} %pad_add_fusion.flags, f32[3,2,9,160,128]{4,3,2,1,0:T(8,128)S(1)} %get-tuple-element.53.v.v_in, f32[6,2,8,160,128]{4,3,2,1,0:T(8,128)S(1)} %get-tuple-element.54.s.s_in, f32[6,2,8,144,128]{4,3,2,1,0:T(8,128)S(1)} %get-tuple-element.55.m.m_in), custom_call_target="tpu_custom_call" | custom-call | flops 1310720 | tf_op jit(solution)/shard_map/early/pallas_call | solution.py:837
  11.7 0.5 collective-permute-start.1
  12.2 4.6 %collective-permute-start.2 = (f32[544,128]{1,0:T(8,128)S(1)}, f32[544,128]{1,0:T(8,128)S(1)}, u32[]{:S(2)}, u32[]{:S(2)}) collective-permute-start(f32[544,128]{1,0:T(8,128)S(1)} %get-tuple-element.57), channel_id=1, source_target_pairs={{4,8},{8,4},{5,9},{9,5},{6,10},{10,6},{7,11},{11,7},{20,24},{24,20... | collective-permute-start | bytes 835592 | tf_op jit(solution)/shard_map/ppermute | solution.py:757
  16.8 0.1 collective-permute-start.3
  16.9 2.5 %collective-permute-start.4 = (f32[3,144,128]{2,1,0:T(8,128)S(1)}, f32[3,144,128]{2,1,0:T(8,128)S(1)}, u32[]{:S(2)}, u32[]{:S(2)}) collective-permute-start(f32[3,144,128]{2,1,0:T(8,128)S(1)} %get-tuple-element.59), channel_id=1, source_target_pairs={{1,2},{2,1},{5,6},{6,5},{9,10},{10,9},{13,14},{14,13},{17,18},{18,... | collective-permute-start | bytes 663560 | tf_op jit(solution)/shard_map/ppermute | solution.py:757
  19.4 0.0 collective-permute-done.3.r_a
  19.5 4.7 %collective-permute-done.4.r_b = f32[3,144,128]{2,1,0:T(8,128)S(1)} collective-permute-done((f32[3,144,128]{2,1,0:T(8,128)S(1)}, f32[3,144,128]{2,1,0:T(8,128)S(1)}, u32[]{:S(2)}, u32[]{:S(2)}) %collective-permute-start.4) | collective-permute-done | bytes 221216 | tf_op jit(solution)/shard_map/ppermute | solution.py:757
  24.1 2.1 %widen.1 = (f32[3,2,9,160,128]{4,3,2,1,0:T(8,128)S(1)}, f32[6,2,8,160,128]{4,3,2,1,0:T(8,128)S(1)}, f32[6,2,8,144,128]{4,3,2,1,0:T(8,128)S(1)}, f32[8,2,16,128]{...) custom-call(s32[3]{0:T(128)S(1)} %pad_add_fusion.flags, ...), custom_call_target="tpu_custom_call", output_to_operand_aliasing={{0}: (5, {}), {1}: (6, {}), {2}: (7, {}), {3}: (8, {})} | custom-call | flops 6553600 | tf_op jit(solution)/shard_map/widen/pallas_call | solution.py:842
  26.3 0.1 collective-permute-start.5
  26.3 1.9 %collective-permute-start.6 = (f32[56,128]{1,0:T(8,128)S(1)}, f32[56,128]{1,0:T(8,128)S(1)}, u32[]{:S(2)}, u32[]{:S(2)}) collective-permute-start(f32[56,128]{1,0:T(8,128)S(1)} %get-tuple-element.61), channel_id=1, source_target_pairs={{4,8},{8,4},{5,9},{9,5},{6,10},{10,6},{7,11},{11,7},{20,24},{24,20... | collective-permute-start | bytes 86024 | tf_op jit(solution)/shard_map/ppermute | solution.py:757
  28.3 2.8 %rest.1 = (f32[3,2,9,160,128]{4,3,2,1,0:T(8,128)S(1)}, f32[6,2,8,160,128]{4,3,2,1,0:T(8,128)S(1)}, f32[6,2,8,144,128]{4,3,2,1,0:T(8,128)S(1)}) custom-call(s32[3]{0:T(128)S(1)} %pad_add_fusion.flags, s32[8,128]{1,0:T(8,128)S(1)} %broadcast_select_fusion.thirds, ...), custom_call_target="tpu_custom_call", output_to_operand_aliasing={{0}: (4, {}), {1}: (5, {}), {2}: (6, {})} | custom-call | flops 6553600 | tf_op jit(solution)/shard_map/rest/pallas_call | solution.py:851
  31.1 3.0 %inner.3 = (f32[3,2,9,160,128]{4,3,2,1,0:T(8,128)S(1)}, f32[6,2,8,160,128]{4,3,2,1,0:T(8,128)S(1)}) custom-call(f32[6,2,8,144,128]{4,3,2,1,0:T(8,128)S(1)} %get-tuple-element.65.m.refs_4_.refs_2_, f32[3,2,9,160,128]{4,3,2,1,0:T(8,128)S(1)} %get-tuple-element.66.v_in, ...), custom_call_target="tpu_custom_call", output_to_operand_aliasing={{0}: (1, {}), {1}: (2, {})} | custom-call | flops 26214400 | tf_op jit(solution)/shard_map/inner/pallas_call | solution.py:865
  34.1 0.0 collective-permute-done.5.refs_2_
  34.1 0.0 collective-permute-done.6.refs_3_
  34.1 0.0 collective-permute-done.1.refs_0_
  34.1 0.0 collective-permute-done.2.refs_1_
  34.1 2.0 %boundary.3 = (f32[3,2,9,160,128]{4,3,2,1,0:T(8,128)S(1)}, f32[6,2,8,160,128]{4,3,2,1,0:T(8,128)S(1)}, f32[8,2,16,128]{3,2,1,0:T(8,128)S(1)}, f32[2,144,128]{2,1...) custom-call(s32[3]{0:T(128)S(1)} %pad_add_fusion.flags, ...), custom_call_target="tpu_custom_call", output_to_operand_aliasing={{0}: (7, {}), {1}: (8, {}), {2}: (9, {})} | custom-call | flops 6553600 | tf_op jit(solution)/shard_map/boundary/pallas_call | solution.py:893
  36.1 0.8 %collective-permute-start.7 = (f32[440,128]{1,0:T(8,128)S(1)}, f32[440,128]{1,0:T(8,128)S(1)}, u32[]{:S(2)}, u32[]{:S(2)}) collective-permute-start(f32[440,128]{1,0:T(8,128)S(1)} %get-tuple-element.71), channel_id=1, source_target_pairs={{0,4},{4,0},{8,12},{12,8},{1,5},{5,1},{9,13},{13,9},{2,6},{6,2},{1... | collective-permute-start | bytes 675848 | tf_op jit(solution)/shard_map/ppermute | solution.py:757
  36.9 3.2 %collective-permute-start.8 = (f32[440,128]{1,0:T(8,128)S(1)}, f32[440,128]{1,0:T(8,128)S(1)}, u32[]{:S(2)}, u32[]{:S(2)}) collective-permute-start(f32[440,128]{1,0:T(8,128)S(1)} %get-tuple-element.72), channel_id=1, source_target_pairs={{4,8},{8,4},{5,9},{9,5},{6,10},{10,6},{7,11},{11,7},{20,24},{24,20... | collective-permute-start | bytes 675848 | tf_op jit(solution)/shard_map/ppermute | solution.py:757
  40.1 3.5 %inner.4 = (f32[3,2,9,160,128]{4,3,2,1,0:T(8,128)S(1)}, f32[6,2,8,160,128]{4,3,2,1,0:T(8,128)S(1)}) custom-call(f32[6,2,8,144,128]{4,3,2,1,0:T(8,128)S(1)} %get-tuple-element.65.m.refs_4_.refs_2_, f32[3,2,9,160,128]{4,3,2,1,0:T(8,128)S(1)} %get-tuple-element.74.v_in, ...), custom_call_target="tpu_custom_call", output_to_operand_aliasing={{0}: (1, {}), {1}: (2, {})} | custom-call | flops 26214400 | tf_op jit(solution)/shard_map/inner/pallas_call | solution.py:865
  43.7 0.0 collective-permute-done.7.refs_0_
  43.7 1.9 %collective-permute-done.8.refs_1_ = f32[440,128]{1,0:T(8,128)S(1)} collective-permute-done((f32[440,128]{1,0:T(8,128)S(1)}, f32[440,128]{1,0:T(8,128)S(1)}, u32[]{:S(2)}, u32[]{:S(2)}) %collective-permute-start.8) | collective-permute-done | bytes 225312 | tf_op jit(solution)/shard_map/ppermute | solution.py:757
  45.6 1.9 %boundary.4 = (f32[3,2,9,160,128]{4,3,2,1,0:T(8,128)S(1)}, f32[6,2,8,160,128]{4,3,2,1,0:T(8,128)S(1)}, f32[8,2,16,128]{3,2,1,0:T(8,128)S(1)}, f32[440,128]{1,0:T(8,128)S(1)}, f32[440,128]{1,0:T(8,128)S(1)}) custom-call(s32[3]{0:T(128)S(1)} %pad_add_fusion.flags, ...), custom_call_target="tpu_custom_call", output_to_operand_aliasing={{0}: (6, {}), {1}: (7, {}), {2}: (8, {})} | custom-call | flops 6553600 | tf_op jit(solution)/shard_map/boundary/pallas_call | solution.py:893
  47.5 0.1 collective-permute-start.9
  47.6 3.0 %collective-permute-start.10 = (f32[440,128]{1,0:T(8,128)S(1)}, f32[440,128]{1,0:T(8,128)S(1)}, u32[]{:S(2)}, u32[]{:S(2)}) collective-permute-start(f32[440,128]{1,0:T(8,128)S(1)} %get-tuple-element.80), channel_id=1, source_target_pairs={{4,8},{8,4},{5,9},{9,5},{6,10},{10,6},{7,11},{11,7},{20,24},{24,20... | collective-permute-start | bytes 675848 | tf_op jit(solution)/shard_map/ppermute | solution.py:757
  50.6 4.2 %inner.5 = (f32[3,2,9,160,128]{4,3,2,1,0:T(8,128)S(1)}, f32[6,2,8,160,128]{4,3,2,1,0:T(8,128)S(1)}, f32[3,8,128,128]{3,2,1,0:T(8,128)}, f32[6,8,128,128]{3,2,1,0:T(8,128)}) custom-call(f32[6,2,8,144,128]{4,3,2,1,0:T(8,128)S(1)} %get-tuple-element.65.m.refs_4_.refs_2_, ...), custom_call_target="tpu_custom_call", output_to_operand_aliasing={{0}: (1, {}), {1}: (2, {})} | custom-call | flops 26214400 | tf_op jit(solution)/shard_map/inner/pallas_call | solution.py:865
  54.8 0.0 collective-permute-done.9.refs_0_
  54.8 0.6 %collective-permute-done.10.refs_1_ = f32[440,128]{1,0:T(8,128)S(1)} collective-permute-done((f32[440,128]{1,0:T(8,128)S(1)}, f32[440,128]{1,0:T(8,128)S(1)}, u32[]{:S(2)}, u32[]{:S(2)}) %collective-permute-start.10) | collective-permute-done | bytes 225312 | tf_op jit(solution)/shard_map/ppermute | solution.py:757
  55.4 3.6 %boundary.5 = (f32[3,2,9,160,128]{4,3,2,1,0:T(8,128)S(1)}, f32[6,2,8,160,128]{4,3,2,1,0:T(8,128)S(1)}, f32[8,2,16,128]{3,2,1,0:T(8,128)S(1)}, f32[3,8,128,128]{3...) custom-call(s32[3]{0:T(128)S(1)} %pad_add_fusion.flags, ...), custom_call_target="tpu_custom_call", output_to_operand_aliasing={{0}: (6, {}), {1}: (7, {}), {2}: (8, {}), {3}: (9, {}), {4}... | custom-call | flops 6553600 | tf_op jit(solution)/shard_map/boundary/pallas_call | solution.py:893
  (6 shorter events, 0.0 us)
Async XLA Ops:
  2.5 7.8 %collective-permute-start = (f32[15,4,8,128]{3,2,1,0:T(8,128)S(1)}, f32[15,4,8,128]{3,2,1,0:T(8,128)S(1)}, u32[]{:S(2)}, u32[]{:S(2)}) collective-permute-start(f32[15,4,8,128]{3,2,1,0:T(8,128)S(1)} %edge.1), channel_id=1, source_target_pairs={{0,16},{16,0},{1,17},{17,1},{2,18},{18,2},{3,19},{19,3},{4,20},{20... | collective-permute-start | bytes 737288 | tf_op jit(solution)/shard_map/ppermute | solution.py:808
  11.7 22.4 %collective-permute-start.1 = (f32[544,128]{1,0:T(8,128)S(1)}, f32[544,128]{1,0:T(8,128)S(1)}, u32[]{:S(2)}, u32[]{:S(2)}) collective-permute-start(f32[544,128]{1,0:T(8,128)S(1)} %get-tuple-element.56), channel_id=1, source_target_pairs={{0,4},{4,0},{8,12},{12,8},{1,5},{5,1},{9,13},{13,9},{2,6},{6,2},{1... | collective-permute-start | bytes 835592 | tf_op jit(solution)/shard_map/ppermute | solution.py:757
  12.2 21.9 %collective-permute-start.2 = (f32[544,128]{1,0:T(8,128)S(1)}, f32[544,128]{1,0:T(8,128)S(1)}, u32[]{:S(2)}, u32[]{:S(2)}) collective-permute-start(f32[544,128]{1,0:T(8,128)S(1)} %get-tuple-element.57), channel_id=1, source_target_pairs={{4,8},{8,4},{5,9},{9,5},{6,10},{10,6},{7,11},{11,7},{20,24},{24,20... | collective-permute-start | bytes 835592 | tf_op jit(solution)/shard_map/ppermute | solution.py:757
  16.8 2.6 %collective-permute-start.3 = (f32[3,144,128]{2,1,0:T(8,128)S(1)}, f32[3,144,128]{2,1,0:T(8,128)S(1)}, u32[]{:S(2)}, u32[]{:S(2)}) collective-permute-start(f32[3,144,128]{2,1,0:T(8,128)S(1)} %get-tuple-element.58), channel_id=1, source_target_pairs={{0,1},{1,0},{2,3},{3,2},{4,5},{5,4},{6,7},{7,6},{8,9},{9,8},{10,11... | collective-permute-start | bytes 663560 | tf_op jit(solution)/shard_map/ppermute | solution.py:757
  16.9 7.3 %collective-permute-start.4 = (f32[3,144,128]{2,1,0:T(8,128)S(1)}, f32[3,144,128]{2,1,0:T(8,128)S(1)}, u32[]{:S(2)}, u32[]{:S(2)}) collective-permute-start(f32[3,144,128]{2,1,0:T(8,128)S(1)} %get-tuple-element.59), channel_id=1, source_target_pairs={{1,2},{2,1},{5,6},{6,5},{9,10},{10,9},{13,14},{14,13},{17,18},{18,... | collective-permute-start | bytes 663560 | tf_op jit(solution)/shard_map/ppermute | solution.py:757
  26.3 7.8 %collective-permute-start.5 = (f32[56,128]{1,0:T(8,128)S(1)}, f32[56,128]{1,0:T(8,128)S(1)}, u32[]{:S(2)}, u32[]{:S(2)}) collective-permute-start(f32[56,128]{1,0:T(8,128)S(1)} %get-tuple-element.60), channel_id=1, source_target_pairs={{0,4},{4,0},{8,12},{12,8},{1,5},{5,1},{9,13},{13,9},{2,6},{6,2},{1... | collective-permute-start | bytes 86024 | tf_op jit(solution)/shard_map/ppermute | solution.py:757
  26.3 7.7 %collective-permute-start.6 = (f32[56,128]{1,0:T(8,128)S(1)}, f32[56,128]{1,0:T(8,128)S(1)}, u32[]{:S(2)}, u32[]{:S(2)}) collective-permute-start(f32[56,128]{1,0:T(8,128)S(1)} %get-tuple-element.61), channel_id=1, source_target_pairs={{4,8},{8,4},{5,9},{9,5},{6,10},{10,6},{7,11},{11,7},{20,24},{24,20... | collective-permute-start | bytes 86024 | tf_op jit(solution)/shard_map/ppermute | solution.py:757
  36.1 7.6 %collective-permute-start.7 = (f32[440,128]{1,0:T(8,128)S(1)}, f32[440,128]{1,0:T(8,128)S(1)}, u32[]{:S(2)}, u32[]{:S(2)}) collective-permute-start(f32[440,128]{1,0:T(8,128)S(1)} %get-tuple-element.71), channel_id=1, source_target_pairs={{0,4},{4,0},{8,12},{12,8},{1,5},{5,1},{9,13},{13,9},{2,6},{6,2},{1... | collective-permute-start | bytes 675848 | tf_op jit(solution)/shard_map/ppermute | solution.py:757
  36.9 8.6 %collective-permute-start.8 = (f32[440,128]{1,0:T(8,128)S(1)}, f32[440,128]{1,0:T(8,128)S(1)}, u32[]{:S(2)}, u32[]{:S(2)}) collective-permute-start(f32[440,128]{1,0:T(8,128)S(1)} %get-tuple-element.72), channel_id=1, source_target_pairs={{4,8},{8,4},{5,9},{9,5},{6,10},{10,6},{7,11},{11,7},{20,24},{24,20... | collective-permute-start | bytes 675848 | tf_op jit(solution)/shard_map/ppermute | solution.py:757
  47.5 7.3 %collective-permute-start.9 = (f32[440,128]{1,0:T(8,128)S(1)}, f32[440,128]{1,0:T(8,128)S(1)}, u32[]{:S(2)}, u32[]{:S(2)}) collective-permute-start(f32[440,128]{1,0:T(8,128)S(1)} %get-tuple-element.79), channel_id=1, source_target_pairs={{0,4},{4,0},{8,12},{12,8},{1,5},{5,1},{9,13},{13,9},{2,6},{6,2},{1... | collective-permute-start | bytes 675848 | tf_op jit(solution)/shard_map/ppermute | solution.py:757
  47.6 7.9 %collective-permute-start.10 = (f32[440,128]{1,0:T(8,128)S(1)}, f32[440,128]{1,0:T(8,128)S(1)}, u32[]{:S(2)}, u32[]{:S(2)}) collective-permute-start(f32[440,128]{1,0:T(8,128)S(1)} %get-tuple-element.80), channel_id=1, source_target_pairs={{4,8},{8,4},{5,9},{9,5},{6,10},{10,6},{7,11},{11,7},{20,24},{24,20... | collective-permute-start | bytes 675848 | tf_op jit(solution)/shard_map/ppermute | solution.py:757

commit v6 on v5

--- a/solution.py
+++ b/solution.py
@@ -266,35 +266,6 @@
     fault[SLIP, 0, 0:ny, :] = slip[...]
 
 
-def early_kernel(flags, v, s, m, y_a, y_b):
-    ny, width = m.shape[2], m.shape[4]
-    nx = m.shape[3] - 16
-    odd = flags[1] == 1
-    lanes = lane_index((8, width))
-    first = lanes == 0
-    span = nx + 8
-    for row in row_tiles(nx):
-        up = [at(s, c, 0, ny - 1, row) for c in ALONG_Y]
-        own = {c: at(s, c, 0, 0, row) for c in range(6)}
-        behind = {c: jnp.where(first, 0.0, roll(own[c], 1)) for c in (XZ, YZ, ZZ)}
-        lower_x = {c: own[c] - at(s, c, 0, 0, row - 1) for c in (XX, XY, XZ)}
-        buoyancy = m[B, 0, 0, pl.ds(row, 8), :]
-        total = (
-            lower_x[XX] + own[XY] + (own[XZ] - behind[XZ]),
-            lower_x[XY] + own[YY] + (own[YZ] - behind[YZ]),
-            lower_x[XZ] + own[YZ] + (own[ZZ] - behind[ZZ]),
-        )
-        at_row = packed_row(row, nx)
-        for c in range(3):
-            down = at(v, c, 0, 0, row) + DT * buoyancy * total[c]
-            to = pl.ds(c * span + at_row, 8)
-            y_a[to, :] = jnp.where(odd, down, up[c])
-            y_b[to, :] = jnp.where(odd, up[c], down)
-        to = pl.ds(3 * span + at_row, 8)
-        y_a[to, :] = buoyancy
-        y_b[to, :] = buoyancy
-
-
 UNROLL = 4
 
 
@@ -352,22 +323,29 @@
         z_b[plane, pl.ds(nx + 8, 8), :] = zeros
 
 
-def write_messages(v, s, eighths, odd, y_a, y_b, strips, nx):
+def write_messages(v, s, buoyancy, eighths, odd, y_a, y_b, strips, nx):
     last = s.shape[2] - 1
     span = nx + 8
+    count = 3 if buoyancy is None else SLOTS
+
+    def pieces(t, row):
+        up = [at(s, c, t, last, row) for c in ALONG_Y]
+        down = [at(v, c, t, 0, row) for c in range(3)]
+        if buoyancy is not None:
+            up.append(buoyancy[B, t, 0, pl.ds(row, 8), :])
+            down.append(up[-1])
+        return up, down
+
     for row in row_tiles(nx):
-        up = [at(s, c, 0, last, row) for c in ALONG_Y]
-        down = [at(v, c, 0, 0, row) for c in range(3)]
-        for k in range(3):
+        up, down = pieces(0, row)
+        for k in range(count):
             to = pl.ds(k * span + packed_row(row, nx), 8)
             y_a[to, :] = jnp.where(odd, down[k], up[k])
             y_b[to, :] = jnp.where(odd, up[k], down[k])
-        up = [at(s, c, 1, last, row) for c in ALONG_Y]
-        down = [at(v, c, 1, 0, row) for c in range(3)]
-        tile = strip_tile(up, down, eighths)
+        tile = strip_tile(*pieces(1, row), eighths)
         if row < nx:
             strips[row : row + 8, :] = tile
-    strip_send(strips, tile, 3, odd, y_a, y_b, 3 * span)
+    strip_send(strips, tile, count, odd, y_a, y_b, count * span)
 
 
 def partial_trials(v, s, m, nx, lanes):
@@ -457,23 +435,11 @@
 
     halo.take(nx + 8, [((0, k), store_fault(k)) for k in range(6)])
     partial_trials(v, s, m, nx, lanes)
-    last = ny - 1
-    halos = eighths[...]
-    for row in row_tiles(nx):
-        buoyancy = m[B, 1, 0, pl.ds(row, 8), :]
-        up = [at(s, c, 1, last, row) for c in ALONG_Y] + [buoyancy]
-        down = [
-            jnp.where(lanes == HALO, roll(at(v, c, 0, 0, row), HALO), at(v, c, 1, 0, row))
-            for c in range(3)
-        ] + [buoyancy]
-        tile = strip_tile(up, down, halos)
-        if row < nx:
-            strips[row : row + 8, :] = tile
-    strip_send(strips, tile, SLOTS, odd_y, y_a, y_b, 0)
+    write_messages(v, s, m, eighths[...], odd_y, y_a, y_b, strips, nx)
     for t in range(2):
         for k in range(8):
             line = fault[min(k, 5), t, 0:1, :]
-            row = STRIP * SLOTS + 8 + 8 * t + k
+            row = SLOTS * (nx + 8 + STRIP) + 8 + 8 * t + k
             y_a[row : row + 1, :] = line
             y_b[row : row + 1, :] = line
 
@@ -546,7 +512,6 @@
         del refs[:n]
         return out
 
-    early_a, early_b = pop(2) if first else (None, None)
     r_a, r_b, m = pop(3)
     if not first:
         (ahead_b,) = pop(1)
@@ -569,27 +534,20 @@
     halos = eighths[...]
 
     count = SLOTS if first else 3
-    main_a, main_b = (early_a, early_b) if first else (r_a, r_b)
-    cross_tile = strip_receive(
-        r_a, r_b, 0 if first else 3 * span, count, odd, turned, strips, lanes
-    )
+    cross_tile = strip_receive(r_a, r_b, count * span, count, odd, turned, strips, lanes)
 
     def received(row):
         at_row = packed_row(row, nx)
-        from_a = [main_a[pl.ds(k * span + at_row, 8), :] for k in range(count)]
-        from_b = [main_b[pl.ds(k * span + at_row, 8), :] for k in range(count)]
+        from_a = [r_a[pl.ds(k * span + at_row, 8), :] for k in range(count)]
+        from_b = [r_b[pl.ds(k * span + at_row, 8), :] for k in range(count)]
         low = [jnp.where(odd, a, b) for a, b in zip(from_a, from_b)]
         high = [jnp.where(odd, b, a) for a, b in zip(from_a, from_b)]
         packed = strips[row : row + 8, :] if row < nx else cross_tile
-        if first:
-            for c in range(3):
-                column = roll(packed, -(STRIP * (SLOTS + c) + 2 * HALO))
-                high[c] = jnp.where(lanes == 0, column, high[c])
         return low, high, packed
 
     if first:
         for t in range(2):
-            to = pl.ds(STRIP * SLOTS + 8 + 8 * t, 8)
+            to = pl.ds(SLOTS * (span + STRIP) + 8 + 8 * t, 8)
             lines = jnp.where(odd, r_b[to, :], r_a[to, :])
             for k in range(6):
                 fault[k, t, ny : ny + 1, :] = lines[k : k + 1, :]
@@ -683,7 +641,7 @@
             stress_tile(v, s, m, y, row, lanes, tiles)
     if not final:
         partial_trials(v, s, m, nx, lanes)
-        write_messages(v, s, halos, odd, y_a, y_b, strips, nx)
+        write_messages(v, s, None, halos, odd, y_a, y_b, strips, nx)
         return
 
     send([plane(s, new_s, c, y) for c in range(6) for y in (0, ny - 1)])
@@ -833,12 +791,7 @@
         flops=10 * unit,
     )(flags, thirds, f_other, fault, v, s, m, z_a, z_b)
     z_a, z_b = pair_swaps(z_a, z_b, "gz")
-    y_shape = f32(4 * (nx + 8), width)
-    early_a, early_b = call(
-        early_kernel, "early", (y_shape, y_shape), [sm] + [vm] * 3, {}, flops=10 * unit
-    )(flags, v, s, m)
-    early_a, early_b = pair_swaps(early_a, early_b, "gy")
-    y_shape = f32(STRIP * SLOTS + 8 + 16, width)
+    y_shape = f32(SLOTS * (nx + 8 + STRIP) + 8 + 16, width)
     v, s, m, fault, y_a, y_b = call(
         widen_kernel,
         "widen",
@@ -872,7 +825,7 @@
             flops=200 * unit,
             out_specs=[vm, vm] + ([hb, hb] if final else []),
         )(m, v, s)
-        args = [flags, eighths] + ([early_a, early_b] if first else []) + [y_a, y_b, m]
+        args = [flags, eighths, y_a, y_b, m]
         args += ([] if first else [ahead_b]) + [v, s, fault] + outs
         at_state = len(args) - len(outs) - 3
         aliases = {at_state + k: k for k in range(3)}

time: 59.4 us -> 55.8 us (0.939)
  starting transfers between devices: 18.4 us -> 16.8 us
  Pallas kernels: 31.7 us -> 30.3 us
  waiting for transfers between devices: 7.97 us -> 7.28 us
    ppermute x10 -> x8, starting transfers between devices: 16.8 us -> 15.2 us  [pair_swaps(): out.append(lax.ppermute(value, axis, pairs))]
    ppermute x10 -> x8, waiting for transfers between devices: 7.2 us -> 6.53 us  [pair_swaps(): out.append(lax.ppermute(value, axis, pairs))]
    pallas_call x1, Pallas kernels: 2.12 us -> 1.44 us  [local(): call(widen_kernel, 'widen', (v_shape, s_shape, m_shape, fault_shape, y_sh...]
    pallas_call x1 -> x0, Pallas kernels: 0.67 us -> none  [local(): call(early_kernel, 'early', (y_shape, y_shape), [sm] + [vm] * 3, {}, flop...]
  transfers between devices with their start and end apart: 11 -> 9, of which waited for: 4 -> 3; matrix products, arithmetic and copies ran while one was open for 0% -> 0% of each run, Pallas kernels for 36% -> 34%
where the time goes in v6:
time: 55.8 us; the launch traced here: 55.4 us
  Pallas kernels  30.3 us (54%)
  starting transfers between devices  16.8 us (30%)
  waiting for transfers between devices  7.28 us (13%)
  between operations  0.84 us (2%)
    ppermute x8, starting transfers between devices, pair_swaps(): out.append(lax.ppermute(value, axis, pairs))  15.2 us
    pallas_call x3, Pallas kernels, local(): call(functools.partial(inner_kernel, first, final), 'inner', (v_shape, s_...  10.8 us
    pallas_call x3, Pallas kernels, local(): call(functools.partial(boundary_kernel, first, final), 'boundary', shapes...  7.5 us
    ppermute x8, waiting for transfers between devices, pair_swaps(): out.append(lax.ppermute(value, axis, pairs))  6.53 us
    pallas_call x1, Pallas kernels, local(): call(load_kernel, 'load', (v_shape, s_shape, m_shape, fault_shape, z_shap...  5.36 us
    pallas_call x1, Pallas kernels, local(): call(rest_kernel, 'rest', (v_shape, s_shape, m_shape), [sm] + [vm] * 6, {...  2.79 us
    pallas_call x1, Pallas kernels, local(): call(edge_kernel, 'edge', (f_shape,), [sm] + [hb] * 8, {}, [pltpu.Semapho...  1.73 us
    ppermute x1, starting transfers between devices, local(): lax.ppermute(f_own, 'gx', [(i, i ^ 1) for i in range(lax.axis_size('gx'))])  1.59 us
  transfers between devices with their start and end apart: 9, of which 3 were waited for; matrix products, arithmetic and copies ran while one was open for 0% of the time, Pallas kernels for 34%

profile of v6, /device:TPU:10, one launch (start us, length us, event | category | flops | bytes accessed | tf_op | source)
XLA Modules:
  0.0 55.4 jit_solution(14761099945778944046)
XLA Ops:
  0.6 0.1 pad_add_fusion.flags
  0.7 1.7 %edge.1 = f32[15,4,8,128]{3,2,1,0:T(8,128)S(1)} custom-call(s32[3]{0:T(128)S(1)} %pad_add_fusion.flags, f32[3,8,128,128]{3,2,1,0:T(8,128)} %velocity.3, f32[6,8,128,128]{3,2,1,0:T(8,128)} %stress.3, f32[8,128,128]{2,1,0:T(8,128)} %rest_0_.3, f32[8,128,128]{2,1,0:T(8,128)} %rest_1_.3, f32[8,128,128]{2,1,0:T(8,128)} %rest_2_.3, f32[8,128,128]{2,1,0:T(8,128)} %rest_3_.3, ...), custom_call_target="tpu_custom_call" | custom-call | flops 131072 | tf_op jit(solution)/shard_map/edge/pallas_call | solution.py:757
  2.5 1.6 %collective-permute-start = (f32[15,4,8,128]{3,2,1,0:T(8,128)S(1)}, f32[15,4,8,128]{3,2,1,0:T(8,128)S(1)}, u32[]{:S(2)}, u32[]{:S(2)}) collective-permute-start(f32[15,4,8,128]{3,2,1,0:T(8,128)S(1)} %edge.1), channel_id=1, source_target_pairs={{0,16},{16,0},{1,17},{17,1},{2,18},{18,2},{3,19},{19,3},{4,20},{20... | collective-permute-start | bytes 737288 | tf_op jit(solution)/shard_map/ppermute | solution.py:766
  4.1 5.4 %load.1 = (f32[3,2,9,160,128]{4,3,2,1,0:T(8,128)S(1)}, f32[6,2,8,160,128]{4,3,2,1,0:T(8,128)S(1)}, f32[6,2,8,144,128]{4,3,2,1,0:T(8,128)S(1)}, f32[8,2,16,128]{3...) custom-call(s32[3]{0:T(128)S(1)} %pad_add_fusion.flags, ...), custom_call_target="tpu_custom_call" | custom-call | flops 13107200 | tf_op jit(solution)/shard_map/load/pallas_call | solution.py:767
  9.5 0.8 %collective-permute-done.f_other = f32[15,4,8,128]{3,2,1,0:T(8,128)S(1)} collective-permute-done((f32[15,4,8,128]{3,2,1,0:T(8,128)S(1)}, f32[15,4,8,128]{3,2,1,0:T(8,128)S(1)}, u32[]{:S(2)}, u32[]{:S(2)}) %collective-permute-start) | collective-permute-done | bytes 245792 | tf_op jit(solution)/shard_map/ppermute | solution.py:766
  10.2 0.8 %cross.1 = (f32[3,2,9,160,128]{4,3,2,1,0:T(8,128)S(1)}, f32[6,2,8,160,128]{4,3,2,1,0:T(8,128)S(1)}, f32[6,2,8,144,128]{4,3,2,1,0:T(8,128)S(1)}, f32[3,144,128]{2,1,0:T(8,128)S(1)}, f32[3,144,128]{2,1,0:T(8,128)S(1)}) custom-call(s32[3]{0:T(128)S(1)} %pad_add_fusion.flags, ...), custom_call_target="tpu_custom_call", output_to_operand_aliasing={{0}: (4, {}), {1}: (5, {}), {2}: (6, {}), {3}: (7, {}), {4}... | custom-call | flops 1310720 | tf_op jit(solution)/shard_map/cross/pallas_call | solution.py:785
  11.0 0.1 collective-permute-start.1
  11.1 2.5 %collective-permute-start.2 = (f32[3,144,128]{2,1,0:T(8,128)S(1)}, f32[3,144,128]{2,1,0:T(8,128)S(1)}, u32[]{:S(2)}, u32[]{:S(2)}) collective-permute-start(f32[3,144,128]{2,1,0:T(8,128)S(1)} %get-tuple-element.52), channel_id=1, source_target_pairs={{1,2},{2,1},{5,6},{6,5},{9,10},{10,9},{13,14},{14,13},{17,18},{18,... | collective-permute-start | bytes 663560 | tf_op jit(solution)/shard_map/ppermute | solution.py:715
  13.6 0.0 collective-permute-done.1.r_a
  13.6 4.7 %collective-permute-done.2.r_b = f32[3,144,128]{2,1,0:T(8,128)S(1)} collective-permute-done((f32[3,144,128]{2,1,0:T(8,128)S(1)}, f32[3,144,128]{2,1,0:T(8,128)S(1)}, u32[]{:S(2)}, u32[]{:S(2)}) %collective-permute-start.2) | collective-permute-done | bytes 221216 | tf_op jit(solution)/shard_map/ppermute | solution.py:715
  18.3 1.4 %widen.1 = (f32[3,2,9,160,128]{4,3,2,1,0:T(8,128)S(1)}, f32[6,2,8,160,128]{4,3,2,1,0:T(8,128)S(1)}, f32[6,2,8,144,128]{4,3,2,1,0:T(8,128)S(1)}, f32[8,2,16,128]{...) custom-call(s32[3]{0:T(128)S(1)} %pad_add_fusion.flags, ...), custom_call_target="tpu_custom_call", output_to_operand_aliasing={{0}: (5, {}), {1}: (6, {}), {2}: (7, {}), {3}: (8, {})} | custom-call | flops 6553600 | tf_op jit(solution)/shard_map/widen/pallas_call | solution.py:795
  19.8 0.5 collective-permute-start.3
  20.3 4.6 %collective-permute-start.4 = (f32[600,128]{1,0:T(8,128)S(1)}, f32[600,128]{1,0:T(8,128)S(1)}, u32[]{:S(2)}, u32[]{:S(2)}) collective-permute-start(f32[600,128]{1,0:T(8,128)S(1)} %get-tuple-element.57), channel_id=1, source_target_pairs={{4,8},{8,4},{5,9},{9,5},{6,10},{10,6},{7,11},{11,7},{20,24},{24,20... | collective-permute-start | bytes 921608 | tf_op jit(solution)/shard_map/ppermute | solution.py:715
  24.9 2.8 %rest.1 = (f32[3,2,9,160,128]{4,3,2,1,0:T(8,128)S(1)}, f32[6,2,8,160,128]{4,3,2,1,0:T(8,128)S(1)}, f32[6,2,8,144,128]{4,3,2,1,0:T(8,128)S(1)}) custom-call(s32[3]{0:T(128)S(1)} %pad_add_fusion.flags, s32[8,128]{1,0:T(8,128)S(1)} %broadcast_select_fusion.thirds, ...), custom_call_target="tpu_custom_call", output_to_operand_aliasing={{0}: (4, {}), {1}: (5, {}), {2}: (6, {})} | custom-call | flops 6553600 | tf_op jit(solution)/shard_map/rest/pallas_call | solution.py:804
  27.7 3.0 %inner.3 = (f32[3,2,9,160,128]{4,3,2,1,0:T(8,128)S(1)}, f32[6,2,8,160,128]{4,3,2,1,0:T(8,128)S(1)}) custom-call(f32[6,2,8,144,128]{4,3,2,1,0:T(8,128)S(1)} %get-tuple-element.61.m.refs_2_, f32[3,2,9,160,128]{4,3,2,1,0:T(8,128)S(1)} %get-tuple-element.62.v_in, ...), custom_call_target="tpu_custom_call", output_to_operand_aliasing={{0}: (1, {}), {1}: (2, {})} | custom-call | flops 26214400 | tf_op jit(solution)/shard_map/inner/pallas_call | solution.py:818
  30.7 0.0 collective-permute-done.3.refs_0_
  30.7 0.0 collective-permute-done.4.refs_1_
  30.7 2.0 %boundary.3 = (f32[3,2,9,160,128]{4,3,2,1,0:T(8,128)S(1)}, f32[6,2,8,160,128]{4,3,2,1,0:T(8,128)S(1)}, f32[8,2,16,128]{3,2,1,0:T(8,128)S(1)}, f32[2,144,128]{2,1...) custom-call(s32[3]{0:T(128)S(1)} %pad_add_fusion.flags, ...), custom_call_target="tpu_custom_call", output_to_operand_aliasing={{0}: (5, {}), {1}: (6, {}), {2}: (7, {})} | custom-call | flops 6553600 | tf_op jit(solution)/shard_map/boundary/pallas_call | solution.py:846
  32.7 0.1 collective-permute-start.5
  32.8 3.3 %collective-permute-start.6 = (f32[440,128]{1,0:T(8,128)S(1)}, f32[440,128]{1,0:T(8,128)S(1)}, u32[]{:S(2)}, u32[]{:S(2)}) collective-permute-start(f32[440,128]{1,0:T(8,128)S(1)} %get-tuple-element.68), channel_id=1, source_target_pairs={{4,8},{8,4},{5,9},{9,5},{6,10},{10,6},{7,11},{11,7},{20,24},{24,20... | collective-permute-start | bytes 675848 | tf_op jit(solution)/shard_map/ppermute | solution.py:715
  36.1 3.5 %inner.4 = (f32[3,2,9,160,128]{4,3,2,1,0:T(8,128)S(1)}, f32[6,2,8,160,128]{4,3,2,1,0:T(8,128)S(1)}) custom-call(f32[6,2,8,144,128]{4,3,2,1,0:T(8,128)S(1)} %get-tuple-element.61.m.refs_2_, f32[3,2,9,160,128]{4,3,2,1,0:T(8,128)S(1)} %get-tuple-element.70.v_in, ...), custom_call_target="tpu_custom_call", output_to_operand_aliasing={{0}: (1, {}), {1}: (2, {})} | custom-call | flops 26214400 | tf_op jit(solution)/shard_map/inner/pallas_call | solution.py:818
  39.6 0.0 collective-permute-done.5.refs_0_
  39.6 1.8 %collective-permute-done.6.refs_1_ = f32[440,128]{1,0:T(8,128)S(1)} collective-permute-done((f32[440,128]{1,0:T(8,128)S(1)}, f32[440,128]{1,0:T(8,128)S(1)}, u32[]{:S(2)}, u32[]{:S(2)}) %collective-permute-start.6) | collective-permute-done | bytes 225312 | tf_op jit(solution)/shard_map/ppermute | solution.py:715
  41.5 1.9 %boundary.4 = (f32[3,2,9,160,128]{4,3,2,1,0:T(8,128)S(1)}, f32[6,2,8,160,128]{4,3,2,1,0:T(8,128)S(1)}, f32[8,2,16,128]{3,2,1,0:T(8,128)S(1)}, f32[440,128]{1,0:T(8,128)S(1)}, f32[440,128]{1,0:T(8,128)S(1)}) custom-call(s32[3]{0:T(128)S(1)} %pad_add_fusion.flags, ...), custom_call_target="tpu_custom_call", output_to_operand_aliasing={{0}: (6, {}), {1}: (7, {}), {2}: (8, {})} | custom-call | flops 6553600 | tf_op jit(solution)/shard_map/boundary/pallas_call | solution.py:846
  43.4 0.1 collective-permute-start.7
  43.5 4.1 %collective-permute-start.8 = (f32[440,128]{1,0:T(8,128)S(1)}, f32[440,128]{1,0:T(8,128)S(1)}, u32[]{:S(2)}, u32[]{:S(2)}) collective-permute-start(f32[440,128]{1,0:T(8,128)S(1)} %get-tuple-element.76), channel_id=1, source_target_pairs={{4,8},{8,4},{5,9},{9,5},{6,10},{10,6},{7,11},{11,7},{20,24},{24,20... | collective-permute-start | bytes 675848 | tf_op jit(solution)/shard_map/ppermute | solution.py:715
  47.6 4.2 %inner.5 = (f32[3,2,9,160,128]{4,3,2,1,0:T(8,128)S(1)}, f32[6,2,8,160,128]{4,3,2,1,0:T(8,128)S(1)}, f32[3,8,128,128]{3,2,1,0:T(8,128)}, f32[6,8,128,128]{3,2,1,0:T(8,128)}) custom-call(f32[6,2,8,144,128]{4,3,2,1,0:T(8,128)S(1)} %get-tuple-element.61.m.refs_2_, ...), custom_call_target="tpu_custom_call", output_to_operand_aliasing={{0}: (1, {}), {1}: (2, {})} | custom-call | flops 26214400 | tf_op jit(solution)/shard_map/inner/pallas_call | solution.py:818
  51.8 0.0 collective-permute-done.7.refs_0_
  51.8 0.0 collective-permute-done.8.refs_1_
  51.8 3.6 %boundary.5 = (f32[3,2,9,160,128]{4,3,2,1,0:T(8,128)S(1)}, f32[6,2,8,160,128]{4,3,2,1,0:T(8,128)S(1)}, f32[8,2,16,128]{3,2,1,0:T(8,128)S(1)}, f32[3,8,128,128]{3...) custom-call(s32[3]{0:T(128)S(1)} %pad_add_fusion.flags, ...), custom_call_target="tpu_custom_call", output_to_operand_aliasing={{0}: (6, {}), {1}: (7, {}), {2}: (8, {}), {3}: (9, {}), {4}... | custom-call | flops 6553600 | tf_op jit(solution)/shard_map/boundary/pallas_call | solution.py:846
  (6 shorter events, 0.0 us)
Async XLA Ops:
  2.5 7.8 %collective-permute-start = (f32[15,4,8,128]{3,2,1,0:T(8,128)S(1)}, f32[15,4,8,128]{3,2,1,0:T(8,128)S(1)}, u32[]{:S(2)}, u32[]{:S(2)}) collective-permute-start(f32[15,4,8,128]{3,2,1,0:T(8,128)S(1)} %edge.1), channel_id=1, source_target_pairs={{0,16},{16,0},{1,17},{17,1},{2,18},{18,2},{3,19},{19,3},{4,20},{20... | collective-permute-start | bytes 737288 | tf_op jit(solution)/shard_map/ppermute | solution.py:766
  11.0 2.6 %collective-permute-start.1 = (f32[3,144,128]{2,1,0:T(8,128)S(1)}, f32[3,144,128]{2,1,0:T(8,128)S(1)}, u32[]{:S(2)}, u32[]{:S(2)}) collective-permute-start(f32[3,144,128]{2,1,0:T(8,128)S(1)} %get-tuple-element.51), channel_id=1, source_target_pairs={{0,1},{1,0},{2,3},{3,2},{4,5},{5,4},{6,7},{7,6},{8,9},{9,8},{10,11... | collective-permute-start | bytes 663560 | tf_op jit(solution)/shard_map/ppermute | solution.py:715
  11.1 7.3 %collective-permute-start.2 = (f32[3,144,128]{2,1,0:T(8,128)S(1)}, f32[3,144,128]{2,1,0:T(8,128)S(1)}, u32[]{:S(2)}, u32[]{:S(2)}) collective-permute-start(f32[3,144,128]{2,1,0:T(8,128)S(1)} %get-tuple-element.52), channel_id=1, source_target_pairs={{1,2},{2,1},{5,6},{6,5},{9,10},{10,9},{13,14},{14,13},{17,18},{18,... | collective-permute-start | bytes 663560 | tf_op jit(solution)/shard_map/ppermute | solution.py:715
  19.8 10.9 %collective-permute-start.3 = (f32[600,128]{1,0:T(8,128)S(1)}, f32[600,128]{1,0:T(8,128)S(1)}, u32[]{:S(2)}, u32[]{:S(2)}) collective-permute-start(f32[600,128]{1,0:T(8,128)S(1)} %get-tuple-element.56), channel_id=1, source_target_pairs={{0,4},{4,0},{8,12},{12,8},{1,5},{5,1},{9,13},{13,9},{2,6},{6,2},{1... | collective-permute-start | bytes 921608 | tf_op jit(solution)/shard_map/ppermute | solution.py:715
  20.3 10.4 %collective-permute-start.4 = (f32[600,128]{1,0:T(8,128)S(1)}, f32[600,128]{1,0:T(8,128)S(1)}, u32[]{:S(2)}, u32[]{:S(2)}) collective-permute-start(f32[600,128]{1,0:T(8,128)S(1)} %get-tuple-element.57), channel_id=1, source_target_pairs={{4,8},{8,4},{5,9},{9,5},{6,10},{10,6},{7,11},{11,7},{20,24},{24,20... | collective-permute-start | bytes 921608 | tf_op jit(solution)/shard_map/ppermute | solution.py:715
  32.7 7.0 %collective-permute-start.5 = (f32[440,128]{1,0:T(8,128)S(1)}, f32[440,128]{1,0:T(8,128)S(1)}, u32[]{:S(2)}, u32[]{:S(2)}) collective-permute-start(f32[440,128]{1,0:T(8,128)S(1)} %get-tuple-element.67), channel_id=1, source_target_pairs={{0,4},{4,0},{8,12},{12,8},{1,5},{5,1},{9,13},{13,9},{2,6},{6,2},{1... | collective-permute-start | bytes 675848 | tf_op jit(solution)/shard_map/ppermute | solution.py:715
  32.8 8.7 %collective-permute-start.6 = (f32[440,128]{1,0:T(8,128)S(1)}, f32[440,128]{1,0:T(8,128)S(1)}, u32[]{:S(2)}, u32[]{:S(2)}) collective-permute-start(f32[440,128]{1,0:T(8,128)S(1)} %get-tuple-element.68), channel_id=1, source_target_pairs={{4,8},{8,4},{5,9},{9,5},{6,10},{10,6},{7,11},{11,7},{20,24},{24,20... | collective-permute-start | bytes 675848 | tf_op jit(solution)/shard_map/ppermute | solution.py:715
  43.4 8.4 %collective-permute-start.7 = (f32[440,128]{1,0:T(8,128)S(1)}, f32[440,128]{1,0:T(8,128)S(1)}, u32[]{:S(2)}, u32[]{:S(2)}) collective-permute-start(f32[440,128]{1,0:T(8,128)S(1)} %get-tuple-element.75), channel_id=1, source_target_pairs={{0,4},{4,0},{8,12},{12,8},{1,5},{5,1},{9,13},{13,9},{2,6},{6,2},{1... | collective-permute-start | bytes 675848 | tf_op jit(solution)/shard_map/ppermute | solution.py:715
  43.5 8.3 %collective-permute-start.8 = (f32[440,128]{1,0:T(8,128)S(1)}, f32[440,128]{1,0:T(8,128)S(1)}, u32[]{:S(2)}, u32[]{:S(2)}) collective-permute-start(f32[440,128]{1,0:T(8,128)S(1)} %get-tuple-element.76), channel_id=1, source_target_pairs={{4,8},{8,4},{5,9},{9,5},{6,10},{10,6},{7,11},{11,7},{20,24},{24,20... | collective-permute-start | bytes 675848 | tf_op jit(solution)/shard_map/ppermute | solution.py:715

commit v7 on v6

--- a/solution.py
+++ b/solution.py
@@ -24,7 +24,10 @@
 
 VMEM = pltpu.MemorySpace.VMEM
 HBM = pltpu.MemorySpace.HBM
-SMEM = pltpu.MemorySpace.SMEM
+
+
+def odd_on(axis):
+    return lax.rem(lax.axis_index(axis), 2) == 1
 
 
 def in_vmem():
@@ -33,10 +36,6 @@
 
 def in_hbm():
     return pl.BlockSpec(memory_space=HBM)
-
-
-def in_smem():
-    return pl.BlockSpec(memory_space=SMEM)
 
 
 def roll(values, by):
@@ -181,13 +180,13 @@
     return row if row < nx else nx
 
 
-def edge_kernel(flags, velocity, stress, *rest):
+def edge_kernel(velocity, stress, *rest):
     raw_m, out, sem = rest[:6], rest[6], rest[7]
     ny, nx = velocity.shape[1:3]
     sources = [velocity.at[c] for c in range(3)] + [stress.at[c] for c in range(6)] + list(raw_m)
     for side, row in ((0, nx - CROSS), (1, 0)):
 
-        @pl.when(flags[0] == side)
+        @pl.when(lax.axis_index("gx") == side)
         def _(row=row):
             copies = []
             for f, source in enumerate(sources):
@@ -201,7 +200,7 @@
                 copy.wait()
 
 
-def load_kernel(flags, thirds, velocity, stress, *rest):
+def load_kernel(thirds, velocity, stress, *rest):
     raw_m, small = rest[:6], rest[6:13]
     v, s, m, fault, z_a, z_b = rest[13:19]
     pre, ids, mask, rate, slip, region_a, region_normal, sems = rest[19:]
@@ -237,7 +236,7 @@
                 v[c, t, y, PAD + cross + 8 : 2 * PAD + cross + 8, :] = zeros
 
     per_plane = fields_per_plane(ny, width)
-    odd = flags[2] == 1
+    odd = odd_on("gz")
     group = thirds[...]
     for plane in range(z_slots(ny, width)[1]):
         for key in FIELDS[plane * per_plane : (plane + 1) * per_plane]:
@@ -292,15 +291,15 @@
     return pieces
 
 
-def cross_kernel(flags, thirds, f_other, fault, v_in, s_in, m_in, za_in, zb_in, v, s, m, z_a, z_b):
+def cross_kernel(thirds, f_other, fault, v_in, s_in, m_in, za_in, zb_in, v, s, m, z_a, z_b):
     ny, width = m.shape[2], m.shape[4]
     nx = z_a.shape[1] - 16
     cross = cross_row(nx)
-    odd = flags[2] == 1
+    odd = odd_on("gz")
     group = thirds[...]
     planes = z_slots(ny, width)[1]
     rows = lax.broadcasted_iota(jnp.int32, (8, width), 0)
-    minus = flags[0] == 0
+    minus = lax.axis_index("gx") == 0
     keep = jnp.where(minus, 7 - rows, rows) >= 8 - CROSS
     for f, (kind, c) in enumerate(FIELDS):
         shift = 0 if kind == "m" else PAD
@@ -409,22 +408,22 @@
     halo.take(nx, fields(cross_row(nx)))
 
 
-def rest_kernel(flags, thirds, r_a, r_b, v_in, s_in, m_in, v, s, m):
+def rest_kernel(thirds, r_a, r_b, v_in, s_in, m_in, v, s, m):
     nx = r_a.shape[1] - 16
     planes = z_slots(m.shape[2], m.shape[4])[1]
-    halo = ZHalo(flags[2] == 1, thirds[...], r_a, r_b, planes)
+    halo = ZHalo(odd_on("gz"), thirds[...], r_a, r_b, planes)
     unpack_fields(halo, v, s, m, nx, False)
 
 
 def widen_kernel(
-    flags, thirds, eighths, r_a, r_b, v_in, s_in, m_in, f_in, v, s, m, fault, y_a, y_b, strips
+    thirds, eighths, r_a, r_b, v_in, s_in, m_in, f_in, v, s, m, fault, y_a, y_b, strips
 ):
     ny, width = m.shape[2], m.shape[4]
     nx = r_a.shape[1] - 16
     planes = z_slots(ny, width)[1]
-    odd_y = flags[1] == 1
+    odd_y = odd_on("gy")
     lanes = lane_index((8, width))
-    halo = ZHalo(flags[2] == 1, thirds[...], r_a, r_b, planes)
+    halo = ZHalo(odd_on("gz"), thirds[...], r_a, r_b, planes)
     unpack_fields(halo, v, s, m, nx, True)
 
     def store_fault(k):
@@ -504,7 +503,7 @@
         lax.fori_loop(1, ny - 1, wait, 0)
 
 
-def boundary_kernel(first, final, flags, eighths, *refs):
+def boundary_kernel(first, final, eighths, *refs):
     refs = list(refs)
 
     def pop(n):
@@ -529,7 +528,7 @@
     nx = m.shape[3] - 16
     cross = cross_row(nx)
     span = nx + 8
-    odd = flags[1] == 1
+    odd = odd_on("gy")
     lanes = lane_index((8, width))
     halos = eighths[...]
 
@@ -570,7 +569,7 @@
     places = ((0, (nx - 1, cross)), (1, (0, cross + 7)))
     for side, pair in places:
 
-        @pl.when(flags[0] == side)
+        @pl.when(lax.axis_index("gx") == side)
         def _(pair=pair):
             for which, row in enumerate(pair):
                 for t in range(2):
@@ -586,7 +585,7 @@
                                 line = ahead_b[t, row : row + 1, :]
                             fault[OWN_B + which, t, y : y + 1, :] = line
 
-    minus = flags[0] == 0
+    minus = lax.axis_index("gx") == 0
     sign = jnp.where(minus, DT, -DT)
     for t in range(2):
         for half in range(0, fault.shape[2], 8):
@@ -608,7 +607,7 @@
             stress_tile(v, s, m, y, row, lanes, (0,) if final else (0, 1))
     for side, pair in places:
 
-        @pl.when(flags[0] == side)
+        @pl.when(lax.axis_index("gx") == side)
         def _(pair=pair):
             for which, row in enumerate(pair):
                 for c in range(3):
@@ -735,8 +734,6 @@
 ):
     ny, nx, width = buoyancy.shape
     assert nx == width
-    across, along, dip = (lax.axis_index(k) for k in ("gx", "gy", "gz"))
-    flags = jnp.stack([across, along % 2, dip % 2]).astype(jnp.int32)
     lanes = jnp.broadcast_to(jnp.arange(width, dtype=jnp.int32), (8, width))
     thirds, eighths = lanes // HALO, lanes // STRIP
     rows = cross_row(nx) + 8
@@ -748,7 +745,7 @@
     planes = z_slots(ny, width)[1]
     z_shape = f32(planes, nx + 16, width)
     unit = ny * nx * width
-    vm, hb, sm = in_vmem(), in_hbm(), in_smem()
+    vm, hb = in_vmem(), in_hbm()
     raw = [velocity, stress, buoyancy, stiff_xx, stiff_xz, stiff_zz, shear_vert, shear_horiz]
     raw += [prestress, region_ids, fault_mask, inverse_rate, slip_prev, region_a, region_normal]
     raw = [pltpu.with_memory_space_constraint(k, HBM) for k in raw]
@@ -758,17 +755,17 @@
         edge_kernel,
         "edge",
         (f_shape,),
-        [sm] + [hb] * 8,
+        [hb] * 8,
         {},
         [pltpu.SemaphoreType.DMA((2 * len(FIELDS),))],
         flops=unit,
-    )(flags, *raw[:8])
+    )(*raw[:8])
     f_other = lax.ppermute(f_own, "gx", [(i, i ^ 1) for i in range(lax.axis_size("gx"))])
     v, s, m, fault, z_a, z_b = call(
         load_kernel,
         "load",
         (v_shape, s_shape, m_shape, fault_shape, z_shape, z_shape),
-        [sm, vm] + [hb] * 15,
+        [vm] + [hb] * 15,
         {},
         [
             pltpu.VMEM(prestress.shape, jnp.float32),
@@ -781,34 +778,34 @@
             pltpu.SemaphoreType.DMA((22,)),
         ],
         flops=100 * unit,
-    )(flags, thirds, *raw)
+    )(thirds, *raw)
     v, s, m, z_a, z_b = call(
         cross_kernel,
         "cross",
         (v_shape, s_shape, m_shape, z_shape, z_shape),
-        [sm] + [vm] * 8,
-        {4: 0, 5: 1, 6: 2, 7: 3, 8: 4},
+        [vm] * 8,
+        {3: 0, 4: 1, 5: 2, 6: 3, 7: 4},
         flops=10 * unit,
-    )(flags, thirds, f_other, fault, v, s, m, z_a, z_b)
+    )(thirds, f_other, fault, v, s, m, z_a, z_b)
     z_a, z_b = pair_swaps(z_a, z_b, "gz")
     y_shape = f32(SLOTS * (nx + 8 + STRIP) + 8 + 16, width)
     v, s, m, fault, y_a, y_b = call(
         widen_kernel,
         "widen",
         (v_shape, s_shape, m_shape, fault_shape, y_shape, y_shape),
-        [sm] + [vm] * 8,
-        {5: 0, 6: 1, 7: 2, 8: 3},
+        [vm] * 8,
+        {4: 0, 5: 1, 6: 2, 7: 3},
         [pltpu.VMEM((nx, width), jnp.float32)],
         flops=50 * unit,
-    )(flags, thirds, eighths, z_a, z_b, v, s, m, fault)
+    )(thirds, eighths, z_a, z_b, v, s, m, fault)
     v, s, m = call(
         rest_kernel,
         "rest",
         (v_shape, s_shape, m_shape),
-        [sm] + [vm] * 6,
-        {4: 0, 5: 1, 6: 2},
+        [vm] * 6,
+        {3: 0, 4: 1, 5: 2},
         flops=50 * unit,
-    )(flags, thirds, z_a, z_b, v, s, m)
+    )(thirds, z_a, z_b, v, s, m)
     y_shape = f32(3 * (nx + 8) + STRIP * 3 + 8, width)
     ahead_b = None
     out_shapes = (HBM((3, ny, nx, width), jnp.float32), HBM((6, ny, nx, width), jnp.float32))
@@ -825,7 +822,7 @@
             flops=200 * unit,
             out_specs=[vm, vm] + ([hb, hb] if final else []),
         )(m, v, s)
-        args = [flags, eighths, y_a, y_b, m]
+        args = [eighths, y_a, y_b, m]
         args += ([] if first else [ahead_b]) + [v, s, fault] + outs
         at_state = len(args) - len(outs) - 3
         aliases = {at_state + k: k for k in range(3)}
@@ -847,7 +844,7 @@
             functools.partial(boundary_kernel, first, final),
             "boundary",
             shapes,
-            [sm] + [vm] * (len(args) - 1 - len(outs)) + [hb] * len(outs),
+            [vm] * (len(args) - len(outs)) + [hb] * len(outs),
             aliases,
             scratch,
             flops=50 * unit,

time: 55.8 us -> 53.8 us (0.964)
  Pallas kernels: 30.3 us -> 26 us
  waiting for transfers between devices: 7.28 us -> 8.57 us
  starting transfers between devices: 16.8 us -> 18 us
    pallas_call x3, Pallas kernels: 7.5 us -> 5.82 us  [local(): call(functools.partial(boundary_kernel, first, final), 'boundary', shapes...]
    ppermute x8, starting transfers between devices: 15.2 us -> 16.4 us  [pair_swaps(): out.append(lax.ppermute(value, axis, pairs))]
    pallas_call x2, Pallas kernels: 4.52 us -> 3.45 us  [the longest x1 2.25 us: local(): call(rest_kernel, 'rest', (v_shape, s_shape, m_shape), [vm] * 6, {3: 0, 4...]
    ppermute x8, waiting for transfers between devices: 6.53 us -> 7.26 us  [pair_swaps(): out.append(lax.ppermute(value, axis, pairs))]
  transfers between devices with their start and end apart: 9 -> 9, of which waited for: 3 -> 4; matrix products, arithmetic and copies ran while one was open for 0% -> 0% of each run, Pallas kernels for 34% -> 33%
where the time goes in v7:
time: 53.8 us; the launch traced here: 53.4 us
  Pallas kernels  26 us (48%)
  starting transfers between devices  18 us (33%)
  waiting for transfers between devices  8.57 us (16%)
  between operations  0.81 us (2%)
    ppermute x8, starting transfers between devices, pair_swaps(): out.append(lax.ppermute(value, axis, pairs))  16.4 us
    pallas_call x3, Pallas kernels, local(): call(functools.partial(inner_kernel, first, final), 'inner', (v_shape, s_...  10.8 us
    ppermute x8, waiting for transfers between devices, pair_swaps(): out.append(lax.ppermute(value, axis, pairs))  7.26 us
    pallas_call x3, Pallas kernels, local(): call(functools.partial(boundary_kernel, first, final), 'boundary', shapes...  5.82 us
    pallas_call x1, Pallas kernels, local(): call(load_kernel, 'load', (v_shape, s_shape, m_shape, fault_shape, z_shap...  4.81 us
    pallas_call x1, Pallas kernels, local(): call(rest_kernel, 'rest', (v_shape, s_shape, m_shape), [vm] * 6, {3: 0, 4...  2.25 us
    ppermute x1, starting transfers between devices, local(): lax.ppermute(f_own, 'gx', [(i, i ^ 1) for i in range(lax.axis_size('gx'))])  1.59 us
    ppermute x1, waiting for transfers between devices, local(): lax.ppermute(f_own, 'gx', [(i, i ^ 1) for i in range(lax.axis_size('gx'))])  1.3 us
  transfers between devices with their start and end apart: 9, of which 4 were waited for; matrix products, arithmetic and copies ran while one was open for 0% of the time, Pallas kernels for 33%

profile of v7, /device:TPU:10, one launch (start us, length us, event | category | flops | bytes accessed | tf_op | source)
XLA Modules:
  0.0 53.4 jit_solution(7477777064360360671)
XLA Ops:
  0.6 1.2 %edge.1 = f32[15,4,8,128]{3,2,1,0:T(8,128)S(1)} custom-call(f32[3,8,128,128]{3,2,1,0:T(8,128)} %velocity.3, f32[6,8,128,128]{3,2,1,0:T(8,128)} %stress.3, f32[8,128,128]{2,1,0:T(8,128)} %rest_0_.3, f32[8,128,128]{2,1,0:T(8,128)} %rest_1_.3, f32[8,128,128]{2,1,0:T(8,128)} %rest_2_.3, f32[8,128,128]{2,1,0:T(8,128)} %rest_3_.3, f32[8,128,128]{2,1,0:T(8,128)} %rest_4_.3, ...), custom_call_target="tpu_custom_call" | custom-call | flops 131072 | tf_op jit(solution)/shard_map/edge/pallas_call | solution.py:754
  1.8 1.6 %collective-permute-start = (f32[15,4,8,128]{3,2,1,0:T(8,128)S(1)}, f32[15,4,8,128]{3,2,1,0:T(8,128)S(1)}, u32[]{:S(2)}, u32[]{:S(2)}) collective-permute-start(f32[15,4,8,128]{3,2,1,0:T(8,128)S(1)} %edge.1), channel_id=1, source_target_pairs={{0,16},{16,0},{1,17},{17,1},{2,18},{18,2},{3,19},{19,3},{4,20},{20... | collective-permute-start | bytes 737288 | tf_op jit(solution)/shard_map/ppermute | solution.py:763
  3.5 4.8 %load.1 = (f32[3,2,9,160,128]{4,3,2,1,0:T(8,128)S(1)}, f32[6,2,8,160,128]{4,3,2,1,0:T(8,128)S(1)}, f32[6,2,8,144,128]{4,3,2,1,0:T(8,128)S(1)}, f32[8,2,16,128]{3...) custom-call(s32[8,128]{1,0:T(8,128)S(1)} %broadcast_select_fusion.thirds, ...), custom_call_target="tpu_custom_call" | custom-call | flops 13107200 | tf_op jit(solution)/shard_map/load/pallas_call | solution.py:764
  8.3 1.3 %collective-permute-done.f_other = f32[15,4,8,128]{3,2,1,0:T(8,128)S(1)} collective-permute-done((f32[15,4,8,128]{3,2,1,0:T(8,128)S(1)}, f32[15,4,8,128]{3,2,1,0:T(8,128)S(1)}, u32[]{:S(2)}, u32[]{:S(2)}) %collective-permute-start) | collective-permute-done | bytes 245792 | tf_op jit(solution)/shard_map/ppermute | solution.py:763
  9.6 0.2 cross.1
  9.8 0.1 collective-permute-start.1
  9.9 2.5 %collective-permute-start.2 = (f32[3,144,128]{2,1,0:T(8,128)S(1)}, f32[3,144,128]{2,1,0:T(8,128)S(1)}, u32[]{:S(2)}, u32[]{:S(2)}) collective-permute-start(f32[3,144,128]{2,1,0:T(8,128)S(1)} %get-tuple-element.52), channel_id=1, source_target_pairs={{1,2},{2,1},{5,6},{6,5},{9,10},{10,9},{13,14},{14,13},{17,18},{18,... | collective-permute-start | bytes 663560 | tf_op jit(solution)/shard_map/ppermute | solution.py:714
  12.5 0.0 collective-permute-done.1.r_a
  12.5 4.7 %collective-permute-done.2.r_b = f32[3,144,128]{2,1,0:T(8,128)S(1)} collective-permute-done((f32[3,144,128]{2,1,0:T(8,128)S(1)}, f32[3,144,128]{2,1,0:T(8,128)S(1)}, u32[]{:S(2)}, u32[]{:S(2)}) %collective-permute-start.2) | collective-permute-done | bytes 221216 | tf_op jit(solution)/shard_map/ppermute | solution.py:714
  17.2 0.9 %widen.1 = (f32[3,2,9,160,128]{4,3,2,1,0:T(8,128)S(1)}, f32[6,2,8,160,128]{4,3,2,1,0:T(8,128)S(1)}, f32[6,2,8,144,128]{4,3,2,1,0:T(8,128)S(1)}, f32[8,2,16,128]{...) custom-call(s32[8,128]{1,0:T(8,128)S(1)} %broadcast_select_fusion.th, ...), custom_call_target="tpu_custom_call", output_to_operand_aliasing={{0}: (4, {}), {1}: (5, {}), {2}: (6, {}), {3}: (7, {})} | custom-call | flops 6553600 | tf_op jit(solution)/shard_map/widen/pallas_call | solution.py:792
  18.1 0.5 collective-permute-start.3
  18.6 4.6 %collective-permute-start.4 = (f32[600,128]{1,0:T(8,128)S(1)}, f32[600,128]{1,0:T(8,128)S(1)}, u32[]{:S(2)}, u32[]{:S(2)}) collective-permute-start(f32[600,128]{1,0:T(8,128)S(1)} %get-tuple-element.57), channel_id=1, source_target_pairs={{4,8},{8,4},{5,9},{9,5},{6,10},{10,6},{7,11},{11,7},{20,24},{24,20... | collective-permute-start | bytes 921608 | tf_op jit(solution)/shard_map/ppermute | solution.py:714
  23.2 2.2 %rest.1 = (f32[3,2,9,160,128]{4,3,2,1,0:T(8,128)S(1)}, f32[6,2,8,160,128]{4,3,2,1,0:T(8,128)S(1)}, f32[6,2,8,144,128]{4,3,2,1,0:T(8,128)S(1)}) custom-call(s32[8,128]{1,0:T(8,128)S(1)} %broadcast_select_fusion.thirds, f32[3,144,128]{2,1,0:T(8,128)S(1)} %collective-permute-done.1.r_a, ...), custom_call_target="tpu_custom_call", output_to_operand_aliasing={{0}: (3, {}), {1}: (4, {}), {2}: (5, {})} | custom-call | flops 6553600 | tf_op jit(solution)/shard_map/rest/pallas_call | solution.py:801
  25.4 3.0 %inner.3 = (f32[3,2,9,160,128]{4,3,2,1,0:T(8,128)S(1)}, f32[6,2,8,160,128]{4,3,2,1,0:T(8,128)S(1)}) custom-call(f32[6,2,8,144,128]{4,3,2,1,0:T(8,128)S(1)} %get-tuple-element.61.m.refs_2_, f32[3,2,9,160,128]{4,3,2,1,0:T(8,128)S(1)} %get-tuple-element.62.v_in, ...), custom_call_target="tpu_custom_call", output_to_operand_aliasing={{0}: (1, {}), {1}: (2, {})} | custom-call | flops 26214400 | tf_op jit(solution)/shard_map/inner/pallas_call | solution.py:815
  28.4 0.0 collective-permute-done.3.refs_0_
  28.4 0.2 collective-permute-done.4.refs_1_
  28.6 1.4 %boundary.3 = (f32[3,2,9,160,128]{4,3,2,1,0:T(8,128)S(1)}, f32[6,2,8,160,128]{4,3,2,1,0:T(8,128)S(1)}, f32[8,2,16,128]{3,2,1,0:T(8,128)S(1)}, f32[2,144,128]{2,1...) custom-call(s32[8,128]{1,0:T(8,128)S(1)} %broadcast_select_fusion.1., ...), custom_call_target="tpu_custom_call", output_to_operand_aliasing={{0}: (4, {}), {1}: (5, {}), {2}: (6, {})} | custom-call | flops 6553600 | tf_op jit(solution)/shard_map/boundary/pallas_call | solution.py:843
  30.1 0.1 collective-permute-start.5
  30.1 4.4 %collective-permute-start.6 = (f32[440,128]{1,0:T(8,128)S(1)}, f32[440,128]{1,0:T(8,128)S(1)}, u32[]{:S(2)}, u32[]{:S(2)}) collective-permute-start(f32[440,128]{1,0:T(8,128)S(1)} %get-tuple-element.68), channel_id=1, source_target_pairs={{4,8},{8,4},{5,9},{9,5},{6,10},{10,6},{7,11},{11,7},{20,24},{24,20... | collective-permute-start | bytes 675848 | tf_op jit(solution)/shard_map/ppermute | solution.py:714
  34.5 3.5 %inner.4 = (f32[3,2,9,160,128]{4,3,2,1,0:T(8,128)S(1)}, f32[6,2,8,160,128]{4,3,2,1,0:T(8,128)S(1)}) custom-call(f32[6,2,8,144,128]{4,3,2,1,0:T(8,128)S(1)} %get-tuple-element.61.m.refs_2_, f32[3,2,9,160,128]{4,3,2,1,0:T(8,128)S(1)} %get-tuple-element.70.v_in, ...), custom_call_target="tpu_custom_call", output_to_operand_aliasing={{0}: (1, {}), {1}: (2, {})} | custom-call | flops 26214400 | tf_op jit(solution)/shard_map/inner/pallas_call | solution.py:815
  38.1 0.0 collective-permute-done.5.refs_0_
  38.1 2.4 %collective-permute-done.6.refs_1_ = f32[440,128]{1,0:T(8,128)S(1)} collective-permute-done((f32[440,128]{1,0:T(8,128)S(1)}, f32[440,128]{1,0:T(8,128)S(1)}, u32[]{:S(2)}, u32[]{:S(2)}) %collective-permute-start.6) | collective-permute-done | bytes 225312 | tf_op jit(solution)/shard_map/ppermute | solution.py:714
  40.5 1.4 %boundary.4 = (f32[3,2,9,160,128]{4,3,2,1,0:T(8,128)S(1)}, f32[6,2,8,160,128]{4,3,2,1,0:T(8,128)S(1)}, f32[8,2,16,128]{3,2,1,0:T(8,128)S(1)}, f32[440,128]{1,0:T(8,128)S(1)}, f32[440,128]{1,0:T(8,128)S(1)}) custom-call(s32[8,128]{1,0:T(8,128)S(1)} %broadcast_select_fusion.1.eighths, ...), custom_call_target="tpu_custom_call", output_to_operand_aliasing={{0}: (5, {}), {1}: (6, {}), {2}: (7, {})} | custom-call | flops 6553600 | tf_op jit(solution)/shard_map/boundary/pallas_call | solution.py:843
  41.9 0.1 collective-permute-start.7
  41.9 4.2 %collective-permute-start.8 = (f32[440,128]{1,0:T(8,128)S(1)}, f32[440,128]{1,0:T(8,128)S(1)}, u32[]{:S(2)}, u32[]{:S(2)}) collective-permute-start(f32[440,128]{1,0:T(8,128)S(1)} %get-tuple-element.76), channel_id=1, source_target_pairs={{4,8},{8,4},{5,9},{9,5},{6,10},{10,6},{7,11},{11,7},{20,24},{24,20... | collective-permute-start | bytes 675848 | tf_op jit(solution)/shard_map/ppermute | solution.py:714
  46.1 4.2 %inner.5 = (f32[3,2,9,160,128]{4,3,2,1,0:T(8,128)S(1)}, f32[6,2,8,160,128]{4,3,2,1,0:T(8,128)S(1)}, f32[3,8,128,128]{3,2,1,0:T(8,128)}, f32[6,8,128,128]{3,2,1,0:T(8,128)}) custom-call(f32[6,2,8,144,128]{4,3,2,1,0:T(8,128)S(1)} %get-tuple-element.61.m.refs_2_, ...), custom_call_target="tpu_custom_call", output_to_operand_aliasing={{0}: (1, {}), {1}: (2, {})} | custom-call | flops 26214400 | tf_op jit(solution)/shard_map/inner/pallas_call | solution.py:815
  50.4 0.0 collective-permute-done.7.refs_0_
  50.4 0.0 collective-permute-done.8.refs_1_
  50.4 3.0 %boundary.5 = (f32[3,2,9,160,128]{4,3,2,1,0:T(8,128)S(1)}, f32[6,2,8,160,128]{4,3,2,1,0:T(8,128)S(1)}, f32[8,2,16,128]{3,2,1,0:T(8,128)S(1)}, f32[3,8,128,128]{3...) custom-call(s32[8,128]{1,0:T(8,128)S(1)} %broadcast_select_fusion.1., ...), custom_call_target="tpu_custom_call", output_to_operand_aliasing={{0}: (5, {}), {1}: (6, {}), {2}: (7, {}), {3}: (8, {}), {4}... | custom-call | flops 6553600 | tf_op jit(solution)/shard_map/boundary/pallas_call | solution.py:843
  (6 shorter events, 0.0 us)
Async XLA Ops:
  1.8 7.8 %collective-permute-start = (f32[15,4,8,128]{3,2,1,0:T(8,128)S(1)}, f32[15,4,8,128]{3,2,1,0:T(8,128)S(1)}, u32[]{:S(2)}, u32[]{:S(2)}) collective-permute-start(f32[15,4,8,128]{3,2,1,0:T(8,128)S(1)} %edge.1), channel_id=1, source_target_pairs={{0,16},{16,0},{1,17},{17,1},{2,18},{18,2},{3,19},{19,3},{4,20},{20... | collective-permute-start | bytes 737288 | tf_op jit(solution)/shard_map/ppermute | solution.py:763
  9.8 2.6 %collective-permute-start.1 = (f32[3,144,128]{2,1,0:T(8,128)S(1)}, f32[3,144,128]{2,1,0:T(8,128)S(1)}, u32[]{:S(2)}, u32[]{:S(2)}) collective-permute-start(f32[3,144,128]{2,1,0:T(8,128)S(1)} %get-tuple-element.51), channel_id=1, source_target_pairs={{0,1},{1,0},{2,3},{3,2},{4,5},{5,4},{6,7},{7,6},{8,9},{9,8},{10,11... | collective-permute-start | bytes 663560 | tf_op jit(solution)/shard_map/ppermute | solution.py:714
  9.9 7.3 %collective-permute-start.2 = (f32[3,144,128]{2,1,0:T(8,128)S(1)}, f32[3,144,128]{2,1,0:T(8,128)S(1)}, u32[]{:S(2)}, u32[]{:S(2)}) collective-permute-start(f32[3,144,128]{2,1,0:T(8,128)S(1)} %get-tuple-element.52), channel_id=1, source_target_pairs={{1,2},{2,1},{5,6},{6,5},{9,10},{10,9},{13,14},{14,13},{17,18},{18,... | collective-permute-start | bytes 663560 | tf_op jit(solution)/shard_map/ppermute | solution.py:714
  18.1 10.4 %collective-permute-start.3 = (f32[600,128]{1,0:T(8,128)S(1)}, f32[600,128]{1,0:T(8,128)S(1)}, u32[]{:S(2)}, u32[]{:S(2)}) collective-permute-start(f32[600,128]{1,0:T(8,128)S(1)} %get-tuple-element.56), channel_id=1, source_target_pairs={{0,4},{4,0},{8,12},{12,8},{1,5},{5,1},{9,13},{13,9},{2,6},{6,2},{1... | collective-permute-start | bytes 921608 | tf_op jit(solution)/shard_map/ppermute | solution.py:714
  18.6 10.1 %collective-permute-start.4 = (f32[600,128]{1,0:T(8,128)S(1)}, f32[600,128]{1,0:T(8,128)S(1)}, u32[]{:S(2)}, u32[]{:S(2)}) collective-permute-start(f32[600,128]{1,0:T(8,128)S(1)} %get-tuple-element.57), channel_id=1, source_target_pairs={{4,8},{8,4},{5,9},{9,5},{6,10},{10,6},{7,11},{11,7},{20,24},{24,20... | collective-permute-start | bytes 921608 | tf_op jit(solution)/shard_map/ppermute | solution.py:714
  30.1 8.0 %collective-permute-start.5 = (f32[440,128]{1,0:T(8,128)S(1)}, f32[440,128]{1,0:T(8,128)S(1)}, u32[]{:S(2)}, u32[]{:S(2)}) collective-permute-start(f32[440,128]{1,0:T(8,128)S(1)} %get-tuple-element.67), channel_id=1, source_target_pairs={{0,4},{4,0},{8,12},{12,8},{1,5},{5,1},{9,13},{13,9},{2,6},{6,2},{1... | collective-permute-start | bytes 675848 | tf_op jit(solution)/shard_map/ppermute | solution.py:714
  30.1 10.3 %collective-permute-start.6 = (f32[440,128]{1,0:T(8,128)S(1)}, f32[440,128]{1,0:T(8,128)S(1)}, u32[]{:S(2)}, u32[]{:S(2)}) collective-permute-start(f32[440,128]{1,0:T(8,128)S(1)} %get-tuple-element.68), channel_id=1, source_target_pairs={{4,8},{8,4},{5,9},{9,5},{6,10},{10,6},{7,11},{11,7},{20,24},{24,20... | collective-permute-start | bytes 675848 | tf_op jit(solution)/shard_map/ppermute | solution.py:714
  41.9 8.5 %collective-permute-start.7 = (f32[440,128]{1,0:T(8,128)S(1)}, f32[440,128]{1,0:T(8,128)S(1)}, u32[]{:S(2)}, u32[]{:S(2)}) collective-permute-start(f32[440,128]{1,0:T(8,128)S(1)} %get-tuple-element.75), channel_id=1, source_target_pairs={{0,4},{4,0},{8,12},{12,8},{1,5},{5,1},{9,13},{13,9},{2,6},{6,2},{1... | collective-permute-start | bytes 675848 | tf_op jit(solution)/shard_map/ppermute | solution.py:714
  41.9 8.5 %collective-permute-start.8 = (f32[440,128]{1,0:T(8,128)S(1)}, f32[440,128]{1,0:T(8,128)S(1)}, u32[]{:S(2)}, u32[]{:S(2)}) collective-permute-start(f32[440,128]{1,0:T(8,128)S(1)} %get-tuple-element.76), channel_id=1, source_target_pairs={{4,8},{8,4},{5,9},{9,5},{6,10},{10,6},{7,11},{11,7},{20,24},{24,20... | collective-permute-start | bytes 675848 | tf_op jit(solution)/shard_map/ppermute | solution.py:714
